TPU v7x, 256 devices: a whole 4x4x8 slice. The times are simulated.
256 devices in a mesh: row: 16 (over y_hi, x, core), col: 16 (over z, y_lo).
Axes of the slice: x: 4, y: 4 (y_hi: 2, y_lo: 2; y = y_hi * 2 + y_lo), z: 8, core: 2. Of those that a mesh axis runs over, the one named last changes fastest.
Arguments:
- blocks: bfloat16 [16, 16, 368, 128, 128], P('row', 'col'), may hold values from -0.125 to 0.125
- block_rows: int32 [16, 16, 368], P('row', 'col'), may hold values from 0 to 127, as said below
- block_cols: int32 [16, 16, 368], P('row', 'col'), may hold values from 0 to 127
- counts: int32 [16, 16], P('row', 'col'), may hold values from 1 to 368, as said below
- features: bfloat16 [262144, 256], P(('col', 'row')), may hold values from -6 to 6
Outputs:
- aggregated: bfloat16 [262144, 256], P(('row', 'col'))
Inputs may be any that keep to these rules, and one draw needn't show every extreme that they name: `block_rows`: within one tile the live slots name distinct pairs of block row and block column. `counts`: some tile holds exactly 368 live blocks in every draw.
All inputs are finite; a program needn't handle non-finite values.
Results may differ from a plain program's by a relative error of at most 0.013.
Values may be sent and summed in bfloat16 or wider, within the bound.
No kernel may reach another device: no remote copies, remote signals or barrier semaphores. Data moves between devices by JAX's collectives and lax.ppermute only.
A program may use at most 128 MiB of HBM per device.

v0:
```python
import jax
import jax.numpy as jnp
from jax import lax
from jax.experimental import pallas as pl
from jax.experimental.pallas import tpu as pltpu
from jax.sharding import Mesh
from jax.sharding import PartitionSpec as P


ROW = ("yh", "x", "c")
COL = ("z", "yl")
GROUP = 16
BUFFERS = 4
LATE = 4
EARLY = 8 - LATE
MESSAGES = (2, 3, 3)


def shift(array, axis, step):
    n = lax.axis_size(axis)
    return lax.ppermute(array, axis, [(i, (i + step) % n) for i in range(n)])


def tile_product(blocks, packed, count, core, pieces, places):
    bs, width = pieces[0].shape[1:]
    half = width // 2
    n_pieces, n_cols, n_rows = len(pieces), 128, 128
    late_rows, part_rows = 16 * LATE, 8
    late_parts, parts = late_rows // part_rows, n_rows // part_rows
    lates = []
    for other, row in ((False, 8 * LATE), (True, 8 * LATE), (False, 0), (True, 0)):
        first = 0
        for n in MESSAGES:
            lates.append((other, row, first, n))
            first += n
    shapes = [(n * LATE, bs, half) for *_, n in lates]

    def body(count_ref, core_ref, packed_ref, blocks_ref, *rest):
        piece_refs, out_ref = rest[:n_pieces], rest[n_pieces]
        late_refs = rest[n_pieces + 1 : n_pieces + 1 + len(lates)]
        acc, panel, weights, staged, *rest = rest[n_pieces + 1 + len(lates) :]
        late_staged, (piece_sem, weight_sem, out_sem, late_sem) = rest[: len(lates)], rest[len(lates) :]
        groups = (count_ref[0] + GROUP - 1) // GROUP

        def weight_copies(group):
            slot = lax.rem(group, BUFFERS)
            return [
                pltpu.make_async_copy(
                    blocks_ref.at[packed_ref[group * GROUP + i] & 511],
                    weights.at[slot, i],
                    weight_sem.at[slot, i],
                )
                for i in range(GROUP)
            ]

        def fetch(group):
            @pl.when(group < groups)
            def _():
                for copy in weight_copies(group):
                    copy.start()

        piece_copies = [
            pltpu.make_async_copy(ref, panel.at[pl.ds(place, piece.shape[0])], piece_sem.at[i])
            for i, (ref, piece, place) in enumerate(zip(piece_refs, pieces, places))
        ]
        for copy in piece_copies:
            copy.start()
        for group in range(BUFFERS - 1):
            fetch(group)

        def clear(i, _):
            acc[i] = jnp.zeros((bs, width), jnp.float32)
            return 0

        lax.fori_loop(0, n_rows + 1, clear, 0)
        for copy in piece_copies:
            copy.wait()

        def out_copy(at, slot):
            return pltpu.make_async_copy(
                staged.at[slot], out_ref.at[pl.ds(at * part_rows, part_rows)], out_sem.at[slot]
            )

        def late_copy(i):
            return pltpu.make_async_copy(late_staged[i], late_refs[i], late_sem.at[i])

        def write_late(on_core):
            for i, (other, row, first, n) in enumerate(lates):
                up = other == (on_core == 1)
                lane = 0 if up else half

                def group_of(at, _, i=i, row=row, first=first, up=up, lane=lane):
                    distance = 7 - first - at if up else lax.rem(first + 1 + at, 8)
                    for k in range(LATE):
                        value = acc[row + distance * LATE + k, :, lane : lane + half]
                        late_staged[i][at * LATE + k] = value.astype(jnp.bfloat16)
                    return 0

                lax.fori_loop(0, n, group_of, 0)
                late_copy(i).start()

        def write(part, _):
            @pl.when(jnp.logical_and(part == late_parts - 1, core_ref[0] == 0))
            def _():
                write_late(0)

            @pl.when(jnp.logical_and(part == late_parts - 1, core_ref[0] == 1))
            def _():
                write_late(1)

            @pl.when(part >= late_parts)
            def _():
                at = part - late_parts
                slot = lax.rem(at, 2)

                @pl.when(at >= 2)
                def _():
                    out_copy(at - 2, slot).wait()

                for i in range(part_rows):
                    staged[slot, i] = acc[part * part_rows + i].astype(jnp.bfloat16)
                out_copy(at, slot).start()

            return 0

        def one_group(group, finished):
            slot = lax.rem(group, BUFFERS)
            fetch(group + BUFFERS - 1)
            for copy in weight_copies(group):
                copy.wait()
            for i in range(GROUP):
                entry = packed_ref[group * GROUP + i]
                row = 128 - (entry >> 16)
                col = (entry >> 9) & 127
                acc[row] += jnp.dot(weights[slot, i], panel[col], preferred_element_type=jnp.float32)
            ready = (128 - (packed_ref[(group + 1) * GROUP] >> 16)) // part_rows
            lax.fori_loop(finished, ready, write, 0)
            return ready

        finished = lax.fori_loop(0, groups, one_group, 0)
        lax.fori_loop(finished, parts, write, 0)
        for slot in range(2):
            out_copy(0, slot).wait()
        for i in range(len(lates)):
            late_copy(i).wait()

    anywhere = pl.BlockSpec(memory_space=pl.ANY)
    hbm = pl.BlockSpec(memory_space=pltpu.MemorySpace.HBM)
    smem = pl.BlockSpec(memory_space=pltpu.SMEM)
    early_shape = jax.ShapeDtypeStruct((16 * EARLY, bs, width), jnp.bfloat16)
    return pl.pallas_call(
        body,
        out_shape=[early_shape] + [jax.ShapeDtypeStruct(shape, jnp.bfloat16) for shape in shapes],
        in_specs=[smem, smem, smem, hbm] + [anywhere] * n_pieces,
        out_specs=[hbm] + [anywhere] * len(lates),
        scratch_shapes=[
            pltpu.VMEM((n_rows + 1, bs, width), jnp.float32),
            pltpu.VMEM((n_cols, bs, width), jnp.bfloat16),
            pltpu.VMEM((BUFFERS, GROUP, bs, bs), jnp.bfloat16),
            pltpu.VMEM((2, part_rows, bs, width), jnp.bfloat16),
            *[pltpu.VMEM(shape, jnp.bfloat16) for shape in shapes],
            pltpu.SemaphoreType.DMA((n_pieces,)),
            pltpu.SemaphoreType.DMA((BUFFERS, GROUP)),
            pltpu.SemaphoreType.DMA((2,)),
            pltpu.SemaphoreType.DMA((len(lates),)),
        ],
        compiler_params=pltpu.CompilerParams(vmem_limit_bytes=50 * 2**20),
        cost_estimate=pl.CostEstimate(
            flops=n_rows * 3 * 2 * bs * bs * width, bytes_accessed=30 * 2**20, transcendentals=0
        ),
        name="tile_product",
    )(count, core, packed, blocks, *pieces)


def gather_panel(own):
    half = own.shape[0] // 2
    got = [(own, 0, 0, 0)]
    across = shift(own, "yh", 1)
    got.append((across, 1, 0, 0))
    for part, dyh in ((own, 0), (across, 1)):
        before = shift(part, "x", 1)
        after = shift(part, "x", -1)
        far_low = shift(before[:half], "x", 1)
        far_high = shift(after[half:], "x", -1)
        got += [(before, dyh, 3, 0), (after, dyh, 1, 0), (far_low, dyh, 2, 0), (far_high, dyh, 2, half)]
    pieces, places = [], []
    for part, dyh, dx, at in got:
        for dc in range(2):
            pieces.append(shift(part, "c", 1) if dc else part)
            places.append(((dyh * 4 + dx) * 2 + dc) * 8 + at)
    return pieces, places


def sort_slots(rows, cols, live, total):
    slots = jnp.arange(rows.shape[0], dtype=jnp.int32)
    key = jnp.where(live, rows, 128) * 512 + slots
    rank = jnp.sum((key[None, :] < key[:, None]).astype(jnp.int32), axis=1)
    entry = jnp.where(live, slots + 512 * cols + 65536 * (128 - rows), 0)
    places = jnp.arange(total, dtype=jnp.int32)
    picked = jnp.where(rank[:, None] == places[None, :], entry[:, None], 0)
    return jnp.sum(picked, axis=0)


def flip(array, axes):
    n = 2 ** len(axes)
    return lax.ppermute(array, axes, [(i, n - 1 - i) for i in range(n)])


def on_device(blocks, block_rows, block_cols, counts, features):
    bs = blocks.shape[-1]
    width = features.shape[1]
    yh, x, c = (lax.axis_index(name) for name in ROW)
    z, yl = (lax.axis_index(name) for name in COL)
    rows, cols, count = block_rows[0, 0], block_cols[0, 0], counts[0]
    live = jnp.arange(rows.shape[0], dtype=jnp.int32) < count[0]
    owner, within = rows // 8, rows % 8
    to_z, away = owner // 2, jnp.bitwise_xor(owner % 2, yl)
    early_row = 16 * LATE + (to_z * 2 + away) * EARLY + within - LATE
    late_row = (away * 8 + (to_z - z) % 8) * LATE + within
    rows = jnp.where(within < LATE, late_row, early_row)
    holder = cols // 8
    distance = (
        jnp.bitwise_xor(holder // 8, yh) * 8 + ((holder // 2 - x) % 4) * 2 + jnp.bitwise_xor(holder % 2, c)
    )
    packed = sort_slots(rows, distance * 8 + cols % 8, live, rows.shape[0] + 2 * GROUP)
    pieces, places = gather_panel(features.reshape(-1, bs, width))
    early, *parts = tile_product(
        blocks[0, 0], packed, count, c.reshape(1), pieces, places
    )
    early = lax.psum_scatter(early, "z", scatter_dimension=0, tiled=True)

    n = len(MESSAGES)
    joined = []
    for i in range(n):
        mine = flip(parts[i], ("yl",))
        theirs = flip(parts[n + i], ("c", "yl"))
        kept_theirs = flip(parts[3 * n + i], ("c",))
        shape = (MESSAGES[i], 1, LATE, bs, width // 2)
        both = jnp.concatenate(
            [(parts[2 * n + i] + mine).reshape(shape), (kept_theirs + theirs).reshape(shape)], 1
        )
        both = lax.optimization_barrier(both)
        joined += [both[k] for k in range(MESSAGES[i])]
    moving = joined[0]
    around = [(i, (i + 1) % 8) for i in range(8)] + [(8 + i, 8 + (i - 1) % 8) for i in range(8)]
    for step in range(7):
        moving = lax.ppermute(moving, ("c", "z"), around)
        moving = joined[step + 1] + moving
    other_half = flip(moving[1], ("c",))
    last = flip(early[EARLY:], ("yl",))
    own_half = moving[0]
    low = jnp.where(c == 0, own_half, other_half)
    high = jnp.where(c == 0, other_half, own_half)
    late = jnp.concatenate([low, high], 2)
    return jnp.concatenate([late, early[:EARLY] + last], 0).reshape(-1, width)


def solution(mesh):
    finer = Mesh(mesh.devices.reshape(2, 4, 2, 8, 2), ROW + COL)
    placed = (
        P(ROW, COL, None, None, None),
        P(ROW, COL, None),
        P(ROW, COL, None),
        P(ROW, COL),
        P(COL + ROW, None),
    )

    return jax.shard_map(on_device, mesh=finer, in_specs=placed, out_specs=P(ROW + COL, None), check_vma=False)
```

profile of v0, /device:TPU:1, one launch (start us, length us, event | category | flops | bytes accessed | tf_op | source)
XLA Modules:
  0.0 184.3 jit_solution(3840505266259064836)
XLA Ops:
  6.5 3.7 %collective-permute-start.1 = (bf16[8,128,256]{2,1,0:T(8,128)(2,1)}, bf16[8,128,256]{2,1,0:T(8,128)(2,1)}, u32[]{:S(2)}, u32[]{:S(2)}) collective-permute-start(bf16[8,128,256]{2,1,0:T(8,128)(2,1)} %bitcast.72), channel_id=1, source_target_pairs={{0,128},{128,0},{1,129},{129,1},{2,130},{130,2},{3,131},{131,3},{4... | collective-permute-start | bytes 1572872 | tf_op jit(solution)/shard_map/ppermute | solution.py:21
  10.3 2.5 %collective-permute-start.5 = (bf16[8,128,256]{2,1,0:T(8,128)(2,1)}, bf16[8,128,256]{2,1,0:T(8,128)(2,1)S(1)}, u32[]{:S(2)}, u32[]{:S(2)}) collective-permute-start(bf16[8,128,256]{2,1,0:T(8,128)(2,1)} %bitcast.73), channel_id=1, source_target_pairs={{0,96},{32,0},{64,32},{96,64},{1,97},{33,1},{65,33},{97,65},{2,98}... | collective-permute-start | bytes 1572872 | tf_op jit(solution)/shard_map/ppermute | solution.py:21
  12.8 8.4 %collective-permute-done.1.rest_2_ = bf16[8,128,256]{2,1,0:T(8,128)(2,1)} collective-permute-done((bf16[8,128,256]{2,1,0:T(8,128)(2,1)}, bf16[8,128,256]{2,1,0:T(8,128)(2,1)}, u32[]{:S(2)}, u32[]{:S(2)}) %collective-permute-start.1) | collective-permute-done | bytes 524320 | tf_op jit(solution)/shard_map/ppermute | solution.py:21
  21.2 2.0 %collective-permute-start.11 = (bf16[8,128,256]{2,1,0:T(8,128)(2,1)}, bf16[8,128,256]{2,1,0:T(8,128)(2,1)S(1)}, u32[]{:S(2)}, u32[]{:S(2)}) collective-permute-start(bf16[8,128,256]{2,1,0:T(8,128)(2,1)} %collective-permute-done.1.rest_2_), channel_id=1, source_target_pairs={{0,32},{32,64},{64,96},{96,0},{1,33},{33,65},{65,97},{97,1},{2,34}... | collective-permute-start | bytes 1572872 | tf_op jit(solution)/shard_map/ppermute | solution.py:21
  23.2 1.3 collective-permute-start.13
  24.5 2.3 %collective-permute-start.9 = (bf16[4,128,256]{2,1,0:T(8,128)(2,1)S(1)}, bf16[4,128,256]{2,1,0:T(8,128)(2,1)S(1)}, u32[]{:S(2)}, u32[]{:S(2)}) collective-permute-start(bf16[4,128,256]{2,1,0:T(8,128)(2,1)S(1)} %slice.65), channel_id=1, source_target_pairs={{0,96},{32,0},{64,32},{96,64},{1,97},{33,1},{65,33},{97,65},{2,98}... | collective-permute-start | bytes 786440 | tf_op jit(solution)/shard_map/ppermute | solution.py:21
  26.9 3.5 %collective-permute-start = (bf16[8,128,256]{2,1,0:T(8,128)(2,1)}, bf16[8,128,256]{2,1,0:T(8,128)(2,1)S(1)}, u32[]{:S(2)}, u32[]{:S(2)}) collective-permute-start(bf16[8,128,256]{2,1,0:T(8,128)(2,1)} %bitcast.75), channel_id=1, source_target_pairs={{0,16},{16,0},{1,17},{17,1},{2,18},{18,2},{3,19},{19,3},{4,20},{20... | collective-permute-start | bytes 1572872 | tf_op jit(solution)/shard_map/ppermute | solution.py:21
  30.4 10.3 %collective-permute-done.9.rest_10_ = bf16[4,128,256]{2,1,0:T(8,128)(2,1)S(1)} collective-permute-done((bf16[4,128,256]{2,1,0:T(8,128)(2,1)S(1)}, bf16[4,128,256]{2,1,0:T(8,128)(2,1)S(1)}, u32[]{:S(2)}, u32[]{:S(2)}) %collective-permute-start.9) | collective-permute-done | bytes 262176 | tf_op jit(solution)/shard_map/ppermute | solution.py:21
  40.7 2.7 %collective-permute-start.2 = (bf16[8,128,256]{2,1,0:T(8,128)(2,1)}, bf16[8,128,256]{2,1,0:T(8,128)(2,1)}, u32[]{:S(2)}, u32[]{:S(2)}) collective-permute-start(bf16[8,128,256]{2,1,0:T(8,128)(2,1)} %collective-permute-done.1.rest_2_), channel_id=1, source_target_pairs={{0,16},{16,0},{1,17},{17,1},{2,18},{18,2},{3,19},{19,3},{4,20},{20... | collective-permute-start | bytes 1572872 | tf_op jit(solution)/shard_map/ppermute | solution.py:21
  43.4 2.0 %collective-permute-start.4 = (bf16[8,128,256]{2,1,0:T(8,128)(2,1)S(1)}, bf16[8,128,256]{2,1,0:T(8,128)(2,1)}, u32[]{:S(2)}, u32[]{:S(2)}) collective-permute-start(bf16[8,128,256]{2,1,0:T(8,128)(2,1)S(1)} %collective-permute-done.3.rest_4_), channel_id=1, source_target_pairs={{0,16},{16,0},{1,17},{17,1},{2,18},{18,2},{3,19},{19,3},{4,20},{20... | collective-permute-start | bytes 1572872 | tf_op jit(solution)/shard_map/ppermute | solution.py:21
  45.9 0.7 slice.66
  47.3 2.1 %collective-permute-start.17 = (bf16[4,128,256]{2,1,0:T(8,128)(2,1)S(1)}, bf16[4,128,256]{2,1,0:T(8,128)(2,1)S(1)}, u32[]{:S(2)}, u32[]{:S(2)}) collective-permute-start(bf16[4,128,256]{2,1,0:T(8,128)(2,1)S(1)} %slice.67), channel_id=1, source_target_pairs={{0,96},{32,0},{64,32},{96,64},{1,97},{33,1},{65,33},{97,65},{2,98}... | collective-permute-start | bytes 786440 | tf_op jit(solution)/shard_map/ppermute | solution.py:21
  50.1 0.7 reduce
  50.8 0.9 collective-permute-start.6
  52.2 0.7 reduce.1
  52.9 2.9 %collective-permute-done.15.rest_16_ = bf16[4,128,256]{2,1,0:T(8,128)(2,1)S(1)} collective-permute-done((bf16[4,128,256]{2,1,0:T(8,128)(2,1)}, bf16[4,128,256]{2,1,0:T(8,128)(2,1)S(1)}, u32[]{:S(2)}, u32[]{:S(2)}) %collective-permute-start.15) | collective-permute-done | bytes 262176 | tf_op jit(solution)/shard_map/ppermute | solution.py:21
  55.8 1.1 collective-permute-start.16
  57.3 0.7 collective-permute-done.16.rest_17_
  58.4 12.8 %tile_product.1 = (bf16[64,128,256]{2,1,0:T(8,128)(2,1)}, bf16[8,128,128]{2,1,0:T(8,128)(2,1)S(1)}, bf16[12,128,128]{2,1,0:T(8,128)(2,1)S(1)}, bf16[12,128,128]{...) custom-call(s32[1]{0:T(128)} %bitcast.62.count_ref, ...), custom_call_target="tpu_custom_call" | custom-call | flops 3221225472 | bytes 31457280 | tf_op jit(solution)/shard_map/tile_product/pallas_call | solution.py:151
  71.3 3.0 %collective-permute-start.26 = (bf16[8,128,128]{2,1,0:T(8,128)(2,1)S(1)}, bf16[8,128,128]{2,1,0:T(8,128)(2,1)S(1)}, u32[]{:S(2)}, u32[]{:S(2)}) collective-permute-start(bf16[8,128,128]{2,1,0:T(8,128)(2,1)S(1)} %get-tuple-element.28), channel_id=1, source_target_pairs={{0,16},{16,0},{1,17},{17,1},{2,18},{18,2},{3,19},{19,3},{4,20},{20... | collective-permute-start | bytes 786440 | tf_op jit(solution)/shard_map/ppermute | solution.py:206
  74.3 3.9 %collective-permute-done.25 = bf16[8,128,128]{2,1,0:T(8,128)(2,1)S(1)} collective-permute-done((bf16[8,128,128]{2,1,0:T(8,128)(2,1)S(1)}, bf16[8,128,128]{2,1,0:T(8,128)(2,1)S(1)}, u32[]{:S(2)}, u32[]{:S(2)}) %collective-permute-start.25) | collective-permute-done | bytes 262176 | tf_op jit(solution)/shard_map/ppermute | solution.py:206
  78.3 6.7 %collective-permute-done.27 = bf16[8,128,128]{2,1,0:T(8,128)(2,1)S(1)} collective-permute-done((bf16[8,128,128]{2,1,0:T(8,128)(2,1)S(1)}, bf16[8,128,128]{2,1,0:T(8,128)(2,1)S(1)}, u32[]{:S(2)}, u32[]{:S(2)}) %collective-permute-start.27) | collective-permute-done | bytes 262176 | tf_op jit(solution)/shard_map/ppermute | solution.py:206
  85.1 6.5 %collective-permute-start.28 = (bf16[2,4,128,128]{3,2,1,0:T(8,128)(2,1)S(1)}, bf16[2,4,128,128]{3,2,1,0:T(8,128)(2,1)S(1)}, u32[]{:S(2)}, u32[]{:S(2)}) collective-permute-start(bf16[2,4,128,128]{3,2,1,0:T(8,128)(2,1)S(1)} %slice_bitcast_fusion), channel_id=1, source_target_pairs={{0,2},{2,4},{4,6},{6,8},{8,10},{10,12},{12,14},{14,0},{16,30},{18,... | collective-permute-start | bytes 786440 | tf_op jit(solution)/shard_map/ppermute | solution.py:247
  91.6 1.3 collective-permute-start.22
  93.5 6.9 %collective-permute-done.28 = bf16[2,4,128,128]{3,2,1,0:T(8,128)(2,1)S(1)} collective-permute-done((bf16[2,4,128,128]{3,2,1,0:T(8,128)(2,1)S(1)}, bf16[2,4,128,128]{3,2,1,0:T(8,128)(2,1)S(1)}, u32[]{:S(2)}, u32[]{:S(2)}) %collective-permute-start.28) | collective-permute-done | bytes 262176 | tf_op jit(solution)/shard_map/ppermute | solution.py:247
  100.4 3.6 %collective-permute-start.29 = (bf16[2,4,128,128]{3,2,1,0:T(8,128)(2,1)S(1)}, bf16[2,4,128,128]{3,2,1,0:T(8,128)(2,1)S(1)}, u32[]{:S(2)}, u32[]{:S(2)}) collective-permute-start(bf16[2,4,128,128]{3,2,1,0:T(8,128)(2,1)S(1)} %fusion), channel_id=1, source_target_pairs={{0,2},{2,4},{4,6},{6,8},{8,10},{10,12},{12,14},{14,0},{16,30},{18,... | collective-permute-start | bytes 786440 | tf_op jit(solution)/shard_map/ppermute | solution.py:247
  104.0 1.1 add.305
  105.2 4.1 %collective-permute-done.24 = bf16[12,128,128]{2,1,0:T(8,128)(2,1)S(1)} collective-permute-done((bf16[12,128,128]{2,1,0:T(8,128)(2,1)}, bf16[12,128,128]{2,1,0:T(8,128)(2,1)S(1)}, u32[]{:S(2)}, u32[]{:S(2)}) %collective-permute-start.24) | collective-permute-done | bytes 393248 | tf_op jit(solution)/shard_map/ppermute | solution.py:206
  109.5 2.4 %collective-permute-done.29 = bf16[2,4,128,128]{3,2,1,0:T(8,128)(2,1)S(1)} collective-permute-done((bf16[2,4,128,128]{3,2,1,0:T(8,128)(2,1)S(1)}, bf16[2,4,128,128]{3,2,1,0:T(8,128)(2,1)S(1)}, u32[]{:S(2)}, u32[]{:S(2)}) %collective-permute-start.29) | collective-permute-done | bytes 262176 | tf_op jit(solution)/shard_map/ppermute | solution.py:247
  111.9 3.6 %collective-permute-start.30 = (bf16[2,4,128,128]{3,2,1,0:T(8,128)(2,1)S(1)}, bf16[2,4,128,128]{3,2,1,0:T(8,128)(2,1)S(1)}, u32[]{:S(2)}, u32[]{:S(2)}) collective-permute-start(bf16[2,4,128,128]{3,2,1,0:T(8,128)(2,1)S(1)} %fusion.1), channel_id=1, source_target_pairs={{0,2},{2,4},{4,6},{6,8},{8,10},{10,12},{12,14},{14,0},{16,30},{18,... | collective-permute-start | bytes 786440 | tf_op jit(solution)/shard_map/ppermute | solution.py:247
  115.5 9.0 %collective-permute-done.30 = bf16[2,4,128,128]{3,2,1,0:T(8,128)(2,1)S(1)} collective-permute-done((bf16[2,4,128,128]{3,2,1,0:T(8,128)(2,1)S(1)}, bf16[2,4,128,128]{3,2,1,0:T(8,128)(2,1)S(1)}, u32[]{:S(2)}, u32[]{:S(2)}) %collective-permute-start.30) | collective-permute-done | bytes 262176 | tf_op jit(solution)/shard_map/ppermute | solution.py:247
  124.5 3.6 %collective-permute-start.31 = (bf16[2,4,128,128]{3,2,1,0:T(8,128)(2,1)S(1)}, bf16[2,4,128,128]{3,2,1,0:T(8,128)(2,1)S(1)}, u32[]{:S(2)}, u32[]{:S(2)}) collective-permute-start(bf16[2,4,128,128]{3,2,1,0:T(8,128)(2,1)S(1)} %fusion.2), channel_id=1, source_target_pairs={{0,2},{2,4},{4,6},{6,8},{8,10},{10,12},{12,14},{14,0},{16,30},{18,... | collective-permute-start | bytes 786440 | tf_op jit(solution)/shard_map/ppermute | solution.py:247
  128.1 2.4 %collective-permute-start.19 = (bf16[12,128,128]{2,1,0:T(8,128)(2,1)S(1)}, bf16[12,128,128]{2,1,0:T(8,128)(2,1)S(1)}, u32[]{:S(2)}, u32[]{:S(2)}) collective-permute-start(bf16[12,128,128]{2,1,0:T(8,128)(2,1)S(1)} %get-tuple-element.19), channel_id=1, source_target_pairs={{0,1},{1,0},{2,3},{3,2},{4,5},{5,4},{6,7},{7,6},{8,9},{9,8},{10,11... | collective-permute-start | bytes 1179656 | tf_op jit(solution)/shard_map/ppermute | solution.py:206
  130.5 1.3 collective-permute-start.20
  131.8 1.7 collective-permute-start.21
  133.5 3.7 %collective-permute-done.31 = bf16[2,4,128,128]{3,2,1,0:T(8,128)(2,1)S(1)} collective-permute-done((bf16[2,4,128,128]{3,2,1,0:T(8,128)(2,1)S(1)}, bf16[2,4,128,128]{3,2,1,0:T(8,128)(2,1)S(1)}, u32[]{:S(2)}, u32[]{:S(2)}) %collective-permute-start.31) | collective-permute-done | bytes 262176 | tf_op jit(solution)/shard_map/ppermute | solution.py:247
  137.2 3.6 %collective-permute-start.32 = (bf16[2,4,128,128]{3,2,1,0:T(8,128)(2,1)S(1)}, bf16[2,4,128,128]{3,2,1,0:T(8,128)(2,1)S(1)}, u32[]{:S(2)}, u32[]{:S(2)}) collective-permute-start(bf16[2,4,128,128]{3,2,1,0:T(8,128)(2,1)S(1)} %fusion.3), channel_id=1, source_target_pairs={{0,2},{2,4},{4,6},{6,8},{8,10},{10,12},{12,14},{14,0},{16,30},{18,... | collective-permute-start | bytes 786440 | tf_op jit(solution)/shard_map/ppermute | solution.py:247
  140.9 7.7 %collective-permute-done.21 = bf16[12,128,128]{2,1,0:T(8,128)(2,1)S(1)} collective-permute-done((bf16[12,128,128]{2,1,0:T(8,128)(2,1)S(1)}, bf16[12,128,128]{2,1,0:T(8,128)(2,1)S(1)}, u32[]{:S(2)}, u32[]{:S(2)}) %collective-permute-start.21) | collective-permute-done | bytes 393248 | tf_op jit(solution)/shard_map/ppermute | solution.py:206
  148.8 1.4 collective-permute-start.33
  150.2 3.9 %collective-permute-done.33 = bf16[2,4,128,128]{3,2,1,0:T(8,128)(2,1)S(1)} collective-permute-done((bf16[2,4,128,128]{3,2,1,0:T(8,128)(2,1)S(1)}, bf16[2,4,128,128]{3,2,1,0:T(8,128)(2,1)S(1)}, u32[]{:S(2)}, u32[]{:S(2)}) %collective-permute-start.33) | collective-permute-done | bytes 262176 | tf_op jit(solution)/shard_map/ppermute | solution.py:247
  154.2 2.6 %collective-permute-start.34 = (bf16[2,4,128,128]{3,2,1,0:T(8,128)(2,1)S(1)}, bf16[2,4,128,128]{3,2,1,0:T(8,128)(2,1)S(1)}, u32[]{:S(2)}, u32[]{:S(2)}) collective-permute-start(bf16[2,4,128,128]{3,2,1,0:T(8,128)(2,1)S(1)} %fusion.5), channel_id=1, source_target_pairs={{0,2},{2,4},{4,6},{6,8},{8,10},{10,12},{12,14},{14,0},{16,30},{18,... | collective-permute-start | bytes 786440 | tf_op jit(solution)/shard_map/ppermute | solution.py:247
  156.7 3.3 %collective-permute-done.34 = bf16[2,4,128,128]{3,2,1,0:T(8,128)(2,1)S(1)} collective-permute-done((bf16[2,4,128,128]{3,2,1,0:T(8,128)(2,1)S(1)}, bf16[2,4,128,128]{3,2,1,0:T(8,128)(2,1)S(1)}, u32[]{:S(2)}, u32[]{:S(2)}) %collective-permute-start.34) | collective-permute-done | bytes 262176 | tf_op jit(solution)/shard_map/ppermute | solution.py:247
  160.1 6.6 %collective-permute-start.35 = (bf16[4,128,128]{2,1,0:T(8,128)(2,1)S(1)}, bf16[4,128,128]{2,1,0:T(8,128)(2,1)S(1)}, u32[]{:S(2)}, u32[]{:S(2)}) collective-permute-start(bf16[4,128,128]{2,1,0:T(8,128)(2,1)S(1)} %slice_bitcast_fusion.8), channel_id=1, source_target_pairs={{0,16},{16,0},{1,17},{17,1},{2,18},{18,2},{3,19},{19,3},{4,20},{20... | collective-permute-start | bytes 393224 | tf_op jit(solution)/shard_map/ppermute | solution.py:206
  166.7 1.0 slice.79
  167.7 1.1 collective-permute-start.36
  168.8 6.8 %collective-permute-done.36 = bf16[4,128,256]{2,1,0:T(8,128)(2,1)S(1)} collective-permute-done((bf16[4,128,256]{2,1,0:T(8,128)(2,1)S(1)}, bf16[4,128,256]{2,1,0:T(8,128)(2,1)S(1)}, u32[]{:S(2)}, u32[]{:S(2)}) %collective-permute-start.36) | collective-permute-done | bytes 262176 | tf_op jit(solution)/shard_map/ppermute | solution.py:206
  175.6 1.0 slice_add_fusion
  176.6 0.8 pad_maximum_fusion.3
  (78 shorter events, 4.3 us)
Async XLA Ops:
  6.5 160.2 %reduce-scatter.2.cloned.1.call-start = ((), (), s32[]{:S(2)}) async-start(), calls=%async_computation.1 | async-start | bytes 4718592 | tf_op jit(solution)/shard_map/reduce_scatter | solution.py:230
  6.5 14.7 %collective-permute-start.1 = (bf16[8,128,256]{2,1,0:T(8,128)(2,1)}, bf16[8,128,256]{2,1,0:T(8,128)(2,1)}, u32[]{:S(2)}, u32[]{:S(2)}) collective-permute-start(bf16[8,128,256]{2,1,0:T(8,128)(2,1)} %bitcast.72), channel_id=1, source_target_pairs={{0,128},{128,0},{1,129},{129,1},{2,130},{130,2},{3,131},{131,3},{4... | collective-permute-start | bytes 1572872 | tf_op jit(solution)/shard_map/ppermute | solution.py:21
  10.3 14.2 %collective-permute-start.5 = (bf16[8,128,256]{2,1,0:T(8,128)(2,1)}, bf16[8,128,256]{2,1,0:T(8,128)(2,1)S(1)}, u32[]{:S(2)}, u32[]{:S(2)}) collective-permute-start(bf16[8,128,256]{2,1,0:T(8,128)(2,1)} %bitcast.73), channel_id=1, source_target_pairs={{0,96},{32,0},{64,32},{96,64},{1,97},{33,1},{65,33},{97,65},{2,98}... | collective-permute-start | bytes 1572872 | tf_op jit(solution)/shard_map/ppermute | solution.py:21
  12.7 14.1 %collective-permute-start.3 = (bf16[8,128,256]{2,1,0:T(8,128)(2,1)}, bf16[8,128,256]{2,1,0:T(8,128)(2,1)S(1)}, u32[]{:S(2)}, u32[]{:S(2)}) collective-permute-start(bf16[8,128,256]{2,1,0:T(8,128)(2,1)} %bitcast.74), channel_id=1, source_target_pairs={{0,32},{32,64},{64,96},{96,0},{1,33},{33,65},{65,97},{97,1},{2,34}... | collective-permute-start | bytes 1572872 | tf_op jit(solution)/shard_map/ppermute | solution.py:21
  21.2 24.2 %collective-permute-start.11 = (bf16[8,128,256]{2,1,0:T(8,128)(2,1)}, bf16[8,128,256]{2,1,0:T(8,128)(2,1)S(1)}, u32[]{:S(2)}, u32[]{:S(2)}) collective-permute-start(bf16[8,128,256]{2,1,0:T(8,128)(2,1)} %collective-permute-done.1.rest_2_), channel_id=1, source_target_pairs={{0,32},{32,64},{64,96},{96,0},{1,33},{33,65},{65,97},{97,1},{2,34}... | collective-permute-start | bytes 1572872 | tf_op jit(solution)/shard_map/ppermute | solution.py:21
  23.2 22.3 %collective-permute-start.13 = (bf16[8,128,256]{2,1,0:T(8,128)(2,1)}, bf16[8,128,256]{2,1,0:T(8,128)(2,1)S(1)}, u32[]{:S(2)}, u32[]{:S(2)}) collective-permute-start(bf16[8,128,256]{2,1,0:T(8,128)(2,1)} %collective-permute-done.1.rest_2_), channel_id=1, source_target_pairs={{0,96},{32,0},{64,32},{96,64},{1,97},{33,1},{65,33},{97,65},{2,98}... | collective-permute-start | bytes 1572872 | tf_op jit(solution)/shard_map/ppermute | solution.py:21
  24.5 33.9 %copy-start = (bf16[8,128,256]{2,1,0:T(8,128)(2,1)}, bf16[8,128,256]{2,1,0:T(8,128)(2,1)S(1)}, u32[]{:S(2)}) copy-start(bf16[8,128,256]{2,1,0:T(8,128)(2,1)S(1)} %collective-permute-done.5.rest_6_) | copy-start | bytes 1572868
  24.5 16.2 %collective-permute-start.9 = (bf16[4,128,256]{2,1,0:T(8,128)(2,1)S(1)}, bf16[4,128,256]{2,1,0:T(8,128)(2,1)S(1)}, u32[]{:S(2)}, u32[]{:S(2)}) collective-permute-start(bf16[4,128,256]{2,1,0:T(8,128)(2,1)S(1)} %slice.65), channel_id=1, source_target_pairs={{0,96},{32,0},{64,32},{96,64},{1,97},{33,1},{65,33},{97,65},{2,98}... | collective-permute-start | bytes 786440 | tf_op jit(solution)/shard_map/ppermute | solution.py:21
  26.8 31.6 %copy-start.1 = (bf16[8,128,256]{2,1,0:T(8,128)(2,1)}, bf16[8,128,256]{2,1,0:T(8,128)(2,1)S(1)}, u32[]{:S(2)}) copy-start(bf16[8,128,256]{2,1,0:T(8,128)(2,1)S(1)} %collective-permute-done.3.rest_4_) | copy-start | bytes 1572868
  26.8 16.5 %collective-permute-start.7 = (bf16[4,128,256]{2,1,0:T(8,128)(2,1)S(1)}, bf16[4,128,256]{2,1,0:T(8,128)(2,1)S(1)}, u32[]{:S(2)}, u32[]{:S(2)}) collective-permute-start(bf16[4,128,256]{2,1,0:T(8,128)(2,1)S(1)} %slice.64), channel_id=1, source_target_pairs={{0,32},{32,64},{64,96},{96,0},{1,33},{33,65},{65,97},{97,1},{2,34}... | collective-permute-start | bytes 786440 | tf_op jit(solution)/shard_map/ppermute | solution.py:21
  26.9 19.7 %collective-permute-start = (bf16[8,128,256]{2,1,0:T(8,128)(2,1)}, bf16[8,128,256]{2,1,0:T(8,128)(2,1)S(1)}, u32[]{:S(2)}, u32[]{:S(2)}) collective-permute-start(bf16[8,128,256]{2,1,0:T(8,128)(2,1)} %bitcast.75), channel_id=1, source_target_pairs={{0,16},{16,0},{1,17},{17,1},{2,18},{18,2},{3,19},{19,3},{4,20},{20... | collective-permute-start | bytes 1572872 | tf_op jit(solution)/shard_map/ppermute | solution.py:21
  40.7 10.9 %collective-permute-start.2 = (bf16[8,128,256]{2,1,0:T(8,128)(2,1)}, bf16[8,128,256]{2,1,0:T(8,128)(2,1)}, u32[]{:S(2)}, u32[]{:S(2)}) collective-permute-start(bf16[8,128,256]{2,1,0:T(8,128)(2,1)} %collective-permute-done.1.rest_2_), channel_id=1, source_target_pairs={{0,16},{16,0},{1,17},{17,1},{2,18},{18,2},{3,19},{19,3},{4,20},{20... | collective-permute-start | bytes 1572872 | tf_op jit(solution)/shard_map/ppermute | solution.py:21
  43.4 8.4 %collective-permute-start.4 = (bf16[8,128,256]{2,1,0:T(8,128)(2,1)S(1)}, bf16[8,128,256]{2,1,0:T(8,128)(2,1)}, u32[]{:S(2)}, u32[]{:S(2)}) collective-permute-start(bf16[8,128,256]{2,1,0:T(8,128)(2,1)S(1)} %collective-permute-done.3.rest_4_), channel_id=1, source_target_pairs={{0,16},{16,0},{1,17},{17,1},{2,18},{18,2},{3,19},{19,3},{4,20},{20... | collective-permute-start | bytes 1572872 | tf_op jit(solution)/shard_map/ppermute | solution.py:21
  45.4 13.0 %copy-start.2 = (bf16[8,128,256]{2,1,0:T(8,128)(2,1)}, bf16[8,128,256]{2,1,0:T(8,128)(2,1)S(1)}, u32[]{:S(2)}) copy-start(bf16[8,128,256]{2,1,0:T(8,128)(2,1)S(1)} %collective-permute-done.11.rest_12_) | copy-start | bytes 1572868
  45.4 1.9 %collective-permute-start.10 = (bf16[4,128,256]{2,1,0:T(8,128)(2,1)S(1)}, bf16[4,128,256]{2,1,0:T(8,128)(2,1)S(1)}, u32[]{:S(2)}, u32[]{:S(2)}) collective-permute-start(bf16[4,128,256]{2,1,0:T(8,128)(2,1)S(1)} %collective-permute-done.9.rest_10_), channel_id=1, source_target_pairs={{0,16},{16,0},{1,17},{17,1},{2,18},{18,2},{3,19},{19,3},{4,20},{20... | collective-permute-start | bytes 786440 | tf_op jit(solution)/shard_map/ppermute | solution.py:21
  45.5 1.8 copy-start.3
  45.5 5.3 %collective-permute-start.8 = (bf16[4,128,256]{2,1,0:T(8,128)(2,1)S(1)}, bf16[4,128,256]{2,1,0:T(8,128)(2,1)S(1)}, u32[]{:S(2)}, u32[]{:S(2)}) collective-permute-start(bf16[4,128,256]{2,1,0:T(8,128)(2,1)S(1)} %collective-permute-done.7.rest_8_), channel_id=1, source_target_pairs={{0,16},{16,0},{1,17},{17,1},{2,18},{18,2},{3,19},{19,3},{4,20},{20... | collective-permute-start | bytes 786440 | tf_op jit(solution)/shard_map/ppermute | solution.py:21
  46.6 2.8 %copy-start.4 = (bf16[8,128,256]{2,1,0:T(8,128)(2,1)}, bf16[8,128,256]{2,1,0:T(8,128)(2,1)S(1)}, u32[]{:S(2)}) copy-start(bf16[8,128,256]{2,1,0:T(8,128)(2,1)S(1)} %collective-permute-done.rest_1_) | copy-start | bytes 1572868
  46.6 9.2 %collective-permute-start.15 = (bf16[4,128,256]{2,1,0:T(8,128)(2,1)}, bf16[4,128,256]{2,1,0:T(8,128)(2,1)S(1)}, u32[]{:S(2)}, u32[]{:S(2)}) collective-permute-start(bf16[4,128,256]{2,1,0:T(8,128)(2,1)} %slice.66), channel_id=1, source_target_pairs={{0,32},{32,64},{64,96},{96,0},{1,33},{33,65},{65,97},{97,1},{2,34}... | collective-permute-start | bytes 786440 | tf_op jit(solution)/shard_map/ppermute | solution.py:21
  47.3 9.6 %collective-permute-start.17 = (bf16[4,128,256]{2,1,0:T(8,128)(2,1)S(1)}, bf16[4,128,256]{2,1,0:T(8,128)(2,1)S(1)}, u32[]{:S(2)}, u32[]{:S(2)}) collective-permute-start(bf16[4,128,256]{2,1,0:T(8,128)(2,1)S(1)} %slice.67), channel_id=1, source_target_pairs={{0,96},{32,0},{64,32},{96,64},{1,97},{33,1},{65,33},{97,65},{2,98}... | collective-permute-start | bytes 786440 | tf_op jit(solution)/shard_map/ppermute | solution.py:21
  50.8 6.5 %collective-permute-start.6 = (bf16[8,128,256]{2,1,0:T(8,128)(2,1)S(1)}, bf16[8,128,256]{2,1,0:T(8,128)(2,1)}, u32[]{:S(2)}, u32[]{:S(2)}) collective-permute-start(bf16[8,128,256]{2,1,0:T(8,128)(2,1)S(1)} %collective-permute-done.5.rest_6_), channel_id=1, source_target_pairs={{0,16},{16,0},{1,17},{17,1},{2,18},{18,2},{3,19},{19,3},{4,20},{20... | collective-permute-start | bytes 1572872 | tf_op jit(solution)/shard_map/ppermute | solution.py:21
  51.6 5.7 %collective-permute-start.12 = (bf16[8,128,256]{2,1,0:T(8,128)(2,1)S(1)}, bf16[8,128,256]{2,1,0:T(8,128)(2,1)}, u32[]{:S(2)}, u32[]{:S(2)}) collective-permute-start(bf16[8,128,256]{2,1,0:T(8,128)(2,1)S(1)} %collective-permute-done.11.rest_12_), channel_id=1, source_target_pairs={{0,16},{16,0},{1,17},{17,1},{2,18},{18,2},{3,19},{19,3},{4,20},{20... | collective-permute-start | bytes 1572872 | tf_op jit(solution)/shard_map/ppermute | solution.py:21
  51.7 5.6 %collective-permute-start.14 = (bf16[8,128,256]{2,1,0:T(8,128)(2,1)}, bf16[8,128,256]{2,1,0:T(8,128)(2,1)}, u32[]{:S(2)}, u32[]{:S(2)}) collective-permute-start(bf16[8,128,256]{2,1,0:T(8,128)(2,1)} %copy-done.3), channel_id=1, source_target_pairs={{0,16},{16,0},{1,17},{17,1},{2,18},{18,2},{3,19},{19,3},{4,20},{20... | collective-permute-start | bytes 1572872 | tf_op jit(solution)/shard_map/ppermute | solution.py:21
  55.8 2.2 %collective-permute-start.16 = (bf16[4,128,256]{2,1,0:T(8,128)(2,1)S(1)}, bf16[4,128,256]{2,1,0:T(8,128)(2,1)S(1)}, u32[]{:S(2)}, u32[]{:S(2)}) collective-permute-start(bf16[4,128,256]{2,1,0:T(8,128)(2,1)S(1)} %collective-permute-done.15.rest_16_), channel_id=1, source_target_pairs={{0,16},{16,0},{1,17},{17,1},{2,18},{18,2},{3,19},{19,3},{4,20},{20... | collective-permute-start | bytes 786440 | tf_op jit(solution)/shard_map/ppermute | solution.py:21
  56.9 1.5 collective-permute-start.18
  71.2 59.3 %copy-start.7 = (bf16[12,128,128]{2,1,0:T(8,128)(2,1)S(1)}, bf16[12,128,128]{2,1,0:T(8,128)(2,1)}, u32[]{:S(2)}) copy-start(bf16[12,128,128]{2,1,0:T(8,128)(2,1)} %get-tuple-element.20) | copy-start | bytes 1179652
  71.2 60.6 %copy-start.6 = (bf16[12,128,128]{2,1,0:T(8,128)(2,1)S(1)}, bf16[12,128,128]{2,1,0:T(8,128)(2,1)}, u32[]{:S(2)}) copy-start(bf16[12,128,128]{2,1,0:T(8,128)(2,1)} %get-tuple-element.21) | copy-start | bytes 1179652
  71.2 69.6 %copy-start.5 = (bf16[12,128,128]{2,1,0:T(8,128)(2,1)S(1)}, bf16[12,128,128]{2,1,0:T(8,128)(2,1)}, u32[]{:S(2)}) copy-start(bf16[12,128,128]{2,1,0:T(8,128)(2,1)} %get-tuple-element.18) | copy-start | bytes 1179652
  71.2 7.0 %collective-permute-start.25 = (bf16[8,128,128]{2,1,0:T(8,128)(2,1)S(1)}, bf16[8,128,128]{2,1,0:T(8,128)(2,1)S(1)}, u32[]{:S(2)}, u32[]{:S(2)}) collective-permute-start(bf16[8,128,128]{2,1,0:T(8,128)(2,1)S(1)} %get-tuple-element.27), channel_id=1, source_target_pairs={{0,1},{1,0},{2,3},{3,2},{4,5},{5,4},{6,7},{7,6},{8,9},{9,8},{10,11... | collective-permute-start | bytes 786440 | tf_op jit(solution)/shard_map/ppermute | solution.py:206
  71.3 7.0 %collective-permute-start.26 = (bf16[8,128,128]{2,1,0:T(8,128)(2,1)S(1)}, bf16[8,128,128]{2,1,0:T(8,128)(2,1)S(1)}, u32[]{:S(2)}, u32[]{:S(2)}) collective-permute-start(bf16[8,128,128]{2,1,0:T(8,128)(2,1)S(1)} %get-tuple-element.28), channel_id=1, source_target_pairs={{0,16},{16,0},{1,17},{17,1},{2,18},{18,2},{3,19},{19,3},{4,20},{20... | collective-permute-start | bytes 786440 | tf_op jit(solution)/shard_map/ppermute | solution.py:206
  74.3 10.7 %collective-permute-start.27 = (bf16[8,128,128]{2,1,0:T(8,128)(2,1)S(1)}, bf16[8,128,128]{2,1,0:T(8,128)(2,1)S(1)}, u32[]{:S(2)}, u32[]{:S(2)}) collective-permute-start(bf16[8,128,128]{2,1,0:T(8,128)(2,1)S(1)} %get-tuple-element.29), channel_id=1, source_target_pairs={{0,17},{1,16},{16,1},{17,0},{2,19},{3,18},{18,3},{19,2},{4,21},{5,... | collective-permute-start | bytes 786440 | tf_op jit(solution)/shard_map/ppermute | solution.py:206
  85.1 15.3 %collective-permute-start.28 = (bf16[2,4,128,128]{3,2,1,0:T(8,128)(2,1)S(1)}, bf16[2,4,128,128]{3,2,1,0:T(8,128)(2,1)S(1)}, u32[]{:S(2)}, u32[]{:S(2)}) collective-permute-start(bf16[2,4,128,128]{3,2,1,0:T(8,128)(2,1)S(1)} %slice_bitcast_fusion), channel_id=1, source_target_pairs={{0,2},{2,4},{4,6},{6,8},{8,10},{10,12},{12,14},{14,0},{16,30},{18,... | collective-permute-start | bytes 786440 | tf_op jit(solution)/shard_map/ppermute | solution.py:247
  91.6 12.4 %collective-permute-start.22 = (bf16[12,128,128]{2,1,0:T(8,128)(2,1)S(1)}, bf16[12,128,128]{2,1,0:T(8,128)(2,1)S(1)}, u32[]{:S(2)}, u32[]{:S(2)}) collective-permute-start(bf16[12,128,128]{2,1,0:T(8,128)(2,1)S(1)} %get-tuple-element.23), channel_id=1, source_target_pairs={{0,1},{1,0},{2,3},{3,2},{4,5},{5,4},{6,7},{7,6},{8,9},{9,8},{10,11... | collective-permute-start | bytes 1179656 | tf_op jit(solution)/shard_map/ppermute | solution.py:206
  92.9 12.2 %collective-permute-start.23 = (bf16[12,128,128]{2,1,0:T(8,128)(2,1)}, bf16[12,128,128]{2,1,0:T(8,128)(2,1)S(1)}, u32[]{:S(2)}, u32[]{:S(2)}) collective-permute-start(bf16[12,128,128]{2,1,0:T(8,128)(2,1)} %get-tuple-element.24), channel_id=1, source_target_pairs={{0,16},{16,0},{1,17},{17,1},{2,18},{18,2},{3,19},{19,3},{4,20},{20... | collective-permute-start | bytes 1179656 | tf_op jit(solution)/shard_map/ppermute | solution.py:206
  92.9 16.3 %collective-permute-start.24 = (bf16[12,128,128]{2,1,0:T(8,128)(2,1)}, bf16[12,128,128]{2,1,0:T(8,128)(2,1)S(1)}, u32[]{:S(2)}, u32[]{:S(2)}) collective-permute-start(bf16[12,128,128]{2,1,0:T(8,128)(2,1)} %get-tuple-element.25), channel_id=1, source_target_pairs={{0,17},{1,16},{16,1},{17,0},{2,19},{3,18},{18,3},{19,2},{4,21},{5,... | collective-permute-start | bytes 1179656 | tf_op jit(solution)/shard_map/ppermute | solution.py:206
  100.4 11.4 %collective-permute-start.29 = (bf16[2,4,128,128]{3,2,1,0:T(8,128)(2,1)S(1)}, bf16[2,4,128,128]{3,2,1,0:T(8,128)(2,1)S(1)}, u32[]{:S(2)}, u32[]{:S(2)}) collective-permute-start(bf16[2,4,128,128]{3,2,1,0:T(8,128)(2,1)S(1)} %fusion), channel_id=1, source_target_pairs={{0,2},{2,4},{4,6},{6,8},{8,10},{10,12},{12,14},{14,0},{16,30},{18,... | collective-permute-start | bytes 786440 | tf_op jit(solution)/shard_map/ppermute | solution.py:247
  111.9 12.6 %collective-permute-start.30 = (bf16[2,4,128,128]{3,2,1,0:T(8,128)(2,1)S(1)}, bf16[2,4,128,128]{3,2,1,0:T(8,128)(2,1)S(1)}, u32[]{:S(2)}, u32[]{:S(2)}) collective-permute-start(bf16[2,4,128,128]{3,2,1,0:T(8,128)(2,1)S(1)} %fusion.1), channel_id=1, source_target_pairs={{0,2},{2,4},{4,6},{6,8},{8,10},{10,12},{12,14},{14,0},{16,30},{18,... | collective-permute-start | bytes 786440 | tf_op jit(solution)/shard_map/ppermute | solution.py:247
  124.5 12.6 %collective-permute-start.31 = (bf16[2,4,128,128]{3,2,1,0:T(8,128)(2,1)S(1)}, bf16[2,4,128,128]{3,2,1,0:T(8,128)(2,1)S(1)}, u32[]{:S(2)}, u32[]{:S(2)}) collective-permute-start(bf16[2,4,128,128]{3,2,1,0:T(8,128)(2,1)S(1)} %fusion.2), channel_id=1, source_target_pairs={{0,2},{2,4},{4,6},{6,8},{8,10},{10,12},{12,14},{14,0},{16,30},{18,... | collective-permute-start | bytes 786440 | tf_op jit(solution)/shard_map/ppermute | solution.py:247
  128.1 12.7 %collective-permute-start.19 = (bf16[12,128,128]{2,1,0:T(8,128)(2,1)S(1)}, bf16[12,128,128]{2,1,0:T(8,128)(2,1)S(1)}, u32[]{:S(2)}, u32[]{:S(2)}) collective-permute-start(bf16[12,128,128]{2,1,0:T(8,128)(2,1)S(1)} %get-tuple-element.19), channel_id=1, source_target_pairs={{0,1},{1,0},{2,3},{3,2},{4,5},{5,4},{6,7},{7,6},{8,9},{9,8},{10,11... | collective-permute-start | bytes 1179656 | tf_op jit(solution)/shard_map/ppermute | solution.py:206
  130.5 10.4 %collective-permute-start.20 = (bf16[12,128,128]{2,1,0:T(8,128)(2,1)S(1)}, bf16[12,128,128]{2,1,0:T(8,128)(2,1)S(1)}, u32[]{:S(2)}, u32[]{:S(2)}) collective-permute-start(bf16[12,128,128]{2,1,0:T(8,128)(2,1)S(1)} %copy-done.7), channel_id=1, source_target_pairs={{0,16},{16,0},{1,17},{17,1},{2,18},{18,2},{3,19},{19,3},{4,20},{20... | collective-permute-start | bytes 1179656 | tf_op jit(solution)/shard_map/ppermute | solution.py:206
  131.8 16.8 %collective-permute-start.21 = (bf16[12,128,128]{2,1,0:T(8,128)(2,1)S(1)}, bf16[12,128,128]{2,1,0:T(8,128)(2,1)S(1)}, u32[]{:S(2)}, u32[]{:S(2)}) collective-permute-start(bf16[12,128,128]{2,1,0:T(8,128)(2,1)S(1)} %copy-done.6), channel_id=1, source_target_pairs={{0,17},{1,16},{16,1},{17,0},{2,19},{3,18},{18,3},{19,2},{4,21},{5,... | collective-permute-start | bytes 1179656 | tf_op jit(solution)/shard_map/ppermute | solution.py:206
  137.2 11.6 %collective-permute-start.32 = (bf16[2,4,128,128]{3,2,1,0:T(8,128)(2,1)S(1)}, bf16[2,4,128,128]{3,2,1,0:T(8,128)(2,1)S(1)}, u32[]{:S(2)}, u32[]{:S(2)}) collective-permute-start(bf16[2,4,128,128]{3,2,1,0:T(8,128)(2,1)S(1)} %fusion.3), channel_id=1, source_target_pairs={{0,2},{2,4},{4,6},{6,8},{8,10},{10,12},{12,14},{14,0},{16,30},{18,... | collective-permute-start | bytes 786440 | tf_op jit(solution)/shard_map/ppermute | solution.py:247
  148.8 5.3 %collective-permute-start.33 = (bf16[2,4,128,128]{3,2,1,0:T(8,128)(2,1)S(1)}, bf16[2,4,128,128]{3,2,1,0:T(8,128)(2,1)S(1)}, u32[]{:S(2)}, u32[]{:S(2)}) collective-permute-start(bf16[2,4,128,128]{3,2,1,0:T(8,128)(2,1)S(1)} %fusion.4), channel_id=1, source_target_pairs={{0,2},{2,4},{4,6},{6,8},{8,10},{10,12},{12,14},{14,0},{16,30},{18,... | collective-permute-start | bytes 786440 | tf_op jit(solution)/shard_map/ppermute | solution.py:247
  154.2 5.9 %collective-permute-start.34 = (bf16[2,4,128,128]{3,2,1,0:T(8,128)(2,1)S(1)}, bf16[2,4,128,128]{3,2,1,0:T(8,128)(2,1)S(1)}, u32[]{:S(2)}, u32[]{:S(2)}) collective-permute-start(bf16[2,4,128,128]{3,2,1,0:T(8,128)(2,1)S(1)} %fusion.5), channel_id=1, source_target_pairs={{0,2},{2,4},{4,6},{6,8},{8,10},{10,12},{12,14},{14,0},{16,30},{18,... | collective-permute-start | bytes 786440 | tf_op jit(solution)/shard_map/ppermute | solution.py:247
  160.1 8.7 %collective-permute-start.35 = (bf16[4,128,128]{2,1,0:T(8,128)(2,1)S(1)}, bf16[4,128,128]{2,1,0:T(8,128)(2,1)S(1)}, u32[]{:S(2)}, u32[]{:S(2)}) collective-permute-start(bf16[4,128,128]{2,1,0:T(8,128)(2,1)S(1)} %slice_bitcast_fusion.8), channel_id=1, source_target_pairs={{0,16},{16,0},{1,17},{17,1},{2,18},{18,2},{3,19},{19,3},{4,20},{20... | collective-permute-start | bytes 393224 | tf_op jit(solution)/shard_map/ppermute | solution.py:206
  167.7 7.9 %collective-permute-start.36 = (bf16[4,128,256]{2,1,0:T(8,128)(2,1)S(1)}, bf16[4,128,256]{2,1,0:T(8,128)(2,1)S(1)}, u32[]{:S(2)}, u32[]{:S(2)}) collective-permute-start(bf16[4,128,256]{2,1,0:T(8,128)(2,1)S(1)} %slice.79), channel_id=1, source_target_pairs={{0,1},{1,0},{2,3},{3,2},{4,5},{5,4},{6,7},{7,6},{8,9},{9,8},{10,11... | collective-permute-start | bytes 786440 | tf_op jit(solution)/shard_map/ppermute | solution.py:206
Sparse Core Ops, SparseCore 0:
  71.3 71.7 reduce-scatter.1
where the time goes:
time: 185 us; the launch traced here: 184 us
  waiting for transfers between devices  81.7 us (44%)
  starting transfers between devices  68 us (37%)
  between operations  14.4 us (8%)
  Pallas kernels  12.8 us (7%)
  other arithmetic  5.71 us (3%)
    ppermute x7, waiting for transfers between devices, on_device(): moving = lax.ppermute(moving, ('c', 'z'), around)  29.2 us
    ppermute x11, waiting for transfers between devices, flip(): return lax.ppermute(array, axes, [(i, n - 1 - i) for i in range(n)])  29.1 us
    ppermute x19, starting transfers between devices, shift(): return lax.ppermute(array, axis, [(i, (i + step) % n) for i in range(n)])  25.2 us
    ppermute x7, starting transfers between devices, on_device(): moving = lax.ppermute(moving, ('c', 'z'), around)  24.8 us
    ppermute x19, waiting for transfers between devices, shift(): return lax.ppermute(array, axis, [(i, (i + step) % n) for i in range(n)])  23.3 us
    ppermute x11, starting transfers between devices, flip(): return lax.ppermute(array, axes, [(i, n - 1 - i) for i in range(n)])  18 us
    pallas_call x1, Pallas kernels, tile_product(): pl.pallas_call(body, out_shape=[early_shape] + [jax.ShapeDtypeStruct(shap...  12.8 us
  transfers between devices with their start and end apart: 38, of which 17 were waited for; matrix products, arithmetic and copies ran while one was open for 3% of the time, Pallas kernels for 0%

commit v1 on v0

--- a/solution.py
+++ b/solution.py
@@ -13,7 +13,7 @@
 BUFFERS = 4
 LATE = 4
 EARLY = 8 - LATE
-MESSAGES = (2, 3, 3)
+HOPS = 4
 
 
 def shift(array, axis, step):
@@ -23,17 +23,15 @@
 
 def tile_product(blocks, packed, count, core, pieces, places):
     bs, width = pieces[0].shape[1:]
-    half = width // 2
     n_pieces, n_cols, n_rows = len(pieces), 128, 128
     late_rows, part_rows = 16 * LATE, 8
     late_parts, parts = late_rows // part_rows, n_rows // part_rows
     lates = []
-    for other, row in ((False, 8 * LATE), (True, 8 * LATE), (False, 0), (True, 0)):
-        first = 0
-        for n in MESSAGES:
-            lates.append((other, row, first, n))
-            first += n
-    shapes = [(n * LATE, bs, half) for *_, n in lates]
+    for row in (8 * LATE, 0):
+        for other in range(2):
+            lates += [(row, other, hop, LATE if hop else LATE // 2) for hop in range(HOPS)]
+        lates.append((row, None, 0, LATE))
+    shapes = [(n, bs, width) for *_, n in lates]
 
     def body(count_ref, core_ref, packed_ref, blocks_ref, *rest):
         piece_refs, out_ref = rest[:n_pieces], rest[n_pieces]
@@ -84,29 +82,26 @@
         def late_copy(i):
             return pltpu.make_async_copy(late_staged[i], late_refs[i], late_sem.at[i])
 
-        def write_late(on_core):
-            for i, (other, row, first, n) in enumerate(lates):
-                up = other == (on_core == 1)
-                lane = 0 if up else half
-
-                def group_of(at, _, i=i, row=row, first=first, up=up, lane=lane):
-                    distance = 7 - first - at if up else lax.rem(first + 1 + at, 8)
-                    for k in range(LATE):
-                        value = acc[row + distance * LATE + k, :, lane : lane + half]
-                        late_staged[i][at * LATE + k] = value.astype(jnp.bfloat16)
+        def write_late():
+            for i, (row, other, hop, n) in enumerate(lates):
+                if other is None:
+                    distance = skip = 0
+                else:
+                    down = 1 - core_ref[0] if other else core_ref[0]
+                    distance = 4 + hop * (2 * down - 1)
+                    skip = 0 if hop else (1 - down) * (LATE // 2)
+
+                def one_row(k, _, i=i, first=row + distance * LATE + skip):
+                    late_staged[i][k] = acc[first + k].astype(jnp.bfloat16)
                     return 0
 
-                lax.fori_loop(0, n, group_of, 0)
+                lax.fori_loop(0, n, one_row, 0)
                 late_copy(i).start()
 
         def write(part, _):
-            @pl.when(jnp.logical_and(part == late_parts - 1, core_ref[0] == 0))
+            @pl.when(part == late_parts - 1)
             def _():
-                write_late(0)
-
-            @pl.when(jnp.logical_and(part == late_parts - 1, core_ref[0] == 1))
-            def _():
-                write_late(1)
+                write_late()
 
             @pl.when(part >= late_parts)
             def _():
@@ -164,7 +159,7 @@
             pltpu.SemaphoreType.DMA((2,)),
             pltpu.SemaphoreType.DMA((len(lates),)),
         ],
-        compiler_params=pltpu.CompilerParams(vmem_limit_bytes=50 * 2**20),
+        compiler_params=pltpu.CompilerParams(vmem_limit_bytes=59 * 2**20),
         cost_estimate=pl.CostEstimate(
             flops=n_rows * 3 * 2 * bs * bs * width, bytes_accessed=30 * 2**20, transcendentals=0
         ),
@@ -229,29 +224,28 @@
     )
     early = lax.psum_scatter(early, "z", scatter_dimension=0, tiled=True)
 
-    n = len(MESSAGES)
+    sent, kept = parts[: 2 * HOPS + 1], parts[2 * HOPS + 1 :]
     joined = []
-    for i in range(n):
-        mine = flip(parts[i], ("yl",))
-        theirs = flip(parts[n + i], ("c", "yl"))
-        kept_theirs = flip(parts[3 * n + i], ("c",))
-        shape = (MESSAGES[i], 1, LATE, bs, width // 2)
-        both = jnp.concatenate(
-            [(parts[2 * n + i] + mine).reshape(shape), (kept_theirs + theirs).reshape(shape)], 1
-        )
-        both = lax.optimization_barrier(both)
-        joined += [both[k] for k in range(MESSAGES[i])]
+    for hop in range(HOPS):
+        mine = flip(sent[hop], ("yl",))
+        theirs = flip(sent[HOPS + hop], ("c", "yl"))
+        kept_theirs = flip(kept[HOPS + hop], ("c",))
+        joined.append(lax.optimization_barrier(jnp.stack([kept[hop] + mine, kept_theirs + theirs])))
+    near = flip(sent[2 * HOPS], ("yl",))
+    around = [(i, (i + 1) % 8) for i in range(8)] + [(8 + i, 8 + (i - 1) % 8) for i in range(8)]
     moving = joined[0]
-    around = [(i, (i + 1) % 8) for i in range(8)] + [(8 + i, 8 + (i - 1) % 8) for i in range(8)]
-    for step in range(7):
+    for hop in range(HOPS):
         moving = lax.ppermute(moving, ("c", "z"), around)
-        moving = joined[step + 1] + moving
-    other_half = flip(moving[1], ("c",))
+        if hop == HOPS - 1:
+            break
+        if hop == 0:
+            below = jnp.pad(moving, ((0, 0), (LATE // 2, 0), (0, 0), (0, 0)))
+            above = jnp.pad(moving, ((0, 0), (0, LATE // 2), (0, 0), (0, 0)))
+            moving = jnp.where(c == 0, below, above)
+        moving = joined[hop + 1] + moving
+    other_side = flip(moving[1], ("c",))
     last = flip(early[EARLY:], ("yl",))
-    own_half = moving[0]
-    low = jnp.where(c == 0, own_half, other_half)
-    high = jnp.where(c == 0, other_half, own_half)
-    late = jnp.concatenate([low, high], 2)
+    late = moving[0] + other_side + (kept[2 * HOPS] + near)
     return jnp.concatenate([late, early[:EARLY] + last], 0).reshape(-1, width)
 
 

time: 185 us -> 178 us (0.962)
  waiting for transfers between devices: 81.7 us -> 74.1 us
  starting transfers between devices: 68 us -> 63.6 us
  other arithmetic: 5.71 us -> 7.83 us
  local copies, waits for them, and re-layouts: 1.79 us -> 3.87 us
    ppermute x11 -> x15, waiting for transfers between devices: 29.1 us -> 11.7 us  [flip(): return lax.ppermute(array, axes, [(i, n - 1 - i) for i in range(n)])]
    ppermute x7 -> x4, waiting for transfers between devices: 29.2 us -> 40.6 us  [on_device(): moving = lax.ppermute(moving, ('c', 'z'), around)]
    ppermute x7 -> x4, starting transfers between devices: 24.8 us -> 14.6 us  [on_device(): moving = lax.ppermute(moving, ('c', 'z'), around)]
    ppermute x11 -> x15, starting transfers between devices: 18 us -> 23.2 us  [flip(): return lax.ppermute(array, axes, [(i, n - 1 - i) for i in range(n)])]
    another operation x0 -> x12, other arithmetic: none -> 3.24 us  [on_device(): jnp.stack([kept[hop] + mine, kept_theirs + theirs])]
  transfers between devices with their start and end apart: 38 -> 39, of which waited for: 17 -> 13; matrix products, arithmetic and copies ran while one was open for 3% -> 5% of each run, Pallas kernels for 0% -> 0%
where the time goes in v1:
time: 178 us; the launch traced here: 177 us
  waiting for transfers between devices  74.1 us (42%)
  starting transfers between devices  63.6 us (36%)
  between operations  14.4 us (8%)
  Pallas kernels  13.5 us (8%)
  other arithmetic  7.83 us (4%)
  local copies, waits for them, and re-layouts  3.87 us (2%)
    ppermute x4, waiting for transfers between devices, on_device(): moving = lax.ppermute(moving, ('c', 'z'), around)  40.6 us
    ppermute x19, starting transfers between devices, shift(): return lax.ppermute(array, axis, [(i, (i + step) % n) for i in range(n)])  25.7 us
    ppermute x15, starting transfers between devices, flip(): return lax.ppermute(array, axes, [(i, n - 1 - i) for i in range(n)])  23.2 us
    ppermute x19, waiting for transfers between devices, shift(): return lax.ppermute(array, axis, [(i, (i + step) % n) for i in range(n)])  21.9 us
    ppermute x4, starting transfers between devices, on_device(): moving = lax.ppermute(moving, ('c', 'z'), around)  14.6 us
    pallas_call x1, Pallas kernels, tile_product(): pl.pallas_call(body, out_shape=[early_shape] + [jax.ShapeDtypeStruct(shap...  13.5 us
    ppermute x15, waiting for transfers between devices, flip(): return lax.ppermute(array, axes, [(i, n - 1 - i) for i in range(n)])  11.7 us
  transfers between devices with their start and end apart: 39, of which 13 were waited for; matrix products, arithmetic and copies ran while one was open for 5% of the time, Pallas kernels for 0%

profile of v1, /device:TPU:1, one launch (start us, length us, event | category | flops | bytes accessed | tf_op | source)
XLA Modules:
  0.0 177.3 jit_solution(4510642895879366088)
XLA Ops:
  6.5 3.7 %collective-permute-start.1 = (bf16[8,128,256]{2,1,0:T(8,128)(2,1)}, bf16[8,128,256]{2,1,0:T(8,128)(2,1)S(1)}, u32[]{:S(2)}, u32[]{:S(2)}) collective-permute-start(bf16[8,128,256]{2,1,0:T(8,128)(2,1)} %bitcast.34), channel_id=1, source_target_pairs={{0,128},{128,0},{1,129},{129,1},{2,130},{130,2},{3,131},{131,3},{4... | collective-permute-start | bytes 1572872 | tf_op jit(solution)/shard_map/ppermute | solution.py:21
  10.3 2.5 %collective-permute-start.5 = (bf16[8,128,256]{2,1,0:T(8,128)(2,1)}, bf16[8,128,256]{2,1,0:T(8,128)(2,1)S(1)}, u32[]{:S(2)}, u32[]{:S(2)}) collective-permute-start(bf16[8,128,256]{2,1,0:T(8,128)(2,1)} %bitcast.35), channel_id=1, source_target_pairs={{0,96},{32,0},{64,32},{96,64},{1,97},{33,1},{65,33},{97,65},{2,98}... | collective-permute-start | bytes 1572872 | tf_op jit(solution)/shard_map/ppermute | solution.py:21
  12.8 8.4 %collective-permute-done.1.rest_2_ = bf16[8,128,256]{2,1,0:T(8,128)(2,1)S(1)} collective-permute-done((bf16[8,128,256]{2,1,0:T(8,128)(2,1)}, bf16[8,128,256]{2,1,0:T(8,128)(2,1)S(1)}, u32[]{:S(2)}, u32[]{:S(2)}) %collective-permute-start.1) | collective-permute-done | bytes 524320 | tf_op jit(solution)/shard_map/ppermute | solution.py:21
  21.2 1.9 %collective-permute-start.11 = (bf16[8,128,256]{2,1,0:T(8,128)(2,1)S(1)}, bf16[8,128,256]{2,1,0:T(8,128)(2,1)S(1)}, u32[]{:S(2)}, u32[]{:S(2)}) collective-permute-start(bf16[8,128,256]{2,1,0:T(8,128)(2,1)S(1)} %collective-permute-done.1.rest_2_), channel_id=1, source_target_pairs={{0,32},{32,64},{64,96},{96,0},{1,33},{33,65},{65,97},{97,1},{2,34}... | collective-permute-start | bytes 1572872 | tf_op jit(solution)/shard_map/ppermute | solution.py:21
  23.1 1.3 collective-permute-start.13
  24.4 2.4 %collective-permute-start.9 = (bf16[4,128,256]{2,1,0:T(8,128)(2,1)S(1)}, bf16[4,128,256]{2,1,0:T(8,128)(2,1)S(1)}, u32[]{:S(2)}, u32[]{:S(2)}) collective-permute-start(bf16[4,128,256]{2,1,0:T(8,128)(2,1)S(1)} %slice.33), channel_id=1, source_target_pairs={{0,96},{32,0},{64,32},{96,64},{1,97},{33,1},{65,33},{97,65},{2,98}... | collective-permute-start | bytes 786440 | tf_op jit(solution)/shard_map/ppermute | solution.py:21
  26.9 3.5 %collective-permute-start = (bf16[8,128,256]{2,1,0:T(8,128)(2,1)}, bf16[8,128,256]{2,1,0:T(8,128)(2,1)S(1)}, u32[]{:S(2)}, u32[]{:S(2)}) collective-permute-start(bf16[8,128,256]{2,1,0:T(8,128)(2,1)} %bitcast.37), channel_id=1, source_target_pairs={{0,16},{16,0},{1,17},{17,1},{2,18},{18,2},{3,19},{19,3},{4,20},{20... | collective-permute-start | bytes 1572872 | tf_op jit(solution)/shard_map/ppermute | solution.py:21
  30.4 10.0 %collective-permute-done.9.rest_10_ = bf16[4,128,256]{2,1,0:T(8,128)(2,1)S(1)} collective-permute-done((bf16[4,128,256]{2,1,0:T(8,128)(2,1)S(1)}, bf16[4,128,256]{2,1,0:T(8,128)(2,1)S(1)}, u32[]{:S(2)}, u32[]{:S(2)}) %collective-permute-start.9) | collective-permute-done | bytes 262176 | tf_op jit(solution)/shard_map/ppermute | solution.py:21
  40.4 2.7 %collective-permute-start.2 = (bf16[8,128,256]{2,1,0:T(8,128)(2,1)S(1)}, bf16[8,128,256]{2,1,0:T(8,128)(2,1)}, u32[]{:S(2)}, u32[]{:S(2)}) collective-permute-start(bf16[8,128,256]{2,1,0:T(8,128)(2,1)S(1)} %collective-permute-done.1.rest_2_), channel_id=1, source_target_pairs={{0,16},{16,0},{1,17},{17,1},{2,18},{18,2},{3,19},{19,3},{4,20},{20... | collective-permute-start | bytes 1572872 | tf_op jit(solution)/shard_map/ppermute | solution.py:21
  43.4 2.1 %collective-permute-start.4 = (bf16[8,128,256]{2,1,0:T(8,128)(2,1)S(1)}, bf16[8,128,256]{2,1,0:T(8,128)(2,1)}, u32[]{:S(2)}, u32[]{:S(2)}) collective-permute-start(bf16[8,128,256]{2,1,0:T(8,128)(2,1)S(1)} %collective-permute-done.3.rest_4_), channel_id=1, source_target_pairs={{0,16},{16,0},{1,17},{17,1},{2,18},{18,2},{3,19},{19,3},{4,20},{20... | collective-permute-start | bytes 1572872 | tf_op jit(solution)/shard_map/ppermute | solution.py:21
  45.6 0.4 collective-permute-start.8
  46.0 0.7 slice.34
  46.7 0.7 slice.35
  47.5 0.7 copy-done.7
  48.2 2.6 %collective-permute-start.17 = (bf16[4,128,256]{2,1,0:T(8,128)(2,1)}, bf16[4,128,256]{2,1,0:T(8,128)(2,1)}, u32[]{:S(2)}, u32[]{:S(2)}) collective-permute-start(bf16[4,128,256]{2,1,0:T(8,128)(2,1)} %slice.35), channel_id=1, source_target_pairs={{0,96},{32,0},{64,32},{96,64},{1,97},{33,1},{65,33},{97,65},{2,98}... | collective-permute-start | bytes 786440 | tf_op jit(solution)/shard_map/ppermute | solution.py:21
  51.5 0.7 reduce
  52.2 0.8 collective-permute-start.6
  53.6 0.7 reduce.1
  54.3 2.3 %collective-permute-done.15.rest_16_ = bf16[4,128,256]{2,1,0:T(8,128)(2,1)} collective-permute-done((bf16[4,128,256]{2,1,0:T(8,128)(2,1)}, bf16[4,128,256]{2,1,0:T(8,128)(2,1)}, u32[]{:S(2)}, u32[]{:S(2)}) %collective-permute-start.15) | collective-permute-done | bytes 262176 | tf_op jit(solution)/shard_map/ppermute | solution.py:21
  56.6 1.1 collective-permute-start.16
  57.9 0.7 select_reduce_fusion.packed_ref
  60.1 13.5 %tile_product.1 = (bf16[64,128,256]{2,1,0:T(8,128)(2,1)}, bf16[2,128,256]{2,1,0:T(8,128)(2,1)}, bf16[4,128,256]{2,1,0:T(8,128)(2,1)}, bf16[4,128,256]{2,1,0:T(8,...) custom-call(s32[1]{0:T(128)} %bitcast.30.count_ref, ...), custom_call_target="tpu_custom_call" | custom-call | flops 3221225472 | bytes 31457280 | tf_op jit(solution)/shard_map/tile_product/pallas_call | solution.py:146
  73.8 2.7 %collective-permute-start.29 = (bf16[2,128,256]{2,1,0:T(8,128)(2,1)}, bf16[2,128,256]{2,1,0:T(8,128)(2,1)S(1)}, u32[]{:S(2)}, u32[]{:S(2)}) collective-permute-start(bf16[2,128,256]{2,1,0:T(8,128)(2,1)} %get-tuple-element.38), channel_id=1, source_target_pairs={{0,16},{16,0},{1,17},{17,1},{2,18},{18,2},{3,19},{19,3},{4,20},{20... | collective-permute-start | bytes 393224 | tf_op jit(solution)/shard_map/ppermute | solution.py:201
  76.6 1.4 collective-permute-start.25
  77.9 0.8 collective-permute-start.26
  78.7 4.0 %collective-permute-start.27 = (bf16[4,128,256]{2,1,0:T(8,128)(2,1)}, bf16[4,128,256]{2,1,0:T(8,128)(2,1)S(1)}, u32[]{:S(2)}, u32[]{:S(2)}) collective-permute-start(bf16[4,128,256]{2,1,0:T(8,128)(2,1)} %get-tuple-element.35), channel_id=1, source_target_pairs={{0,17},{1,16},{16,1},{17,0},{2,19},{3,18},{18,3},{19,2},{4,21},{5,... | collective-permute-start | bytes 786440 | tf_op jit(solution)/shard_map/ppermute | solution.py:201
  82.7 0.9 add_bitcast_fusion.7
  84.2 3.2 %collective-permute-done.25 = bf16[4,128,256]{2,1,0:T(8,128)(2,1)S(1)} collective-permute-done((bf16[4,128,256]{2,1,0:T(8,128)(2,1)}, bf16[4,128,256]{2,1,0:T(8,128)(2,1)S(1)}, u32[]{:S(2)}, u32[]{:S(2)}) %collective-permute-start.25) | collective-permute-done | bytes 262176 | tf_op jit(solution)/shard_map/ppermute | solution.py:201
  87.4 3.7 %collective-permute-start.24 = (bf16[4,128,256]{2,1,0:T(8,128)(2,1)}, bf16[4,128,256]{2,1,0:T(8,128)(2,1)S(1)}, u32[]{:S(2)}, u32[]{:S(2)}) collective-permute-start(bf16[4,128,256]{2,1,0:T(8,128)(2,1)} %get-tuple-element.31), channel_id=1, source_target_pairs={{0,17},{1,16},{16,1},{17,0},{2,19},{3,18},{18,3},{19,2},{4,21},{5,... | collective-permute-start | bytes 786440 | tf_op jit(solution)/shard_map/ppermute | solution.py:201
  91.2 1.0 add_bitcast_fusion.1
  92.3 1.9 %collective-permute-done.27 = bf16[4,128,256]{2,1,0:T(8,128)(2,1)S(1)} collective-permute-done((bf16[4,128,256]{2,1,0:T(8,128)(2,1)}, bf16[4,128,256]{2,1,0:T(8,128)(2,1)S(1)}, u32[]{:S(2)}, u32[]{:S(2)}) %collective-permute-start.27) | collective-permute-done | bytes 262176 | tf_op jit(solution)/shard_map/ppermute | solution.py:201
  94.2 8.0 %collective-permute-start.31 = (bf16[2,2,128,256]{3,2,1,0:T(8,128)(2,1)S(1)}, bf16[2,2,128,256]{3,2,1,0:T(8,128)(2,1)S(1)}, u32[]{:S(2)}, u32[]{:S(2)}) collective-permute-start(bf16[2,2,128,256]{3,2,1,0:T(8,128)(2,1)S(1)} %pad_maximum_fusion.4), channel_id=1, source_target_pairs={{0,2},{2,4},{4,6},{6,8},{8,10},{10,12},{12,14},{14,0},{16,30},{18,... | collective-permute-start | bytes 786440 | tf_op jit(solution)/shard_map/ppermute | solution.py:238
  102.3 8.8 %collective-permute-done.31 = bf16[2,2,128,256]{3,2,1,0:T(8,128)(2,1)S(1)} collective-permute-done((bf16[2,2,128,256]{3,2,1,0:T(8,128)(2,1)S(1)}, bf16[2,2,128,256]{3,2,1,0:T(8,128)(2,1)S(1)}, u32[]{:S(2)}, u32[]{:S(2)}) %collective-permute-start.31) | collective-permute-done | bytes 262176 | tf_op jit(solution)/shard_map/ppermute | solution.py:238
  111.1 3.0 %collective-permute-start.20 = (bf16[4,128,256]{2,1,0:T(8,128)(2,1)}, bf16[4,128,256]{2,1,0:T(8,128)(2,1)S(1)}, u32[]{:S(2)}, u32[]{:S(2)}) collective-permute-start(bf16[4,128,256]{2,1,0:T(8,128)(2,1)} %get-tuple-element.26), channel_id=1, source_target_pairs={{0,16},{16,0},{1,17},{17,1},{2,18},{18,2},{3,19},{19,3},{4,20},{20... | collective-permute-start | bytes 786440 | tf_op jit(solution)/shard_map/ppermute | solution.py:201
  114.2 1.8 %collective-permute-start.32 = (bf16[2,4,128,256]{3,2,1,0:T(8,128)(2,1)S(1)}, bf16[2,4,128,256]{3,2,1,0:T(8,128)(2,1)S(1)}, u32[]{:S(2)}, u32[]{:S(2)}) collective-permute-start(bf16[2,4,128,256]{3,2,1,0:T(8,128)(2,1)S(1)} %select_add_fusion), channel_id=1, source_target_pairs={{0,2},{2,4},{4,6},{6,8},{8,10},{10,12},{12,14},{14,0},{16,30},{18,... | collective-permute-start | bytes 1572872 | tf_op jit(solution)/shard_map/ppermute | solution.py:238
  116.0 1.0 add_bitcast_fusion.3
  117.2 16.8 %collective-permute-done.32 = bf16[2,4,128,256]{3,2,1,0:T(8,128)(2,1)S(1)} collective-permute-done((bf16[2,4,128,256]{3,2,1,0:T(8,128)(2,1)S(1)}, bf16[2,4,128,256]{3,2,1,0:T(8,128)(2,1)S(1)}, u32[]{:S(2)}, u32[]{:S(2)}) %collective-permute-start.32) | collective-permute-done | bytes 524320 | tf_op jit(solution)/shard_map/ppermute | solution.py:238
  134.2 2.9 %collective-permute-start.33 = (bf16[2,4,128,256]{3,2,1,0:T(8,128)(2,1)S(1)}, bf16[2,4,128,256]{3,2,1,0:T(8,128)(2,1)S(1)}, u32[]{:S(2)}, u32[]{:S(2)}) collective-permute-start(bf16[2,4,128,256]{3,2,1,0:T(8,128)(2,1)S(1)} %add.319), channel_id=1, source_target_pairs={{0,2},{2,4},{4,6},{6,8},{8,10},{10,12},{12,14},{14,0},{16,30},{18,... | collective-permute-start | bytes 1572872 | tf_op jit(solution)/shard_map/ppermute | solution.py:238
  137.3 9.6 %collective-permute-done.33 = bf16[2,4,128,256]{3,2,1,0:T(8,128)(2,1)S(1)} collective-permute-done((bf16[2,4,128,256]{3,2,1,0:T(8,128)(2,1)S(1)}, bf16[2,4,128,256]{3,2,1,0:T(8,128)(2,1)S(1)}, u32[]{:S(2)}, u32[]{:S(2)}) %collective-permute-start.33) | collective-permute-done | bytes 524320 | tf_op jit(solution)/shard_map/ppermute | solution.py:238
  147.0 1.8 %collective-permute-start.34 = (bf16[2,4,128,256]{3,2,1,0:T(8,128)(2,1)S(1)}, bf16[2,4,128,256]{3,2,1,0:T(8,128)(2,1)S(1)}, u32[]{:S(2)}, u32[]{:S(2)}) collective-permute-start(bf16[2,4,128,256]{3,2,1,0:T(8,128)(2,1)S(1)} %add.320), channel_id=1, source_target_pairs={{0,2},{2,4},{4,6},{6,8},{8,10},{10,12},{12,14},{14,0},{16,30},{18,... | collective-permute-start | bytes 1572872 | tf_op jit(solution)/shard_map/ppermute | solution.py:238
  148.8 1.2 collective-permute-start.36
  150.0 5.3 %collective-permute-done.34 = bf16[2,4,128,256]{3,2,1,0:T(8,128)(2,1)S(1)} collective-permute-done((bf16[2,4,128,256]{3,2,1,0:T(8,128)(2,1)S(1)}, bf16[2,4,128,256]{3,2,1,0:T(8,128)(2,1)S(1)}, u32[]{:S(2)}, u32[]{:S(2)}) %collective-permute-start.34) | collective-permute-done | bytes 524320 | tf_op jit(solution)/shard_map/ppermute | solution.py:238
  155.4 4.3 %collective-permute-start.35 = (bf16[4,128,256]{2,1,0:T(8,128)(2,1)S(1)}, bf16[4,128,256]{2,1,0:T(8,128)(2,1)S(1)}, u32[]{:S(2)}, u32[]{:S(2)}) collective-permute-start(bf16[4,128,256]{2,1,0:T(8,128)(2,1)S(1)} %slice_bitcast_fusion), channel_id=1, source_target_pairs={{0,16},{16,0},{1,17},{17,1},{2,18},{18,2},{3,19},{19,3},{4,20},{20... | collective-permute-start | bytes 786440 | tf_op jit(solution)/shard_map/ppermute | solution.py:201
  159.7 1.0 slice.39
  160.7 1.3 collective-permute-start.37
  162.0 6.5 %collective-permute-done.37 = bf16[4,128,256]{2,1,0:T(8,128)(2,1)S(1)} collective-permute-done((bf16[4,128,256]{2,1,0:T(8,128)(2,1)S(1)}, bf16[4,128,256]{2,1,0:T(8,128)(2,1)S(1)}, u32[]{:S(2)}, u32[]{:S(2)}) %collective-permute-start.37) | collective-permute-done | bytes 262176 | tf_op jit(solution)/shard_map/ppermute | solution.py:201
  168.6 1.0 slice_add_fusion
  169.6 0.8 pad_maximum_fusion.3
  (88 shorter events, 4.3 us)
Async XLA Ops:
  6.5 153.2 %reduce-scatter.2.cloned.1.call-start = ((), (), s32[]{:S(2)}) async-start(), calls=%async_computation.1 | async-start | bytes 4718592 | tf_op jit(solution)/shard_map/reduce_scatter | solution.py:225
  6.5 14.7 %collective-permute-start.1 = (bf16[8,128,256]{2,1,0:T(8,128)(2,1)}, bf16[8,128,256]{2,1,0:T(8,128)(2,1)S(1)}, u32[]{:S(2)}, u32[]{:S(2)}) collective-permute-start(bf16[8,128,256]{2,1,0:T(8,128)(2,1)} %bitcast.34), channel_id=1, source_target_pairs={{0,128},{128,0},{1,129},{129,1},{2,130},{130,2},{3,131},{131,3},{4... | collective-permute-start | bytes 1572872 | tf_op jit(solution)/shard_map/ppermute | solution.py:21
  10.3 14.1 %collective-permute-start.5 = (bf16[8,128,256]{2,1,0:T(8,128)(2,1)}, bf16[8,128,256]{2,1,0:T(8,128)(2,1)S(1)}, u32[]{:S(2)}, u32[]{:S(2)}) collective-permute-start(bf16[8,128,256]{2,1,0:T(8,128)(2,1)} %bitcast.35), channel_id=1, source_target_pairs={{0,96},{32,0},{64,32},{96,64},{1,97},{33,1},{65,33},{97,65},{2,98}... | collective-permute-start | bytes 1572872 | tf_op jit(solution)/shard_map/ppermute | solution.py:21
  12.7 14.1 %collective-permute-start.3 = (bf16[8,128,256]{2,1,0:T(8,128)(2,1)}, bf16[8,128,256]{2,1,0:T(8,128)(2,1)S(1)}, u32[]{:S(2)}, u32[]{:S(2)}) collective-permute-start(bf16[8,128,256]{2,1,0:T(8,128)(2,1)} %bitcast.36), channel_id=1, source_target_pairs={{0,32},{32,64},{64,96},{96,0},{1,33},{33,65},{65,97},{97,1},{2,34}... | collective-permute-start | bytes 1572872 | tf_op jit(solution)/shard_map/ppermute | solution.py:21
  21.2 38.2 %copy-start.4 = (bf16[8,128,256]{2,1,0:T(8,128)(2,1)}, bf16[8,128,256]{2,1,0:T(8,128)(2,1)S(1)}, u32[]{:S(2)}) copy-start(bf16[8,128,256]{2,1,0:T(8,128)(2,1)S(1)} %collective-permute-done.1.rest_2_) | copy-start | bytes 1572868
  21.2 24.3 %collective-permute-start.11 = (bf16[8,128,256]{2,1,0:T(8,128)(2,1)S(1)}, bf16[8,128,256]{2,1,0:T(8,128)(2,1)S(1)}, u32[]{:S(2)}, u32[]{:S(2)}) collective-permute-start(bf16[8,128,256]{2,1,0:T(8,128)(2,1)S(1)} %collective-permute-done.1.rest_2_), channel_id=1, source_target_pairs={{0,32},{32,64},{64,96},{96,0},{1,33},{33,65},{65,97},{97,1},{2,34}... | collective-permute-start | bytes 1572872 | tf_op jit(solution)/shard_map/ppermute | solution.py:21
  23.1 22.5 %collective-permute-start.13 = (bf16[8,128,256]{2,1,0:T(8,128)(2,1)S(1)}, bf16[8,128,256]{2,1,0:T(8,128)(2,1)S(1)}, u32[]{:S(2)}, u32[]{:S(2)}) collective-permute-start(bf16[8,128,256]{2,1,0:T(8,128)(2,1)S(1)} %collective-permute-done.1.rest_2_), channel_id=1, source_target_pairs={{0,96},{32,0},{64,32},{96,64},{1,97},{33,1},{65,33},{97,65},{2,98}... | collective-permute-start | bytes 1572872 | tf_op jit(solution)/shard_map/ppermute | solution.py:21
  24.4 35.1 %copy-start = (bf16[8,128,256]{2,1,0:T(8,128)(2,1)}, bf16[8,128,256]{2,1,0:T(8,128)(2,1)S(1)}, u32[]{:S(2)}) copy-start(bf16[8,128,256]{2,1,0:T(8,128)(2,1)S(1)} %collective-permute-done.5.rest_6_) | copy-start | bytes 1572868
  24.4 16.0 %collective-permute-start.9 = (bf16[4,128,256]{2,1,0:T(8,128)(2,1)S(1)}, bf16[4,128,256]{2,1,0:T(8,128)(2,1)S(1)}, u32[]{:S(2)}, u32[]{:S(2)}) collective-permute-start(bf16[4,128,256]{2,1,0:T(8,128)(2,1)S(1)} %slice.33), channel_id=1, source_target_pairs={{0,96},{32,0},{64,32},{96,64},{1,97},{33,1},{65,33},{97,65},{2,98}... | collective-permute-start | bytes 786440 | tf_op jit(solution)/shard_map/ppermute | solution.py:21
  26.8 32.6 %copy-start.1 = (bf16[8,128,256]{2,1,0:T(8,128)(2,1)}, bf16[8,128,256]{2,1,0:T(8,128)(2,1)S(1)}, u32[]{:S(2)}) copy-start(bf16[8,128,256]{2,1,0:T(8,128)(2,1)S(1)} %collective-permute-done.3.rest_4_) | copy-start | bytes 1572868
  26.8 16.5 %collective-permute-start.7 = (bf16[4,128,256]{2,1,0:T(8,128)(2,1)S(1)}, bf16[4,128,256]{2,1,0:T(8,128)(2,1)}, u32[]{:S(2)}, u32[]{:S(2)}) collective-permute-start(bf16[4,128,256]{2,1,0:T(8,128)(2,1)S(1)} %slice.32), channel_id=1, source_target_pairs={{0,32},{32,64},{64,96},{96,0},{1,33},{33,65},{65,97},{97,1},{2,34}... | collective-permute-start | bytes 786440 | tf_op jit(solution)/shard_map/ppermute | solution.py:21
  26.9 20.5 %collective-permute-start = (bf16[8,128,256]{2,1,0:T(8,128)(2,1)}, bf16[8,128,256]{2,1,0:T(8,128)(2,1)S(1)}, u32[]{:S(2)}, u32[]{:S(2)}) collective-permute-start(bf16[8,128,256]{2,1,0:T(8,128)(2,1)} %bitcast.37), channel_id=1, source_target_pairs={{0,16},{16,0},{1,17},{17,1},{2,18},{18,2},{3,19},{19,3},{4,20},{20... | collective-permute-start | bytes 1572872 | tf_op jit(solution)/shard_map/ppermute | solution.py:21
  40.4 19.1 %copy-start.6 = (bf16[4,128,256]{2,1,0:T(8,128)(2,1)}, bf16[4,128,256]{2,1,0:T(8,128)(2,1)S(1)}, u32[]{:S(2)}) copy-start(bf16[4,128,256]{2,1,0:T(8,128)(2,1)S(1)} %collective-permute-done.9.rest_10_) | copy-start | bytes 786436
  40.4 12.6 %collective-permute-start.2 = (bf16[8,128,256]{2,1,0:T(8,128)(2,1)S(1)}, bf16[8,128,256]{2,1,0:T(8,128)(2,1)}, u32[]{:S(2)}, u32[]{:S(2)}) collective-permute-start(bf16[8,128,256]{2,1,0:T(8,128)(2,1)S(1)} %collective-permute-done.1.rest_2_), channel_id=1, source_target_pairs={{0,16},{16,0},{1,17},{17,1},{2,18},{18,2},{3,19},{19,3},{4,20},{20... | collective-permute-start | bytes 1572872 | tf_op jit(solution)/shard_map/ppermute | solution.py:21
  43.4 9.8 %collective-permute-start.4 = (bf16[8,128,256]{2,1,0:T(8,128)(2,1)S(1)}, bf16[8,128,256]{2,1,0:T(8,128)(2,1)}, u32[]{:S(2)}, u32[]{:S(2)}) collective-permute-start(bf16[8,128,256]{2,1,0:T(8,128)(2,1)S(1)} %collective-permute-done.3.rest_4_), channel_id=1, source_target_pairs={{0,16},{16,0},{1,17},{17,1},{2,18},{18,2},{3,19},{19,3},{4,20},{20... | collective-permute-start | bytes 1572872 | tf_op jit(solution)/shard_map/ppermute | solution.py:21
  45.5 14.0 %copy-start.2 = (bf16[8,128,256]{2,1,0:T(8,128)(2,1)}, bf16[8,128,256]{2,1,0:T(8,128)(2,1)S(1)}, u32[]{:S(2)}) copy-start(bf16[8,128,256]{2,1,0:T(8,128)(2,1)S(1)} %collective-permute-done.11.rest_12_) | copy-start | bytes 1572868
  45.5 2.0 %collective-permute-start.10 = (bf16[4,128,256]{2,1,0:T(8,128)(2,1)S(1)}, bf16[4,128,256]{2,1,0:T(8,128)(2,1)S(1)}, u32[]{:S(2)}, u32[]{:S(2)}) collective-permute-start(bf16[4,128,256]{2,1,0:T(8,128)(2,1)S(1)} %collective-permute-done.9.rest_10_), channel_id=1, source_target_pairs={{0,16},{16,0},{1,17},{17,1},{2,18},{18,2},{3,19},{19,3},{4,20},{20... | collective-permute-start | bytes 786440 | tf_op jit(solution)/shard_map/ppermute | solution.py:21
  45.6 13.9 %copy-start.3 = (bf16[8,128,256]{2,1,0:T(8,128)(2,1)}, bf16[8,128,256]{2,1,0:T(8,128)(2,1)S(1)}, u32[]{:S(2)}) copy-start(bf16[8,128,256]{2,1,0:T(8,128)(2,1)S(1)} %collective-permute-done.13.rest_14_) | copy-start | bytes 1572868
  45.6 6.6 %collective-permute-start.8 = (bf16[4,128,256]{2,1,0:T(8,128)(2,1)}, bf16[4,128,256]{2,1,0:T(8,128)(2,1)}, u32[]{:S(2)}, u32[]{:S(2)}) collective-permute-start(bf16[4,128,256]{2,1,0:T(8,128)(2,1)} %collective-permute-done.7.rest_8_), channel_id=1, source_target_pairs={{0,16},{16,0},{1,17},{17,1},{2,18},{18,2},{3,19},{19,3},{4,20},{20... | collective-permute-start | bytes 786440 | tf_op jit(solution)/shard_map/ppermute | solution.py:21
  47.4 9.2 %collective-permute-start.15 = (bf16[4,128,256]{2,1,0:T(8,128)(2,1)}, bf16[4,128,256]{2,1,0:T(8,128)(2,1)}, u32[]{:S(2)}, u32[]{:S(2)}) collective-permute-start(bf16[4,128,256]{2,1,0:T(8,128)(2,1)} %slice.34), channel_id=1, source_target_pairs={{0,32},{32,64},{64,96},{96,0},{1,33},{33,65},{65,97},{97,1},{2,34}... | collective-permute-start | bytes 786440 | tf_op jit(solution)/shard_map/ppermute | solution.py:21
  48.2 9.5 %collective-permute-start.17 = (bf16[4,128,256]{2,1,0:T(8,128)(2,1)}, bf16[4,128,256]{2,1,0:T(8,128)(2,1)}, u32[]{:S(2)}, u32[]{:S(2)}) collective-permute-start(bf16[4,128,256]{2,1,0:T(8,128)(2,1)} %slice.35), channel_id=1, source_target_pairs={{0,96},{32,0},{64,32},{96,64},{1,97},{33,1},{65,33},{97,65},{2,98}... | collective-permute-start | bytes 786440 | tf_op jit(solution)/shard_map/ppermute | solution.py:21
  52.2 6.5 %collective-permute-start.6 = (bf16[8,128,256]{2,1,0:T(8,128)(2,1)S(1)}, bf16[8,128,256]{2,1,0:T(8,128)(2,1)}, u32[]{:S(2)}, u32[]{:S(2)}) collective-permute-start(bf16[8,128,256]{2,1,0:T(8,128)(2,1)S(1)} %collective-permute-done.5.rest_6_), channel_id=1, source_target_pairs={{0,16},{16,0},{1,17},{17,1},{2,18},{18,2},{3,19},{19,3},{4,20},{20... | collective-permute-start | bytes 1572872 | tf_op jit(solution)/shard_map/ppermute | solution.py:21
  53.0 5.6 %collective-permute-start.12 = (bf16[8,128,256]{2,1,0:T(8,128)(2,1)S(1)}, bf16[8,128,256]{2,1,0:T(8,128)(2,1)}, u32[]{:S(2)}, u32[]{:S(2)}) collective-permute-start(bf16[8,128,256]{2,1,0:T(8,128)(2,1)S(1)} %collective-permute-done.11.rest_12_), channel_id=1, source_target_pairs={{0,16},{16,0},{1,17},{17,1},{2,18},{18,2},{3,19},{19,3},{4,20},{20... | collective-permute-start | bytes 1572872 | tf_op jit(solution)/shard_map/ppermute | solution.py:21
  53.1 5.5 %collective-permute-start.14 = (bf16[8,128,256]{2,1,0:T(8,128)(2,1)S(1)}, bf16[8,128,256]{2,1,0:T(8,128)(2,1)}, u32[]{:S(2)}, u32[]{:S(2)}) collective-permute-start(bf16[8,128,256]{2,1,0:T(8,128)(2,1)S(1)} %collective-permute-done.13.rest_14_), channel_id=1, source_target_pairs={{0,16},{16,0},{1,17},{17,1},{2,18},{18,2},{3,19},{19,3},{4,20},{20... | collective-permute-start | bytes 1572872 | tf_op jit(solution)/shard_map/ppermute | solution.py:21
  56.6 2.4 %collective-permute-start.16 = (bf16[4,128,256]{2,1,0:T(8,128)(2,1)}, bf16[4,128,256]{2,1,0:T(8,128)(2,1)S(1)}, u32[]{:S(2)}, u32[]{:S(2)}) collective-permute-start(bf16[4,128,256]{2,1,0:T(8,128)(2,1)} %collective-permute-done.15.rest_16_), channel_id=1, source_target_pairs={{0,16},{16,0},{1,17},{17,1},{2,18},{18,2},{3,19},{19,3},{4,20},{20... | collective-permute-start | bytes 786440 | tf_op jit(solution)/shard_map/ppermute | solution.py:21
  57.7 1.7 collective-permute-start.18
  73.7 63.5 %copy-start.11 = (bf16[4,128,256]{2,1,0:T(8,128)(2,1)S(1)}, bf16[4,128,256]{2,1,0:T(8,128)(2,1)}, u32[]{:S(2)}) copy-start(bf16[4,128,256]{2,1,0:T(8,128)(2,1)} %get-tuple-element.24) | copy-start | bytes 786436
  73.7 75.2 %copy-start.12 = (bf16[4,128,256]{2,1,0:T(8,128)(2,1)S(1)}, bf16[4,128,256]{2,1,0:T(8,128)(2,1)}, u32[]{:S(2)}) copy-start(bf16[4,128,256]{2,1,0:T(8,128)(2,1)} %get-tuple-element.41) | copy-start | bytes 786436
  73.7 88.3 %copy-start.10 = (bf16[4,128,256]{2,1,0:T(8,128)(2,1)S(1)}, bf16[4,128,256]{2,1,0:T(8,128)(2,1)}, u32[]{:S(2)}) copy-start(bf16[4,128,256]{2,1,0:T(8,128)(2,1)} %get-tuple-element.40) | copy-start | bytes 786436
  73.7 5.0 %collective-permute-start.28 = (bf16[2,128,256]{2,1,0:T(8,128)(2,1)}, bf16[2,128,256]{2,1,0:T(8,128)(2,1)S(1)}, u32[]{:S(2)}, u32[]{:S(2)}) collective-permute-start(bf16[2,128,256]{2,1,0:T(8,128)(2,1)} %get-tuple-element.37), channel_id=1, source_target_pairs={{0,1},{1,0},{2,3},{3,2},{4,5},{5,4},{6,7},{7,6},{8,9},{9,8},{10,11... | collective-permute-start | bytes 393224 | tf_op jit(solution)/shard_map/ppermute | solution.py:201
  73.8 9.8 %collective-permute-start.29 = (bf16[2,128,256]{2,1,0:T(8,128)(2,1)}, bf16[2,128,256]{2,1,0:T(8,128)(2,1)S(1)}, u32[]{:S(2)}, u32[]{:S(2)}) collective-permute-start(bf16[2,128,256]{2,1,0:T(8,128)(2,1)} %get-tuple-element.38), channel_id=1, source_target_pairs={{0,16},{16,0},{1,17},{17,1},{2,18},{18,2},{3,19},{19,3},{4,20},{20... | collective-permute-start | bytes 393224 | tf_op jit(solution)/shard_map/ppermute | solution.py:201
  76.5 7.2 %collective-permute-start.30 = (bf16[2,128,256]{2,1,0:T(8,128)(2,1)}, bf16[2,128,256]{2,1,0:T(8,128)(2,1)S(1)}, u32[]{:S(2)}, u32[]{:S(2)}) collective-permute-start(bf16[2,128,256]{2,1,0:T(8,128)(2,1)} %get-tuple-element.39), channel_id=1, source_target_pairs={{0,17},{1,16},{16,1},{17,0},{2,19},{3,18},{18,3},{19,2},{4,21},{5,... | collective-permute-start | bytes 393224 | tf_op jit(solution)/shard_map/ppermute | solution.py:201
  76.6 10.9 %collective-permute-start.25 = (bf16[4,128,256]{2,1,0:T(8,128)(2,1)}, bf16[4,128,256]{2,1,0:T(8,128)(2,1)S(1)}, u32[]{:S(2)}, u32[]{:S(2)}) collective-permute-start(bf16[4,128,256]{2,1,0:T(8,128)(2,1)} %get-tuple-element.33), channel_id=1, source_target_pairs={{0,1},{1,0},{2,3},{3,2},{4,5},{5,4},{6,7},{7,6},{8,9},{9,8},{10,11... | collective-permute-start | bytes 786440 | tf_op jit(solution)/shard_map/ppermute | solution.py:201
  77.9 14.3 %collective-permute-start.26 = (bf16[4,128,256]{2,1,0:T(8,128)(2,1)}, bf16[4,128,256]{2,1,0:T(8,128)(2,1)S(1)}, u32[]{:S(2)}, u32[]{:S(2)}) collective-permute-start(bf16[4,128,256]{2,1,0:T(8,128)(2,1)} %get-tuple-element.34), channel_id=1, source_target_pairs={{0,16},{16,0},{1,17},{17,1},{2,18},{18,2},{3,19},{19,3},{4,20},{20... | collective-permute-start | bytes 786440 | tf_op jit(solution)/shard_map/ppermute | solution.py:201
  78.7 15.5 %collective-permute-start.27 = (bf16[4,128,256]{2,1,0:T(8,128)(2,1)}, bf16[4,128,256]{2,1,0:T(8,128)(2,1)S(1)}, u32[]{:S(2)}, u32[]{:S(2)}) collective-permute-start(bf16[4,128,256]{2,1,0:T(8,128)(2,1)} %get-tuple-element.35), channel_id=1, source_target_pairs={{0,17},{1,16},{16,1},{17,0},{2,19},{3,18},{18,3},{19,2},{4,21},{5,... | collective-permute-start | bytes 786440 | tf_op jit(solution)/shard_map/ppermute | solution.py:201
  83.7 30.5 %collective-permute-start.22 = (bf16[4,128,256]{2,1,0:T(8,128)(2,1)}, bf16[4,128,256]{2,1,0:T(8,128)(2,1)S(1)}, u32[]{:S(2)}, u32[]{:S(2)}) collective-permute-start(bf16[4,128,256]{2,1,0:T(8,128)(2,1)} %get-tuple-element.29), channel_id=1, source_target_pairs={{0,1},{1,0},{2,3},{3,2},{4,5},{5,4},{6,7},{7,6},{8,9},{9,8},{10,11... | collective-permute-start | bytes 786440 | tf_op jit(solution)/shard_map/ppermute | solution.py:201
  83.8 33.2 %collective-permute-start.23 = (bf16[4,128,256]{2,1,0:T(8,128)(2,1)}, bf16[4,128,256]{2,1,0:T(8,128)(2,1)S(1)}, u32[]{:S(2)}, u32[]{:S(2)}) collective-permute-start(bf16[4,128,256]{2,1,0:T(8,128)(2,1)} %get-tuple-element.30), channel_id=1, source_target_pairs={{0,16},{16,0},{1,17},{17,1},{2,18},{18,2},{3,19},{19,3},{4,20},{20... | collective-permute-start | bytes 786440 | tf_op jit(solution)/shard_map/ppermute | solution.py:201
  87.4 29.7 %collective-permute-start.24 = (bf16[4,128,256]{2,1,0:T(8,128)(2,1)}, bf16[4,128,256]{2,1,0:T(8,128)(2,1)S(1)}, u32[]{:S(2)}, u32[]{:S(2)}) collective-permute-start(bf16[4,128,256]{2,1,0:T(8,128)(2,1)} %get-tuple-element.31), channel_id=1, source_target_pairs={{0,17},{1,16},{16,1},{17,0},{2,19},{3,18},{18,3},{19,2},{4,21},{5,... | collective-permute-start | bytes 786440 | tf_op jit(solution)/shard_map/ppermute | solution.py:201
  92.2 44.9 %collective-permute-start.19 = (bf16[4,128,256]{2,1,0:T(8,128)(2,1)}, bf16[4,128,256]{2,1,0:T(8,128)(2,1)S(1)}, u32[]{:S(2)}, u32[]{:S(2)}) collective-permute-start(bf16[4,128,256]{2,1,0:T(8,128)(2,1)} %get-tuple-element.25), channel_id=1, source_target_pairs={{0,1},{1,0},{2,3},{3,2},{4,5},{5,4},{6,7},{7,6},{8,9},{9,8},{10,11... | collective-permute-start | bytes 786440 | tf_op jit(solution)/shard_map/ppermute | solution.py:201
  94.2 16.9 %collective-permute-start.31 = (bf16[2,2,128,256]{3,2,1,0:T(8,128)(2,1)S(1)}, bf16[2,2,128,256]{3,2,1,0:T(8,128)(2,1)S(1)}, u32[]{:S(2)}, u32[]{:S(2)}) collective-permute-start(bf16[2,2,128,256]{3,2,1,0:T(8,128)(2,1)S(1)} %pad_maximum_fusion.4), channel_id=1, source_target_pairs={{0,2},{2,4},{4,6},{6,8},{8,10},{10,12},{12,14},{14,0},{16,30},{18,... | collective-permute-start | bytes 786440 | tf_op jit(solution)/shard_map/ppermute | solution.py:238
  111.1 26.1 %collective-permute-start.20 = (bf16[4,128,256]{2,1,0:T(8,128)(2,1)}, bf16[4,128,256]{2,1,0:T(8,128)(2,1)S(1)}, u32[]{:S(2)}, u32[]{:S(2)}) collective-permute-start(bf16[4,128,256]{2,1,0:T(8,128)(2,1)} %get-tuple-element.26), channel_id=1, source_target_pairs={{0,16},{16,0},{1,17},{17,1},{2,18},{18,2},{3,19},{19,3},{4,20},{20... | collective-permute-start | bytes 786440 | tf_op jit(solution)/shard_map/ppermute | solution.py:201
  114.2 19.9 %collective-permute-start.32 = (bf16[2,4,128,256]{3,2,1,0:T(8,128)(2,1)S(1)}, bf16[2,4,128,256]{3,2,1,0:T(8,128)(2,1)S(1)}, u32[]{:S(2)}, u32[]{:S(2)}) collective-permute-start(bf16[2,4,128,256]{3,2,1,0:T(8,128)(2,1)S(1)} %select_add_fusion), channel_id=1, source_target_pairs={{0,2},{2,4},{4,6},{6,8},{8,10},{10,12},{12,14},{14,0},{16,30},{18,... | collective-permute-start | bytes 1572872 | tf_op jit(solution)/shard_map/ppermute | solution.py:238
  117.0 20.2 %collective-permute-start.21 = (bf16[4,128,256]{2,1,0:T(8,128)(2,1)}, bf16[4,128,256]{2,1,0:T(8,128)(2,1)S(1)}, u32[]{:S(2)}, u32[]{:S(2)}) collective-permute-start(bf16[4,128,256]{2,1,0:T(8,128)(2,1)} %get-tuple-element.27), channel_id=1, source_target_pairs={{0,17},{1,16},{16,1},{17,0},{2,19},{3,18},{18,3},{19,2},{4,21},{5,... | collective-permute-start | bytes 786440 | tf_op jit(solution)/shard_map/ppermute | solution.py:201
  134.2 12.7 %collective-permute-start.33 = (bf16[2,4,128,256]{3,2,1,0:T(8,128)(2,1)S(1)}, bf16[2,4,128,256]{3,2,1,0:T(8,128)(2,1)S(1)}, u32[]{:S(2)}, u32[]{:S(2)}) collective-permute-start(bf16[2,4,128,256]{3,2,1,0:T(8,128)(2,1)S(1)} %add.319), channel_id=1, source_target_pairs={{0,2},{2,4},{4,6},{6,8},{8,10},{10,12},{12,14},{14,0},{16,30},{18,... | collective-permute-start | bytes 1572872 | tf_op jit(solution)/shard_map/ppermute | solution.py:238
  147.0 8.4 %collective-permute-start.34 = (bf16[2,4,128,256]{3,2,1,0:T(8,128)(2,1)S(1)}, bf16[2,4,128,256]{3,2,1,0:T(8,128)(2,1)S(1)}, u32[]{:S(2)}, u32[]{:S(2)}) collective-permute-start(bf16[2,4,128,256]{3,2,1,0:T(8,128)(2,1)S(1)} %add.320), channel_id=1, source_target_pairs={{0,2},{2,4},{4,6},{6,8},{8,10},{10,12},{12,14},{14,0},{16,30},{18,... | collective-permute-start | bytes 1572872 | tf_op jit(solution)/shard_map/ppermute | solution.py:238
  148.8 13.1 %collective-permute-start.36 = (bf16[4,128,256]{2,1,0:T(8,128)(2,1)S(1)}, bf16[4,128,256]{2,1,0:T(8,128)(2,1)S(1)}, u32[]{:S(2)}, u32[]{:S(2)}) collective-permute-start(bf16[4,128,256]{2,1,0:T(8,128)(2,1)S(1)} %copy-done.12), channel_id=1, source_target_pairs={{0,1},{1,0},{2,3},{3,2},{4,5},{5,4},{6,7},{7,6},{8,9},{9,8},{10,11... | collective-permute-start | bytes 786440 | tf_op jit(solution)/shard_map/ppermute | solution.py:201
  155.4 6.6 %collective-permute-start.35 = (bf16[4,128,256]{2,1,0:T(8,128)(2,1)S(1)}, bf16[4,128,256]{2,1,0:T(8,128)(2,1)S(1)}, u32[]{:S(2)}, u32[]{:S(2)}) collective-permute-start(bf16[4,128,256]{2,1,0:T(8,128)(2,1)S(1)} %slice_bitcast_fusion), channel_id=1, source_target_pairs={{0,16},{16,0},{1,17},{17,1},{2,18},{18,2},{3,19},{19,3},{4,20},{20... | collective-permute-start | bytes 786440 | tf_op jit(solution)/shard_map/ppermute | solution.py:201
  160.7 7.9 %collective-permute-start.37 = (bf16[4,128,256]{2,1,0:T(8,128)(2,1)S(1)}, bf16[4,128,256]{2,1,0:T(8,128)(2,1)S(1)}, u32[]{:S(2)}, u32[]{:S(2)}) collective-permute-start(bf16[4,128,256]{2,1,0:T(8,128)(2,1)S(1)} %slice.39), channel_id=1, source_target_pairs={{0,1},{1,0},{2,3},{3,2},{4,5},{5,4},{6,7},{7,6},{8,9},{9,8},{10,11... | collective-permute-start | bytes 786440 | tf_op jit(solution)/shard_map/ppermute | solution.py:201
  (4 other events, 14.2 us)
Sparse Core Ops, SparseCore 0:
  73.8 70.8 reduce-scatter.1

commit v2 on v1

--- a/solution.py
+++ b/solution.py
@@ -169,15 +169,20 @@
 
 def gather_panel(own):
     half = own.shape[0] // 2
-    got = [(own, 0, 0, 0)]
+
+    def around_x(part, dyh, at):
+        middle = part.shape[0] // 2
+        before, after = shift(part, "x", 1), shift(part, "x", -1)
+        low, high = before[:middle], after[middle:]
+        far = [(shift(low, "x", 1), dyh, 2, at), (shift(high, "x", -1), dyh, 2, at + middle)]
+        return before, after, low, [(before, dyh, 3, at), (after, dyh, 1, at), *far]
+
     across = shift(own, "yh", 1)
-    got.append((across, 1, 0, 0))
-    for part, dyh in ((own, 0), (across, 1)):
-        before = shift(part, "x", 1)
-        after = shift(part, "x", -1)
-        far_low = shift(before[:half], "x", 1)
-        far_high = shift(after[half:], "x", -1)
-        got += [(before, dyh, 3, 0), (after, dyh, 1, 0), (far_low, dyh, 2, 0), (far_high, dyh, 2, half)]
+    _, after, low, near_side = around_x(own, 0, 0)
+    got = [(own, 0, 0, 0), (across, 1, 0, 0), *near_side]
+    got += [(shift(low, "yh", 1), 1, 3, 0), (shift(after[:half], "yh", 1), 1, 1, 0)]
+    got.append((shift(near_side[2][0], "yh", 1), 1, 2, 0))
+    got += around_x(across[half:], 1, half)[3]
     pieces, places = [], []
     for part, dyh, dx, at in got:
         for dc in range(2):

time: 178 us -> 175 us (0.983)
  waiting for transfers between devices: 74.1 us -> 69.8 us
  starting transfers between devices: 63.6 us -> 67.6 us
  local copies, waits for them, and re-layouts: 3.87 us -> 1.78 us
    ppermute x19 -> x25, starting transfers between devices: 25.7 us -> 30.2 us  [shift(): return lax.ppermute(array, axis, [(i, (i + step) % n) for i in range(n)])]
    ppermute x4, waiting for transfers between devices: 40.6 us -> 38 us  [on_device(): moving = lax.ppermute(moving, ('c', 'z'), around)]
    ppermute x19 -> x25, waiting for transfers between devices: 21.9 us -> 19.5 us  [shift(): return lax.ppermute(array, axis, [(i, (i + step) % n) for i in range(n)])]
  transfers between devices with their start and end apart: 39 -> 45, of which waited for: 13 -> 15; matrix products, arithmetic and copies ran while one was open for 5% -> 4% of each run, Pallas kernels for 0% -> 0%
where the time goes in v2:
time: 175 us
  waiting for transfers between devices  69.8 us (40%)
  starting transfers between devices  67.6 us (39%)
  between operations  14.4 us (8%)
  Pallas kernels  13.6 us (8%)
  other arithmetic  7.84 us (4%)
  local copies, waits for them, and re-layouts  1.78 us (1%)
    ppermute x4, waiting for transfers between devices, on_device(): moving = lax.ppermute(moving, ('c', 'z'), around)  38 us
    ppermute x25, starting transfers between devices, shift(): return lax.ppermute(array, axis, [(i, (i + step) % n) for i in range(n)])  30.2 us
    ppermute x15, starting transfers between devices, flip(): return lax.ppermute(array, axes, [(i, n - 1 - i) for i in range(n)])  22.4 us
    ppermute x25, waiting for transfers between devices, shift(): return lax.ppermute(array, axis, [(i, (i + step) % n) for i in range(n)])  19.5 us
    ppermute x4, starting transfers between devices, on_device(): moving = lax.ppermute(moving, ('c', 'z'), around)  15.1 us
    pallas_call x1, Pallas kernels, tile_product(): pl.pallas_call(body, out_shape=[early_shape] + [jax.ShapeDtypeStruct(shap...  13.6 us
    ppermute x15, waiting for transfers between devices, flip(): return lax.ppermute(array, axes, [(i, n - 1 - i) for i in range(n)])  12.3 us
  transfers between devices with their start and end apart: 45, of which 15 were waited for; matrix products, arithmetic and copies ran while one was open for 4% of the time, Pallas kernels for 0%

profile of v2, /device:TPU:1, one launch (start us, length us, event | category | flops | bytes accessed | tf_op | source)
XLA Modules:
  0.0 175.1 jit_solution(11627769023630220208)
XLA Ops:
  6.5 3.7 %collective-permute-start.1 = (bf16[8,128,256]{2,1,0:T(8,128)(2,1)}, bf16[8,128,256]{2,1,0:T(8,128)(2,1)S(1)}, u32[]{:S(2)}, u32[]{:S(2)}) collective-permute-start(bf16[8,128,256]{2,1,0:T(8,128)(2,1)} %bitcast.34), channel_id=1, source_target_pairs={{0,128},{128,0},{1,129},{129,1},{2,130},{130,2},{3,131},{131,3},{4... | collective-permute-start | bytes 1572872 | tf_op jit(solution)/shard_map/ppermute | solution.py:21
  10.3 1.2 collective-permute-start.3
  11.5 1.5 collective-permute-start.5
  12.9 1.5 collective-permute-start
  14.5 6.7 %collective-permute-done.1.rest_2_ = bf16[8,128,256]{2,1,0:T(8,128)(2,1)S(1)} collective-permute-done((bf16[8,128,256]{2,1,0:T(8,128)(2,1)}, bf16[8,128,256]{2,1,0:T(8,128)(2,1)S(1)}, u32[]{:S(2)}, u32[]{:S(2)}) %collective-permute-start.1) | collective-permute-done | bytes 524320 | tf_op jit(solution)/shard_map/ppermute | solution.py:21
  21.2 2.0 %collective-permute-start.17 = (bf16[4,128,256]{2,1,0:T(8,128)(2,1)S(1)}, bf16[4,128,256]{2,1,0:T(8,128)(2,1)S(1)}, u32[]{:S(2)}, u32[]{:S(2)}) collective-permute-start(bf16[4,128,256]{2,1,0:T(8,128)(2,1)S(1)} %slice.43), channel_id=1, source_target_pairs={{0,32},{32,64},{64,96},{96,0},{1,33},{33,65},{65,97},{97,1},{2,34}... | collective-permute-start | bytes 786440 | tf_op jit(solution)/shard_map/ppermute | solution.py:21
  23.2 1.4 collective-permute-start.19
  24.8 2.6 %collective-permute-start.9 = (bf16[4,128,256]{2,1,0:T(8,128)(2,1)S(1)}, bf16[4,128,256]{2,1,0:T(8,128)(2,1)}, u32[]{:S(2)}, u32[]{:S(2)}) collective-permute-start(bf16[4,128,256]{2,1,0:T(8,128)(2,1)S(1)} %get-tuple-element.46), channel_id=1, source_target_pairs={{0,96},{32,0},{64,32},{96,64},{1,97},{33,1},{65,33},{97,65},{2,98}... | collective-permute-start | bytes 786440 | tf_op jit(solution)/shard_map/ppermute | solution.py:21
  27.5 3.0 %collective-permute-start.13 = (bf16[4,128,256]{2,1,0:T(8,128)(2,1)S(1)}, bf16[4,128,256]{2,1,0:T(8,128)(2,1)}, u32[]{:S(2)}, u32[]{:S(2)}) collective-permute-start(bf16[4,128,256]{2,1,0:T(8,128)(2,1)S(1)} %get-tuple-element.45), channel_id=1, source_target_pairs={{0,128},{128,0},{1,129},{129,1},{2,130},{130,2},{3,131},{131,3},{4... | collective-permute-start | bytes 786440 | tf_op jit(solution)/shard_map/ppermute | solution.py:21
  30.5 2.0 %collective-permute-start.11 = (bf16[4,128,256]{2,1,0:T(8,128)(2,1)S(1)}, bf16[4,128,256]{2,1,0:T(8,128)(2,1)S(1)}, u32[]{:S(2)}, u32[]{:S(2)}) collective-permute-start(bf16[4,128,256]{2,1,0:T(8,128)(2,1)S(1)} %slice.40), channel_id=1, source_target_pairs={{0,128},{128,0},{1,129},{129,1},{2,130},{130,2},{3,131},{131,3},{4... | collective-permute-start | bytes 786440 | tf_op jit(solution)/shard_map/ppermute | solution.py:21
  32.6 2.2 %collective-permute-done.7.rest_8_ = bf16[4,128,256]{2,1,0:T(8,128)(2,1)S(1)} collective-permute-done((bf16[4,128,256]{2,1,0:T(8,128)(2,1)S(1)}, bf16[4,128,256]{2,1,0:T(8,128)(2,1)S(1)}, u32[]{:S(2)}, u32[]{:S(2)}) %collective-permute-start.7) | collective-permute-done | bytes 262176 | tf_op jit(solution)/shard_map/ppermute | solution.py:21
  34.8 1.7 collective-permute-start.23
  36.5 1.9 %collective-permute-done.21.rest_22_ = bf16[2,128,256]{2,1,0:T(8,128)(2,1)S(1)} collective-permute-done((bf16[2,128,256]{2,1,0:T(8,128)(2,1)S(1)}, bf16[2,128,256]{2,1,0:T(8,128)(2,1)S(1)}, u32[]{:S(2)}, u32[]{:S(2)}) %collective-permute-start.21) | collective-permute-done | bytes 131104 | tf_op jit(solution)/shard_map/ppermute | solution.py:21
  38.5 4.9 %collective-permute-start.22 = (bf16[2,128,256]{2,1,0:T(8,128)(2,1)S(1)}, bf16[2,128,256]{2,1,0:T(8,128)(2,1)S(1)}, u32[]{:S(2)}, u32[]{:S(2)}) collective-permute-start(bf16[2,128,256]{2,1,0:T(8,128)(2,1)S(1)} %collective-permute-done.21.rest_22_), channel_id=1, source_target_pairs={{0,16},{16,0},{1,17},{17,1},{2,18},{18,2},{3,19},{19,3},{4,20},{20... | collective-permute-start | bytes 393224 | tf_op jit(solution)/shard_map/ppermute | solution.py:21
  44.7 1.2 collective-permute-done.24.rest_25_
  46.3 6.4 %collective-permute-done.15.rest_16_ = bf16[4,128,256]{2,1,0:T(8,128)(2,1)S(1)} collective-permute-done((bf16[4,128,256]{2,1,0:T(8,128)(2,1)S(1)}, bf16[4,128,256]{2,1,0:T(8,128)(2,1)S(1)}, u32[]{:S(2)}, u32[]{:S(2)}) %collective-permute-start.15) | collective-permute-done | bytes 262176 | tf_op jit(solution)/shard_map/ppermute | solution.py:21
  52.7 0.9 collective-permute-start.14
  54.3 0.7 reduce
  55.0 0.8 collective-permute-start.2
  56.3 0.7 reduce.1
  57.9 0.8 select_reduce_fusion.packed_ref
  60.3 13.6 %tile_product.1 = (bf16[64,128,256]{2,1,0:T(8,128)(2,1)}, bf16[2,128,256]{2,1,0:T(8,128)(2,1)}, bf16[4,128,256]{2,1,0:T(8,128)(2,1)}, bf16[4,128,256]{2,1,0:T(8,...) custom-call(s32[1]{0:T(128)} %bitcast.30.count_ref, ...), custom_call_target="tpu_custom_call" | custom-call | flops 3221225472 | bytes 31457280 | tf_op jit(solution)/shard_map/tile_product/pallas_call | solution.py:146
  74.1 2.6 %collective-permute-start.35 = (bf16[2,128,256]{2,1,0:T(8,128)(2,1)}, bf16[2,128,256]{2,1,0:T(8,128)(2,1)S(1)}, u32[]{:S(2)}, u32[]{:S(2)}) collective-permute-start(bf16[2,128,256]{2,1,0:T(8,128)(2,1)} %get-tuple-element.38), channel_id=1, source_target_pairs={{0,16},{16,0},{1,17},{17,1},{2,18},{18,2},{3,19},{19,3},{4,20},{20... | collective-permute-start | bytes 393224 | tf_op jit(solution)/shard_map/ppermute | solution.py:206
  76.7 1.4 collective-permute-start.31
  78.0 0.8 collective-permute-start.32
  78.8 4.0 %collective-permute-start.33 = (bf16[4,128,256]{2,1,0:T(8,128)(2,1)}, bf16[4,128,256]{2,1,0:T(8,128)(2,1)S(1)}, u32[]{:S(2)}, u32[]{:S(2)}) collective-permute-start(bf16[4,128,256]{2,1,0:T(8,128)(2,1)} %get-tuple-element.35), channel_id=1, source_target_pairs={{0,17},{1,16},{16,1},{17,0},{2,19},{3,18},{18,3},{19,2},{4,21},{5,... | collective-permute-start | bytes 786440 | tf_op jit(solution)/shard_map/ppermute | solution.py:206
  82.9 0.9 add_bitcast_fusion.7
  84.3 3.4 %collective-permute-done.31 = bf16[4,128,256]{2,1,0:T(8,128)(2,1)S(1)} collective-permute-done((bf16[4,128,256]{2,1,0:T(8,128)(2,1)}, bf16[4,128,256]{2,1,0:T(8,128)(2,1)S(1)}, u32[]{:S(2)}, u32[]{:S(2)}) %collective-permute-start.31) | collective-permute-done | bytes 262176 | tf_op jit(solution)/shard_map/ppermute | solution.py:206
  87.8 3.5 %collective-permute-start.30 = (bf16[4,128,256]{2,1,0:T(8,128)(2,1)}, bf16[4,128,256]{2,1,0:T(8,128)(2,1)S(1)}, u32[]{:S(2)}, u32[]{:S(2)}) collective-permute-start(bf16[4,128,256]{2,1,0:T(8,128)(2,1)} %get-tuple-element.31), channel_id=1, source_target_pairs={{0,17},{1,16},{16,1},{17,0},{2,19},{3,18},{18,3},{19,2},{4,21},{5,... | collective-permute-start | bytes 786440 | tf_op jit(solution)/shard_map/ppermute | solution.py:206
  91.3 1.0 add_bitcast_fusion.1
  92.4 1.9 %collective-permute-done.33 = bf16[4,128,256]{2,1,0:T(8,128)(2,1)S(1)} collective-permute-done((bf16[4,128,256]{2,1,0:T(8,128)(2,1)}, bf16[4,128,256]{2,1,0:T(8,128)(2,1)S(1)}, u32[]{:S(2)}, u32[]{:S(2)}) %collective-permute-start.33) | collective-permute-done | bytes 262176 | tf_op jit(solution)/shard_map/ppermute | solution.py:206
  94.3 8.1 %collective-permute-start.37 = (bf16[2,2,128,256]{3,2,1,0:T(8,128)(2,1)S(1)}, bf16[2,2,128,256]{3,2,1,0:T(8,128)(2,1)S(1)}, u32[]{:S(2)}, u32[]{:S(2)}) collective-permute-start(bf16[2,2,128,256]{3,2,1,0:T(8,128)(2,1)S(1)} %pad_maximum_fusion.4), channel_id=1, source_target_pairs={{0,2},{2,4},{4,6},{6,8},{8,10},{10,12},{12,14},{14,0},{16,30},{18,... | collective-permute-start | bytes 786440 | tf_op jit(solution)/shard_map/ppermute | solution.py:243
  102.5 8.9 %collective-permute-done.37 = bf16[2,2,128,256]{3,2,1,0:T(8,128)(2,1)S(1)} collective-permute-done((bf16[2,2,128,256]{3,2,1,0:T(8,128)(2,1)S(1)}, bf16[2,2,128,256]{3,2,1,0:T(8,128)(2,1)S(1)}, u32[]{:S(2)}, u32[]{:S(2)}) %collective-permute-start.37) | collective-permute-done | bytes 262176 | tf_op jit(solution)/shard_map/ppermute | solution.py:243
  111.4 2.9 %collective-permute-start.26 = (bf16[4,128,256]{2,1,0:T(8,128)(2,1)}, bf16[4,128,256]{2,1,0:T(8,128)(2,1)S(1)}, u32[]{:S(2)}, u32[]{:S(2)}) collective-permute-start(bf16[4,128,256]{2,1,0:T(8,128)(2,1)} %get-tuple-element.26), channel_id=1, source_target_pairs={{0,16},{16,0},{1,17},{17,1},{2,18},{18,2},{3,19},{19,3},{4,20},{20... | collective-permute-start | bytes 786440 | tf_op jit(solution)/shard_map/ppermute | solution.py:206
  114.4 1.8 %collective-permute-start.38 = (bf16[2,4,128,256]{3,2,1,0:T(8,128)(2,1)S(1)}, bf16[2,4,128,256]{3,2,1,0:T(8,128)(2,1)S(1)}, u32[]{:S(2)}, u32[]{:S(2)}) collective-permute-start(bf16[2,4,128,256]{3,2,1,0:T(8,128)(2,1)S(1)} %select_add_fusion), channel_id=1, source_target_pairs={{0,2},{2,4},{4,6},{6,8},{8,10},{10,12},{12,14},{14,0},{16,30},{18,... | collective-permute-start | bytes 1572872 | tf_op jit(solution)/shard_map/ppermute | solution.py:243
  116.2 1.0 add_bitcast_fusion.3
  117.4 16.8 %collective-permute-done.38 = bf16[2,4,128,256]{3,2,1,0:T(8,128)(2,1)S(1)} collective-permute-done((bf16[2,4,128,256]{3,2,1,0:T(8,128)(2,1)S(1)}, bf16[2,4,128,256]{3,2,1,0:T(8,128)(2,1)S(1)}, u32[]{:S(2)}, u32[]{:S(2)}) %collective-permute-start.38) | collective-permute-done | bytes 524320 | tf_op jit(solution)/shard_map/ppermute | solution.py:243
  134.4 2.9 %collective-permute-start.39 = (bf16[2,4,128,256]{3,2,1,0:T(8,128)(2,1)S(1)}, bf16[2,4,128,256]{3,2,1,0:T(8,128)(2,1)S(1)}, u32[]{:S(2)}, u32[]{:S(2)}) collective-permute-start(bf16[2,4,128,256]{3,2,1,0:T(8,128)(2,1)S(1)} %add.319), channel_id=1, source_target_pairs={{0,2},{2,4},{4,6},{6,8},{8,10},{10,12},{12,14},{14,0},{16,30},{18,... | collective-permute-start | bytes 1572872 | tf_op jit(solution)/shard_map/ppermute | solution.py:243
  137.4 6.9 %collective-permute-done.39 = bf16[2,4,128,256]{3,2,1,0:T(8,128)(2,1)S(1)} collective-permute-done((bf16[2,4,128,256]{3,2,1,0:T(8,128)(2,1)S(1)}, bf16[2,4,128,256]{3,2,1,0:T(8,128)(2,1)S(1)}, u32[]{:S(2)}, u32[]{:S(2)}) %collective-permute-start.39) | collective-permute-done | bytes 524320 | tf_op jit(solution)/shard_map/ppermute | solution.py:243
  144.4 2.3 %collective-permute-start.40 = (bf16[2,4,128,256]{3,2,1,0:T(8,128)(2,1)S(1)}, bf16[2,4,128,256]{3,2,1,0:T(8,128)(2,1)S(1)}, u32[]{:S(2)}, u32[]{:S(2)}) collective-permute-start(bf16[2,4,128,256]{3,2,1,0:T(8,128)(2,1)S(1)} %add.320), channel_id=1, source_target_pairs={{0,2},{2,4},{4,6},{6,8},{8,10},{10,12},{12,14},{14,0},{16,30},{18,... | collective-permute-start | bytes 1572872 | tf_op jit(solution)/shard_map/ppermute | solution.py:243
  146.7 0.8 collective-permute-start.42
  147.5 5.3 %collective-permute-done.40 = bf16[2,4,128,256]{3,2,1,0:T(8,128)(2,1)S(1)} collective-permute-done((bf16[2,4,128,256]{3,2,1,0:T(8,128)(2,1)S(1)}, bf16[2,4,128,256]{3,2,1,0:T(8,128)(2,1)S(1)}, u32[]{:S(2)}, u32[]{:S(2)}) %collective-permute-start.40) | collective-permute-done | bytes 524320 | tf_op jit(solution)/shard_map/ppermute | solution.py:243
  152.9 4.6 %collective-permute-start.41 = (bf16[4,128,256]{2,1,0:T(8,128)(2,1)S(1)}, bf16[4,128,256]{2,1,0:T(8,128)(2,1)S(1)}, u32[]{:S(2)}, u32[]{:S(2)}) collective-permute-start(bf16[4,128,256]{2,1,0:T(8,128)(2,1)S(1)} %slice_bitcast_fusion), channel_id=1, source_target_pairs={{0,16},{16,0},{1,17},{17,1},{2,18},{18,2},{3,19},{19,3},{4,20},{20... | collective-permute-start | bytes 786440 | tf_op jit(solution)/shard_map/ppermute | solution.py:206
  157.5 1.0 slice.49
  158.5 0.9 collective-permute-start.43
  159.5 6.9 %collective-permute-done.43 = bf16[4,128,256]{2,1,0:T(8,128)(2,1)S(1)} collective-permute-done((bf16[4,128,256]{2,1,0:T(8,128)(2,1)S(1)}, bf16[4,128,256]{2,1,0:T(8,128)(2,1)S(1)}, u32[]{:S(2)}, u32[]{:S(2)}) %collective-permute-start.43) | collective-permute-done | bytes 262176 | tf_op jit(solution)/shard_map/ppermute | solution.py:206
  166.4 1.0 slice_add_fusion
  167.4 0.8 pad_maximum_fusion.3
  (113 shorter events, 6.5 us)
Async XLA Ops:
  6.5 151.0 %reduce-scatter.2.cloned.1.call-start = ((), (), s32[]{:S(2)}) async-start(), calls=%async_computation.1 | async-start | bytes 4718592 | tf_op jit(solution)/shard_map/reduce_scatter | solution.py:230
  6.5 14.7 %collective-permute-start.1 = (bf16[8,128,256]{2,1,0:T(8,128)(2,1)}, bf16[8,128,256]{2,1,0:T(8,128)(2,1)S(1)}, u32[]{:S(2)}, u32[]{:S(2)}) collective-permute-start(bf16[8,128,256]{2,1,0:T(8,128)(2,1)} %bitcast.34), channel_id=1, source_target_pairs={{0,128},{128,0},{1,129},{129,1},{2,130},{130,2},{3,131},{131,3},{4... | collective-permute-start | bytes 1572872 | tf_op jit(solution)/shard_map/ppermute | solution.py:21
  10.3 14.3 %collective-permute-start.3 = (bf16[8,128,256]{2,1,0:T(8,128)(2,1)}, bf16[8,128,256]{2,1,0:T(8,128)(2,1)S(1)}, u32[]{:S(2)}, u32[]{:S(2)}) collective-permute-start(bf16[8,128,256]{2,1,0:T(8,128)(2,1)} %bitcast.35), channel_id=1, source_target_pairs={{0,32},{32,64},{64,96},{96,0},{1,33},{33,65},{65,97},{97,1},{2,34}... | collective-permute-start | bytes 1572872 | tf_op jit(solution)/shard_map/ppermute | solution.py:21
  11.5 13.3 %collective-permute-start.5 = (bf16[8,128,256]{2,1,0:T(8,128)(2,1)}, bf16[8,128,256]{2,1,0:T(8,128)(2,1)S(1)}, u32[]{:S(2)}, u32[]{:S(2)}) collective-permute-start(bf16[8,128,256]{2,1,0:T(8,128)(2,1)} %bitcast.36), channel_id=1, source_target_pairs={{0,96},{32,0},{64,32},{96,64},{1,97},{33,1},{65,33},{97,65},{2,98}... | collective-permute-start | bytes 1572872 | tf_op jit(solution)/shard_map/ppermute | solution.py:21
  12.9 14.5 %collective-permute-start = (bf16[8,128,256]{2,1,0:T(8,128)(2,1)}, bf16[8,128,256]{2,1,0:T(8,128)(2,1)S(1)}, u32[]{:S(2)}, u32[]{:S(2)}) collective-permute-start(bf16[8,128,256]{2,1,0:T(8,128)(2,1)} %bitcast.37), channel_id=1, source_target_pairs={{0,16},{16,0},{1,17},{17,1},{2,18},{18,2},{3,19},{19,3},{4,20},{20... | collective-permute-start | bytes 1572872 | tf_op jit(solution)/shard_map/ppermute | solution.py:21
  21.2 9.3 %collective-permute-start.17 = (bf16[4,128,256]{2,1,0:T(8,128)(2,1)S(1)}, bf16[4,128,256]{2,1,0:T(8,128)(2,1)S(1)}, u32[]{:S(2)}, u32[]{:S(2)}) collective-permute-start(bf16[4,128,256]{2,1,0:T(8,128)(2,1)S(1)} %slice.43), channel_id=1, source_target_pairs={{0,32},{32,64},{64,96},{96,0},{1,33},{33,65},{65,97},{97,1},{2,34}... | collective-permute-start | bytes 786440 | tf_op jit(solution)/shard_map/ppermute | solution.py:21
  23.2 9.3 %collective-permute-start.19 = (bf16[4,128,256]{2,1,0:T(8,128)(2,1)S(1)}, bf16[4,128,256]{2,1,0:T(8,128)(2,1)S(1)}, u32[]{:S(2)}, u32[]{:S(2)}) collective-permute-start(bf16[4,128,256]{2,1,0:T(8,128)(2,1)S(1)} %slice.43), channel_id=1, source_target_pairs={{0,96},{32,0},{64,32},{96,64},{1,97},{33,1},{65,33},{97,65},{2,98}... | collective-permute-start | bytes 786440 | tf_op jit(solution)/shard_map/ppermute | solution.py:21
  24.6 10.2 %collective-permute-start.7 = (bf16[4,128,256]{2,1,0:T(8,128)(2,1)S(1)}, bf16[4,128,256]{2,1,0:T(8,128)(2,1)S(1)}, u32[]{:S(2)}, u32[]{:S(2)}) collective-permute-start(bf16[4,128,256]{2,1,0:T(8,128)(2,1)S(1)} %slice.40), channel_id=1, source_target_pairs={{0,32},{32,64},{64,96},{96,0},{1,33},{33,65},{65,97},{97,1},{2,34}... | collective-permute-start | bytes 786440 | tf_op jit(solution)/shard_map/ppermute | solution.py:21
  24.8 18.6 %collective-permute-start.9 = (bf16[4,128,256]{2,1,0:T(8,128)(2,1)S(1)}, bf16[4,128,256]{2,1,0:T(8,128)(2,1)}, u32[]{:S(2)}, u32[]{:S(2)}) collective-permute-start(bf16[4,128,256]{2,1,0:T(8,128)(2,1)S(1)} %get-tuple-element.46), channel_id=1, source_target_pairs={{0,96},{32,0},{64,32},{96,64},{1,97},{33,1},{65,33},{97,65},{2,98}... | collective-permute-start | bytes 786440 | tf_op jit(solution)/shard_map/ppermute | solution.py:21
  27.5 16.0 %collective-permute-start.13 = (bf16[4,128,256]{2,1,0:T(8,128)(2,1)S(1)}, bf16[4,128,256]{2,1,0:T(8,128)(2,1)}, u32[]{:S(2)}, u32[]{:S(2)}) collective-permute-start(bf16[4,128,256]{2,1,0:T(8,128)(2,1)S(1)} %get-tuple-element.45), channel_id=1, source_target_pairs={{0,128},{128,0},{1,129},{129,1},{2,130},{130,2},{3,131},{131,3},{4... | collective-permute-start | bytes 786440 | tf_op jit(solution)/shard_map/ppermute | solution.py:21
  30.5 13.3 %collective-permute-start.11 = (bf16[4,128,256]{2,1,0:T(8,128)(2,1)S(1)}, bf16[4,128,256]{2,1,0:T(8,128)(2,1)S(1)}, u32[]{:S(2)}, u32[]{:S(2)}) collective-permute-start(bf16[4,128,256]{2,1,0:T(8,128)(2,1)S(1)} %slice.40), channel_id=1, source_target_pairs={{0,128},{128,0},{1,129},{129,1},{2,130},{130,2},{3,131},{131,3},{4... | collective-permute-start | bytes 786440 | tf_op jit(solution)/shard_map/ppermute | solution.py:21
  32.5 6.0 %collective-permute-start.21 = (bf16[2,128,256]{2,1,0:T(8,128)(2,1)S(1)}, bf16[2,128,256]{2,1,0:T(8,128)(2,1)S(1)}, u32[]{:S(2)}, u32[]{:S(2)}) collective-permute-start(bf16[2,128,256]{2,1,0:T(8,128)(2,1)S(1)} %slice.44), channel_id=1, source_target_pairs={{0,32},{32,64},{64,96},{96,0},{1,33},{33,65},{65,97},{97,1},{2,34}... | collective-permute-start | bytes 393224 | tf_op jit(solution)/shard_map/ppermute | solution.py:21
  34.8 9.2 %collective-permute-start.23 = (bf16[2,128,256]{2,1,0:T(8,128)(2,1)S(1)}, bf16[2,128,256]{2,1,0:T(8,128)(2,1)S(1)}, u32[]{:S(2)}, u32[]{:S(2)}) collective-permute-start(bf16[2,128,256]{2,1,0:T(8,128)(2,1)S(1)} %slice.45), channel_id=1, source_target_pairs={{0,96},{32,0},{64,32},{96,64},{1,97},{33,1},{65,33},{97,65},{2,98}... | collective-permute-start | bytes 393224 | tf_op jit(solution)/shard_map/ppermute | solution.py:21
  38.5 5.9 %collective-permute-start.22 = (bf16[2,128,256]{2,1,0:T(8,128)(2,1)S(1)}, bf16[2,128,256]{2,1,0:T(8,128)(2,1)S(1)}, u32[]{:S(2)}, u32[]{:S(2)}) collective-permute-start(bf16[2,128,256]{2,1,0:T(8,128)(2,1)S(1)} %collective-permute-done.21.rest_22_), channel_id=1, source_target_pairs={{0,16},{16,0},{1,17},{17,1},{2,18},{18,2},{3,19},{19,3},{4,20},{20... | collective-permute-start | bytes 393224 | tf_op jit(solution)/shard_map/ppermute | solution.py:21
  43.4 9.3 %collective-permute-start.15 = (bf16[4,128,256]{2,1,0:T(8,128)(2,1)S(1)}, bf16[4,128,256]{2,1,0:T(8,128)(2,1)S(1)}, u32[]{:S(2)}, u32[]{:S(2)}) collective-permute-start(bf16[4,128,256]{2,1,0:T(8,128)(2,1)S(1)} %collective-permute-done.7.rest_8_), channel_id=1, source_target_pairs={{0,128},{128,0},{1,129},{129,1},{2,130},{130,2},{3,131},{131,3},{4... | collective-permute-start | bytes 786440 | tf_op jit(solution)/shard_map/ppermute | solution.py:21
  43.4 11.6 %collective-permute-start.18 = (bf16[4,128,256]{2,1,0:T(8,128)(2,1)S(1)}, bf16[4,128,256]{2,1,0:T(8,128)(2,1)}, u32[]{:S(2)}, u32[]{:S(2)}) collective-permute-start(bf16[4,128,256]{2,1,0:T(8,128)(2,1)S(1)} %collective-permute-done.17.rest_18_), channel_id=1, source_target_pairs={{0,16},{16,0},{1,17},{17,1},{2,18},{18,2},{3,19},{19,3},{4,20},{20... | collective-permute-start | bytes 786440 | tf_op jit(solution)/shard_map/ppermute | solution.py:21
  43.8 12.0 %collective-permute-start.20 = (bf16[4,128,256]{2,1,0:T(8,128)(2,1)S(1)}, bf16[4,128,256]{2,1,0:T(8,128)(2,1)}, u32[]{:S(2)}, u32[]{:S(2)}) collective-permute-start(bf16[4,128,256]{2,1,0:T(8,128)(2,1)S(1)} %collective-permute-done.19.rest_20_), channel_id=1, source_target_pairs={{0,16},{16,0},{1,17},{17,1},{2,18},{18,2},{3,19},{19,3},{4,20},{20... | collective-permute-start | bytes 786440 | tf_op jit(solution)/shard_map/ppermute | solution.py:21
  44.0 11.9 %collective-permute-start.8 = (bf16[4,128,256]{2,1,0:T(8,128)(2,1)S(1)}, bf16[4,128,256]{2,1,0:T(8,128)(2,1)}, u32[]{:S(2)}, u32[]{:S(2)}) collective-permute-start(bf16[4,128,256]{2,1,0:T(8,128)(2,1)S(1)} %collective-permute-done.7.rest_8_), channel_id=1, source_target_pairs={{0,16},{16,0},{1,17},{17,1},{2,18},{18,2},{3,19},{19,3},{4,20},{20... | collective-permute-start | bytes 786440 | tf_op jit(solution)/shard_map/ppermute | solution.py:21
  44.4 1.6 collective-permute-start.24
  46.0 11.1 %collective-permute-start.10 = (bf16[4,128,256]{2,1,0:T(8,128)(2,1)}, bf16[4,128,256]{2,1,0:T(8,128)(2,1)}, u32[]{:S(2)}, u32[]{:S(2)}) collective-permute-start(bf16[4,128,256]{2,1,0:T(8,128)(2,1)} %collective-permute-done.9.rest_10_), channel_id=1, source_target_pairs={{0,16},{16,0},{1,17},{17,1},{2,18},{18,2},{3,19},{19,3},{4,20},{20... | collective-permute-start | bytes 786440 | tf_op jit(solution)/shard_map/ppermute | solution.py:21
  52.7 4.6 %collective-permute-start.14 = (bf16[4,128,256]{2,1,0:T(8,128)(2,1)}, bf16[4,128,256]{2,1,0:T(8,128)(2,1)}, u32[]{:S(2)}, u32[]{:S(2)}) collective-permute-start(bf16[4,128,256]{2,1,0:T(8,128)(2,1)} %collective-permute-done.13.rest_14_), channel_id=1, source_target_pairs={{0,16},{16,0},{1,17},{17,1},{2,18},{18,2},{3,19},{19,3},{4,20},{20... | collective-permute-start | bytes 786440 | tf_op jit(solution)/shard_map/ppermute | solution.py:21
  55.0 4.2 %collective-permute-start.2 = (bf16[8,128,256]{2,1,0:T(8,128)(2,1)S(1)}, bf16[8,128,256]{2,1,0:T(8,128)(2,1)S(1)}, u32[]{:S(2)}, u32[]{:S(2)}) collective-permute-start(bf16[8,128,256]{2,1,0:T(8,128)(2,1)S(1)} %collective-permute-done.1.rest_2_), channel_id=1, source_target_pairs={{0,16},{16,0},{1,17},{17,1},{2,18},{18,2},{3,19},{19,3},{4,20},{20... | collective-permute-start | bytes 1572872 | tf_op jit(solution)/shard_map/ppermute | solution.py:21
  55.8 3.4 %collective-permute-start.4 = (bf16[8,128,256]{2,1,0:T(8,128)(2,1)S(1)}, bf16[8,128,256]{2,1,0:T(8,128)(2,1)}, u32[]{:S(2)}, u32[]{:S(2)}) collective-permute-start(bf16[8,128,256]{2,1,0:T(8,128)(2,1)S(1)} %collective-permute-done.3.rest_4_), channel_id=1, source_target_pairs={{0,16},{16,0},{1,17},{17,1},{2,18},{18,2},{3,19},{19,3},{4,20},{20... | collective-permute-start | bytes 1572872 | tf_op jit(solution)/shard_map/ppermute | solution.py:21
  55.9 3.3 %collective-permute-start.6 = (bf16[8,128,256]{2,1,0:T(8,128)(2,1)S(1)}, bf16[8,128,256]{2,1,0:T(8,128)(2,1)}, u32[]{:S(2)}, u32[]{:S(2)}) collective-permute-start(bf16[8,128,256]{2,1,0:T(8,128)(2,1)S(1)} %collective-permute-done.5.rest_6_), channel_id=1, source_target_pairs={{0,16},{16,0},{1,17},{17,1},{2,18},{18,2},{3,19},{19,3},{4,20},{20... | collective-permute-start | bytes 1572872 | tf_op jit(solution)/shard_map/ppermute | solution.py:21
  57.0 2.1 %collective-permute-start.12 = (bf16[4,128,256]{2,1,0:T(8,128)(2,1)}, bf16[4,128,256]{2,1,0:T(8,128)(2,1)S(1)}, u32[]{:S(2)}, u32[]{:S(2)}) collective-permute-start(bf16[4,128,256]{2,1,0:T(8,128)(2,1)} %copy-done.8), channel_id=1, source_target_pairs={{0,16},{16,0},{1,17},{17,1},{2,18},{18,2},{3,19},{19,3},{4,20},{20... | collective-permute-start | bytes 786440 | tf_op jit(solution)/shard_map/ppermute | solution.py:21
  57.2 2.3 %collective-permute-start.16 = (bf16[4,128,256]{2,1,0:T(8,128)(2,1)}, bf16[4,128,256]{2,1,0:T(8,128)(2,1)S(1)}, u32[]{:S(2)}, u32[]{:S(2)}) collective-permute-start(bf16[4,128,256]{2,1,0:T(8,128)(2,1)} %copy-done.9), channel_id=1, source_target_pairs={{0,16},{16,0},{1,17},{17,1},{2,18},{18,2},{3,19},{19,3},{4,20},{20... | collective-permute-start | bytes 786440 | tf_op jit(solution)/shard_map/ppermute | solution.py:21
  73.9 63.4 %copy-start.13 = (bf16[4,128,256]{2,1,0:T(8,128)(2,1)S(1)}, bf16[4,128,256]{2,1,0:T(8,128)(2,1)}, u32[]{:S(2)}) copy-start(bf16[4,128,256]{2,1,0:T(8,128)(2,1)} %get-tuple-element.24) | copy-start | bytes 786436
  73.9 72.8 %copy-start.18 = (bf16[4,128,256]{2,1,0:T(8,128)(2,1)S(1)}, bf16[4,128,256]{2,1,0:T(8,128)(2,1)}, u32[]{:S(2)}) copy-start(bf16[4,128,256]{2,1,0:T(8,128)(2,1)} %get-tuple-element.41) | copy-start | bytes 786436
  73.9 85.5 %copy-start.12 = (bf16[4,128,256]{2,1,0:T(8,128)(2,1)S(1)}, bf16[4,128,256]{2,1,0:T(8,128)(2,1)}, u32[]{:S(2)}) copy-start(bf16[4,128,256]{2,1,0:T(8,128)(2,1)} %get-tuple-element.40) | copy-start | bytes 786436
  73.9 4.9 %collective-permute-start.34 = (bf16[2,128,256]{2,1,0:T(8,128)(2,1)}, bf16[2,128,256]{2,1,0:T(8,128)(2,1)S(1)}, u32[]{:S(2)}, u32[]{:S(2)}) collective-permute-start(bf16[2,128,256]{2,1,0:T(8,128)(2,1)} %get-tuple-element.37), channel_id=1, source_target_pairs={{0,1},{1,0},{2,3},{3,2},{4,5},{5,4},{6,7},{7,6},{8,9},{9,8},{10,11... | collective-permute-start | bytes 393224 | tf_op jit(solution)/shard_map/ppermute | solution.py:206
  74.1 9.7 %collective-permute-start.35 = (bf16[2,128,256]{2,1,0:T(8,128)(2,1)}, bf16[2,128,256]{2,1,0:T(8,128)(2,1)S(1)}, u32[]{:S(2)}, u32[]{:S(2)}) collective-permute-start(bf16[2,128,256]{2,1,0:T(8,128)(2,1)} %get-tuple-element.38), channel_id=1, source_target_pairs={{0,16},{16,0},{1,17},{17,1},{2,18},{18,2},{3,19},{19,3},{4,20},{20... | collective-permute-start | bytes 393224 | tf_op jit(solution)/shard_map/ppermute | solution.py:206
  76.7 7.2 %collective-permute-start.36 = (bf16[2,128,256]{2,1,0:T(8,128)(2,1)}, bf16[2,128,256]{2,1,0:T(8,128)(2,1)S(1)}, u32[]{:S(2)}, u32[]{:S(2)}) collective-permute-start(bf16[2,128,256]{2,1,0:T(8,128)(2,1)} %get-tuple-element.39), channel_id=1, source_target_pairs={{0,17},{1,16},{16,1},{17,0},{2,19},{3,18},{18,3},{19,2},{4,21},{5,... | collective-permute-start | bytes 393224 | tf_op jit(solution)/shard_map/ppermute | solution.py:206
  76.7 11.1 %collective-permute-start.31 = (bf16[4,128,256]{2,1,0:T(8,128)(2,1)}, bf16[4,128,256]{2,1,0:T(8,128)(2,1)S(1)}, u32[]{:S(2)}, u32[]{:S(2)}) collective-permute-start(bf16[4,128,256]{2,1,0:T(8,128)(2,1)} %get-tuple-element.33), channel_id=1, source_target_pairs={{0,1},{1,0},{2,3},{3,2},{4,5},{5,4},{6,7},{7,6},{8,9},{9,8},{10,11... | collective-permute-start | bytes 786440 | tf_op jit(solution)/shard_map/ppermute | solution.py:206
  78.0 14.3 %collective-permute-start.32 = (bf16[4,128,256]{2,1,0:T(8,128)(2,1)}, bf16[4,128,256]{2,1,0:T(8,128)(2,1)S(1)}, u32[]{:S(2)}, u32[]{:S(2)}) collective-permute-start(bf16[4,128,256]{2,1,0:T(8,128)(2,1)} %get-tuple-element.34), channel_id=1, source_target_pairs={{0,16},{16,0},{1,17},{17,1},{2,18},{18,2},{3,19},{19,3},{4,20},{20... | collective-permute-start | bytes 786440 | tf_op jit(solution)/shard_map/ppermute | solution.py:206
  78.8 15.5 %collective-permute-start.33 = (bf16[4,128,256]{2,1,0:T(8,128)(2,1)}, bf16[4,128,256]{2,1,0:T(8,128)(2,1)S(1)}, u32[]{:S(2)}, u32[]{:S(2)}) collective-permute-start(bf16[4,128,256]{2,1,0:T(8,128)(2,1)} %get-tuple-element.35), channel_id=1, source_target_pairs={{0,17},{1,16},{16,1},{17,0},{2,19},{3,18},{18,3},{19,2},{4,21},{5,... | collective-permute-start | bytes 786440 | tf_op jit(solution)/shard_map/ppermute | solution.py:206
  83.8 30.6 %collective-permute-start.28 = (bf16[4,128,256]{2,1,0:T(8,128)(2,1)}, bf16[4,128,256]{2,1,0:T(8,128)(2,1)S(1)}, u32[]{:S(2)}, u32[]{:S(2)}) collective-permute-start(bf16[4,128,256]{2,1,0:T(8,128)(2,1)} %get-tuple-element.29), channel_id=1, source_target_pairs={{0,1},{1,0},{2,3},{3,2},{4,5},{5,4},{6,7},{7,6},{8,9},{9,8},{10,11... | collective-permute-start | bytes 786440 | tf_op jit(solution)/shard_map/ppermute | solution.py:206
  83.9 33.3 %collective-permute-start.29 = (bf16[4,128,256]{2,1,0:T(8,128)(2,1)}, bf16[4,128,256]{2,1,0:T(8,128)(2,1)S(1)}, u32[]{:S(2)}, u32[]{:S(2)}) collective-permute-start(bf16[4,128,256]{2,1,0:T(8,128)(2,1)} %get-tuple-element.30), channel_id=1, source_target_pairs={{0,16},{16,0},{1,17},{17,1},{2,18},{18,2},{3,19},{19,3},{4,20},{20... | collective-permute-start | bytes 786440 | tf_op jit(solution)/shard_map/ppermute | solution.py:206
  87.8 29.5 %collective-permute-start.30 = (bf16[4,128,256]{2,1,0:T(8,128)(2,1)}, bf16[4,128,256]{2,1,0:T(8,128)(2,1)S(1)}, u32[]{:S(2)}, u32[]{:S(2)}) collective-permute-start(bf16[4,128,256]{2,1,0:T(8,128)(2,1)} %get-tuple-element.31), channel_id=1, source_target_pairs={{0,17},{1,16},{16,1},{17,0},{2,19},{3,18},{18,3},{19,2},{4,21},{5,... | collective-permute-start | bytes 786440 | tf_op jit(solution)/shard_map/ppermute | solution.py:206
  92.3 45.0 %collective-permute-start.25 = (bf16[4,128,256]{2,1,0:T(8,128)(2,1)}, bf16[4,128,256]{2,1,0:T(8,128)(2,1)S(1)}, u32[]{:S(2)}, u32[]{:S(2)}) collective-permute-start(bf16[4,128,256]{2,1,0:T(8,128)(2,1)} %get-tuple-element.25), channel_id=1, source_target_pairs={{0,1},{1,0},{2,3},{3,2},{4,5},{5,4},{6,7},{7,6},{8,9},{9,8},{10,11... | collective-permute-start | bytes 786440 | tf_op jit(solution)/shard_map/ppermute | solution.py:206
  94.3 17.1 %collective-permute-start.37 = (bf16[2,2,128,256]{3,2,1,0:T(8,128)(2,1)S(1)}, bf16[2,2,128,256]{3,2,1,0:T(8,128)(2,1)S(1)}, u32[]{:S(2)}, u32[]{:S(2)}) collective-permute-start(bf16[2,2,128,256]{3,2,1,0:T(8,128)(2,1)S(1)} %pad_maximum_fusion.4), channel_id=1, source_target_pairs={{0,2},{2,4},{4,6},{6,8},{8,10},{10,12},{12,14},{14,0},{16,30},{18,... | collective-permute-start | bytes 786440 | tf_op jit(solution)/shard_map/ppermute | solution.py:243
  111.4 25.9 %collective-permute-start.26 = (bf16[4,128,256]{2,1,0:T(8,128)(2,1)}, bf16[4,128,256]{2,1,0:T(8,128)(2,1)S(1)}, u32[]{:S(2)}, u32[]{:S(2)}) collective-permute-start(bf16[4,128,256]{2,1,0:T(8,128)(2,1)} %get-tuple-element.26), channel_id=1, source_target_pairs={{0,16},{16,0},{1,17},{17,1},{2,18},{18,2},{3,19},{19,3},{4,20},{20... | collective-permute-start | bytes 786440 | tf_op jit(solution)/shard_map/ppermute | solution.py:206
  114.4 19.9 %collective-permute-start.38 = (bf16[2,4,128,256]{3,2,1,0:T(8,128)(2,1)S(1)}, bf16[2,4,128,256]{3,2,1,0:T(8,128)(2,1)S(1)}, u32[]{:S(2)}, u32[]{:S(2)}) collective-permute-start(bf16[2,4,128,256]{3,2,1,0:T(8,128)(2,1)S(1)} %select_add_fusion), channel_id=1, source_target_pairs={{0,2},{2,4},{4,6},{6,8},{8,10},{10,12},{12,14},{14,0},{16,30},{18,... | collective-permute-start | bytes 1572872 | tf_op jit(solution)/shard_map/ppermute | solution.py:243
  117.2 20.1 %collective-permute-start.27 = (bf16[4,128,256]{2,1,0:T(8,128)(2,1)}, bf16[4,128,256]{2,1,0:T(8,128)(2,1)S(1)}, u32[]{:S(2)}, u32[]{:S(2)}) collective-permute-start(bf16[4,128,256]{2,1,0:T(8,128)(2,1)} %get-tuple-element.27), channel_id=1, source_target_pairs={{0,17},{1,16},{16,1},{17,0},{2,19},{3,18},{18,3},{19,2},{4,21},{5,... | collective-permute-start | bytes 786440 | tf_op jit(solution)/shard_map/ppermute | solution.py:206
  134.4 9.9 %collective-permute-start.39 = (bf16[2,4,128,256]{3,2,1,0:T(8,128)(2,1)S(1)}, bf16[2,4,128,256]{3,2,1,0:T(8,128)(2,1)S(1)}, u32[]{:S(2)}, u32[]{:S(2)}) collective-permute-start(bf16[2,4,128,256]{3,2,1,0:T(8,128)(2,1)S(1)} %add.319), channel_id=1, source_target_pairs={{0,2},{2,4},{4,6},{6,8},{8,10},{10,12},{12,14},{14,0},{16,30},{18,... | collective-permute-start | bytes 1572872 | tf_op jit(solution)/shard_map/ppermute | solution.py:243
  144.4 8.4 %collective-permute-start.40 = (bf16[2,4,128,256]{3,2,1,0:T(8,128)(2,1)S(1)}, bf16[2,4,128,256]{3,2,1,0:T(8,128)(2,1)S(1)}, u32[]{:S(2)}, u32[]{:S(2)}) collective-permute-start(bf16[2,4,128,256]{3,2,1,0:T(8,128)(2,1)S(1)} %add.320), channel_id=1, source_target_pairs={{0,2},{2,4},{4,6},{6,8},{8,10},{10,12},{12,14},{14,0},{16,30},{18,... | collective-permute-start | bytes 1572872 | tf_op jit(solution)/shard_map/ppermute | solution.py:243
  146.7 12.7 %collective-permute-start.42 = (bf16[4,128,256]{2,1,0:T(8,128)(2,1)S(1)}, bf16[4,128,256]{2,1,0:T(8,128)(2,1)S(1)}, u32[]{:S(2)}, u32[]{:S(2)}) collective-permute-start(bf16[4,128,256]{2,1,0:T(8,128)(2,1)S(1)} %copy-done.18), channel_id=1, source_target_pairs={{0,1},{1,0},{2,3},{3,2},{4,5},{5,4},{6,7},{7,6},{8,9},{9,8},{10,11... | collective-permute-start | bytes 786440 | tf_op jit(solution)/shard_map/ppermute | solution.py:206
  152.9 6.6 %collective-permute-start.41 = (bf16[4,128,256]{2,1,0:T(8,128)(2,1)S(1)}, bf16[4,128,256]{2,1,0:T(8,128)(2,1)S(1)}, u32[]{:S(2)}, u32[]{:S(2)}) collective-permute-start(bf16[4,128,256]{2,1,0:T(8,128)(2,1)S(1)} %slice_bitcast_fusion), channel_id=1, source_target_pairs={{0,16},{16,0},{1,17},{17,1},{2,18},{18,2},{3,19},{19,3},{4,20},{20... | collective-permute-start | bytes 786440 | tf_op jit(solution)/shard_map/ppermute | solution.py:206
  158.5 7.9 %collective-permute-start.43 = (bf16[4,128,256]{2,1,0:T(8,128)(2,1)S(1)}, bf16[4,128,256]{2,1,0:T(8,128)(2,1)S(1)}, u32[]{:S(2)}, u32[]{:S(2)}) collective-permute-start(bf16[4,128,256]{2,1,0:T(8,128)(2,1)S(1)} %slice.49), channel_id=1, source_target_pairs={{0,1},{1,0},{2,3},{3,2},{4,5},{5,4},{6,7},{7,6},{8,9},{9,8},{10,11... | collective-permute-start | bytes 786440 | tf_op jit(solution)/shard_map/ppermute | solution.py:206
  (16 other events, 282.5 us)
Sparse Core Ops, SparseCore 0:
  74.1 67.1 reduce-scatter.1

commit v3 on v1

--- a/solution.py
+++ b/solution.py
@@ -27,17 +27,18 @@
     late_rows, part_rows = 16 * LATE, 8
     late_parts, parts = late_rows // part_rows, n_rows // part_rows
     lates = []
-    for row in (8 * LATE, 0):
+    for row, unit in ((8 * LATE, LATE), (0, LATE), (late_rows, 2 * EARLY)):
         for other in range(2):
-            lates += [(row, other, hop, LATE if hop else LATE // 2) for hop in range(HOPS)]
-        lates.append((row, None, 0, LATE))
+            lates += [(row, unit, other, hop, unit if hop else unit // 2) for hop in range(HOPS)]
+        lates.append((row, unit, None, 0, unit))
+    n_late = 2 * (2 * HOPS + 1)
     shapes = [(n, bs, width) for *_, n in lates]
 
     def body(count_ref, core_ref, packed_ref, blocks_ref, *rest):
-        piece_refs, out_ref = rest[:n_pieces], rest[n_pieces]
-        late_refs = rest[n_pieces + 1 : n_pieces + 1 + len(lates)]
-        acc, panel, weights, staged, *rest = rest[n_pieces + 1 + len(lates) :]
-        late_staged, (piece_sem, weight_sem, out_sem, late_sem) = rest[: len(lates)], rest[len(lates) :]
+        piece_refs = rest[:n_pieces]
+        late_refs = rest[n_pieces : n_pieces + len(lates)]
+        acc, panel, weights, *rest = rest[n_pieces + len(lates) :]
+        late_staged, (piece_sem, weight_sem, late_sem) = rest[: len(lates)], rest[len(lates) :]
         groups = (count_ref[0] + GROUP - 1) // GROUP
 
         def weight_copies(group):
@@ -74,24 +75,20 @@
         for copy in piece_copies:
             copy.wait()
 
-        def out_copy(at, slot):
-            return pltpu.make_async_copy(
-                staged.at[slot], out_ref.at[pl.ds(at * part_rows, part_rows)], out_sem.at[slot]
-            )
-
         def late_copy(i):
             return pltpu.make_async_copy(late_staged[i], late_refs[i], late_sem.at[i])
 
-        def write_late():
-            for i, (row, other, hop, n) in enumerate(lates):
+        def write_some(chosen):
+            for i in chosen:
+                row, unit, other, hop, n = lates[i]
                 if other is None:
                     distance = skip = 0
                 else:
                     down = 1 - core_ref[0] if other else core_ref[0]
                     distance = 4 + hop * (2 * down - 1)
-                    skip = 0 if hop else (1 - down) * (LATE // 2)
-
-                def one_row(k, _, i=i, first=row + distance * LATE + skip):
+                    skip = 0 if hop else (1 - down) * (unit // 2)
+
+                def one_row(k, _, i=i, first=row + distance * unit + skip):
                     late_staged[i][k] = acc[first + k].astype(jnp.bfloat16)
                     return 0
 
@@ -101,20 +98,11 @@
         def write(part, _):
             @pl.when(part == late_parts - 1)
             def _():
-                write_late()
-
-            @pl.when(part >= late_parts)
+                write_some(range(n_late))
+
+            @pl.when(part == parts - 1)
             def _():
-                at = part - late_parts
-                slot = lax.rem(at, 2)
-
-                @pl.when(at >= 2)
-                def _():
-                    out_copy(at - 2, slot).wait()
-
-                for i in range(part_rows):
-                    staged[slot, i] = acc[part * part_rows + i].astype(jnp.bfloat16)
-                out_copy(at, slot).start()
+                write_some(range(n_late, len(lates)))
 
             return 0
 
@@ -134,29 +122,24 @@
 
         finished = lax.fori_loop(0, groups, one_group, 0)
         lax.fori_loop(finished, parts, write, 0)
-        for slot in range(2):
-            out_copy(0, slot).wait()
         for i in range(len(lates)):
             late_copy(i).wait()
 
     anywhere = pl.BlockSpec(memory_space=pl.ANY)
     hbm = pl.BlockSpec(memory_space=pltpu.MemorySpace.HBM)
     smem = pl.BlockSpec(memory_space=pltpu.SMEM)
-    early_shape = jax.ShapeDtypeStruct((16 * EARLY, bs, width), jnp.bfloat16)
     return pl.pallas_call(
         body,
-        out_shape=[early_shape] + [jax.ShapeDtypeStruct(shape, jnp.bfloat16) for shape in shapes],
+        out_shape=[jax.ShapeDtypeStruct(shape, jnp.bfloat16) for shape in shapes],
         in_specs=[smem, smem, smem, hbm] + [anywhere] * n_pieces,
-        out_specs=[hbm] + [anywhere] * len(lates),
+        out_specs=[anywhere] * len(lates),
         scratch_shapes=[
             pltpu.VMEM((n_rows + 1, bs, width), jnp.float32),
             pltpu.VMEM((n_cols, bs, width), jnp.bfloat16),
             pltpu.VMEM((BUFFERS, GROUP, bs, bs), jnp.bfloat16),
-            pltpu.VMEM((2, part_rows, bs, width), jnp.bfloat16),
             *[pltpu.VMEM(shape, jnp.bfloat16) for shape in shapes],
             pltpu.SemaphoreType.DMA((n_pieces,)),
             pltpu.SemaphoreType.DMA((BUFFERS, GROUP)),
-            pltpu.SemaphoreType.DMA((2,)),
             pltpu.SemaphoreType.DMA((len(lates),)),
         ],
         compiler_params=pltpu.CompilerParams(vmem_limit_bytes=59 * 2**20),
@@ -210,7 +193,7 @@
     live = jnp.arange(rows.shape[0], dtype=jnp.int32) < count[0]
     owner, within = rows // 8, rows % 8
     to_z, away = owner // 2, jnp.bitwise_xor(owner % 2, yl)
-    early_row = 16 * LATE + (to_z * 2 + away) * EARLY + within - LATE
+    early_row = 16 * LATE + ((to_z - z) % 8 * 2 + away) * EARLY + within - LATE
     late_row = (away * 8 + (to_z - z) % 8) * LATE + within
     rows = jnp.where(within < LATE, late_row, early_row)
     holder = cols // 8
@@ -219,12 +202,11 @@
     )
     packed = sort_slots(rows, distance * 8 + cols % 8, live, rows.shape[0] + 2 * GROUP)
     pieces, places = gather_panel(features.reshape(-1, bs, width))
-    early, *parts = tile_product(
+    parts = tile_product(
         blocks[0, 0], packed, count, c.reshape(1), pieces, places
     )
-    early = lax.psum_scatter(early, "z", scatter_dimension=0, tiled=True)
-
-    sent, kept = parts[: 2 * HOPS + 1], parts[2 * HOPS + 1 :]
+    n = 2 * HOPS + 1
+    sent, kept, early = parts[:n], parts[n : 2 * n], parts[2 * n :]
     joined = []
     for hop in range(HOPS):
         mine = flip(sent[hop], ("yl",))
@@ -232,21 +214,30 @@
         kept_theirs = flip(kept[HOPS + hop], ("c",))
         joined.append(lax.optimization_barrier(jnp.stack([kept[hop] + mine, kept_theirs + theirs])))
     near = flip(sent[2 * HOPS], ("yl",))
+    merged = []
+    for hop in range(HOPS):
+        theirs = flip(early[HOPS + hop], ("c",))
+        merged.append(lax.optimization_barrier(jnp.stack([early[hop], theirs])))
     around = [(i, (i + 1) % 8) for i in range(8)] + [(8 + i, 8 + (i - 1) % 8) for i in range(8)]
-    moving = joined[0]
+
+    def widened(array):
+        half = array.shape[1]
+        below = jnp.pad(array, ((0, 0), (half, 0), (0, 0), (0, 0)))
+        above = jnp.pad(array, ((0, 0), (0, half), (0, 0), (0, 0)))
+        return jnp.where(c == 0, below, above)
+
+    moving, large = joined[0], merged[0]
     for hop in range(HOPS):
+        large = lax.ppermute(large, ("c", "z"), around)
         moving = lax.ppermute(moving, ("c", "z"), around)
-        if hop == HOPS - 1:
-            break
-        if hop == 0:
-            below = jnp.pad(moving, ((0, 0), (LATE // 2, 0), (0, 0), (0, 0)))
-            above = jnp.pad(moving, ((0, 0), (0, LATE // 2), (0, 0), (0, 0)))
-            moving = jnp.where(c == 0, below, above)
-        moving = joined[hop + 1] + moving
+        if hop < HOPS - 1:
+            large = merged[hop + 1] + (large if hop else widened(large))
+            moving = joined[hop + 1] + (moving if hop else widened(moving))
+    large = large[0] + flip(large[1], ("c",)) + early[2 * HOPS]
+    last = flip(large[EARLY:], ("yl",))
     other_side = flip(moving[1], ("c",))
-    last = flip(early[EARLY:], ("yl",))
     late = moving[0] + other_side + (kept[2 * HOPS] + near)
-    return jnp.concatenate([late, early[:EARLY] + last], 0).reshape(-1, width)
+    return jnp.concatenate([late, large[:EARLY] + last], 0).reshape(-1, width)
 
 
 def solution(mesh):

time: 178 us -> 173 us (0.972)
  between operations: 14.4 us -> 1.14 us
  waiting for transfers between devices: 74.1 us -> 80.7 us
    ppermute x0 -> x4, starting transfers between devices: none -> 17.6 us  [on_device(): large = lax.ppermute(large, ('c', 'z'), around)]
    ppermute x4, starting transfers between devices: 14.6 us -> 2.08 us  [on_device(): moving = lax.ppermute(moving, ('c', 'z'), around)]
    ppermute x15 -> x20, waiting for transfers between devices: 11.7 us -> 22.8 us  [flip(): return lax.ppermute(array, axes, [(i, n - 1 - i) for i in range(n)])]
    ppermute x4, waiting for transfers between devices: 40.6 us -> 31.1 us  [on_device(): moving = lax.ppermute(moving, ('c', 'z'), around)]
    ppermute x0 -> x4, waiting for transfers between devices: none -> 4.88 us  [on_device(): large = lax.ppermute(large, ('c', 'z'), around)]
    ppermute x15 -> x20, starting transfers between devices: 23.2 us -> 19.6 us  [flip(): return lax.ppermute(array, axes, [(i, n - 1 - i) for i in range(n)])]
    another operation x0 -> x4, other arithmetic: none -> 3.53 us  [on_device(): merged.append(lax.optimization_barrier(jnp.stack([early[hop], theirs])))]
    another operation x12, other arithmetic: 3.24 us -> 1.29 us  [on_device(): jnp.stack([kept[hop] + mine, kept_theirs + theirs])]
  transfers between devices with their start and end apart: 39 -> 47, of which waited for: 13 -> 19; matrix products, arithmetic and copies ran while one was open for 5% -> 6% of each run, Pallas kernels for 0% -> 0%
where the time goes in v3:
time: 173 us; the launch traced here: 172 us
  waiting for transfers between devices  80.7 us (47%)
  starting transfers between devices  64.9 us (38%)
  Pallas kernels  13.2 us (8%)
  other arithmetic  9.43 us (5%)
  local copies, waits for them, and re-layouts  3 us (2%)
    ppermute x4, waiting for transfers between devices, on_device(): moving = lax.ppermute(moving, ('c', 'z'), around)  31.1 us
    ppermute x19, starting transfers between devices, shift(): return lax.ppermute(array, axis, [(i, (i + step) % n) for i in range(n)])  25.6 us
    ppermute x20, waiting for transfers between devices, flip(): return lax.ppermute(array, axes, [(i, n - 1 - i) for i in range(n)])  22.8 us
    ppermute x19, waiting for transfers between devices, shift(): return lax.ppermute(array, axis, [(i, (i + step) % n) for i in range(n)])  21.9 us
    ppermute x20, starting transfers between devices, flip(): return lax.ppermute(array, axes, [(i, n - 1 - i) for i in range(n)])  19.6 us
    ppermute x4, starting transfers between devices, on_device(): large = lax.ppermute(large, ('c', 'z'), around)  17.6 us
    pallas_call x1, Pallas kernels, tile_product(): pl.pallas_call(body, out_shape=[jax.ShapeDtypeStruct(shape, jnp.bfloat16)...  13.2 us
    ppermute x4, waiting for transfers between devices, on_device(): large = lax.ppermute(large, ('c', 'z'), around)  4.88 us
  transfers between devices with their start and end apart: 47, of which 19 were waited for; matrix products, arithmetic and copies ran while one was open for 6% of the time, Pallas kernels for 0%

profile of v3, /device:TPU:1, one launch (start us, length us, event | category | flops | bytes accessed | tf_op | source)
XLA Modules:
  0.0 172.3 jit_solution(6131295660736175061)
XLA Ops:
  0.0 3.7 %collective-permute-start.1 = (bf16[8,128,256]{2,1,0:T(8,128)(2,1)}, bf16[8,128,256]{2,1,0:T(8,128)(2,1)S(1)}, u32[]{:S(2)}, u32[]{:S(2)}) collective-permute-start(bf16[8,128,256]{2,1,0:T(8,128)(2,1)} %bitcast.50), channel_id=1, source_target_pairs={{0,128},{128,0},{1,129},{129,1},{2,130},{130,2},{3,131},{131,3},{4... | collective-permute-start | bytes 1572872 | tf_op jit(solution)/shard_map/ppermute | solution.py:21
  3.7 2.5 %collective-permute-start.5 = (bf16[8,128,256]{2,1,0:T(8,128)(2,1)}, bf16[8,128,256]{2,1,0:T(8,128)(2,1)S(1)}, u32[]{:S(2)}, u32[]{:S(2)}) collective-permute-start(bf16[8,128,256]{2,1,0:T(8,128)(2,1)} %bitcast.51), channel_id=1, source_target_pairs={{0,96},{32,0},{64,32},{96,64},{1,97},{33,1},{65,33},{97,65},{2,98}... | collective-permute-start | bytes 1572872 | tf_op jit(solution)/shard_map/ppermute | solution.py:21
  6.2 8.4 %collective-permute-done.1.rest_2_ = bf16[8,128,256]{2,1,0:T(8,128)(2,1)S(1)} collective-permute-done((bf16[8,128,256]{2,1,0:T(8,128)(2,1)}, bf16[8,128,256]{2,1,0:T(8,128)(2,1)S(1)}, u32[]{:S(2)}, u32[]{:S(2)}) %collective-permute-start.1) | collective-permute-done | bytes 524320 | tf_op jit(solution)/shard_map/ppermute | solution.py:21
  14.7 1.9 %collective-permute-start.11 = (bf16[8,128,256]{2,1,0:T(8,128)(2,1)S(1)}, bf16[8,128,256]{2,1,0:T(8,128)(2,1)S(1)}, u32[]{:S(2)}, u32[]{:S(2)}) collective-permute-start(bf16[8,128,256]{2,1,0:T(8,128)(2,1)S(1)} %collective-permute-done.1.rest_2_), channel_id=1, source_target_pairs={{0,32},{32,64},{64,96},{96,0},{1,33},{33,65},{65,97},{97,1},{2,34}... | collective-permute-start | bytes 1572872 | tf_op jit(solution)/shard_map/ppermute | solution.py:21
  16.6 1.3 collective-permute-start.13
  17.9 2.4 %collective-permute-start.9 = (bf16[4,128,256]{2,1,0:T(8,128)(2,1)S(1)}, bf16[4,128,256]{2,1,0:T(8,128)(2,1)S(1)}, u32[]{:S(2)}, u32[]{:S(2)}) collective-permute-start(bf16[4,128,256]{2,1,0:T(8,128)(2,1)S(1)} %slice.41), channel_id=1, source_target_pairs={{0,96},{32,0},{64,32},{96,64},{1,97},{33,1},{65,33},{97,65},{2,98}... | collective-permute-start | bytes 786440 | tf_op jit(solution)/shard_map/ppermute | solution.py:21
  20.4 3.5 %collective-permute-start = (bf16[8,128,256]{2,1,0:T(8,128)(2,1)}, bf16[8,128,256]{2,1,0:T(8,128)(2,1)S(1)}, u32[]{:S(2)}, u32[]{:S(2)}) collective-permute-start(bf16[8,128,256]{2,1,0:T(8,128)(2,1)} %bitcast.53), channel_id=1, source_target_pairs={{0,16},{16,0},{1,17},{17,1},{2,18},{18,2},{3,19},{19,3},{4,20},{20... | collective-permute-start | bytes 1572872 | tf_op jit(solution)/shard_map/ppermute | solution.py:21
  23.9 10.0 %collective-permute-done.9.rest_10_ = bf16[4,128,256]{2,1,0:T(8,128)(2,1)S(1)} collective-permute-done((bf16[4,128,256]{2,1,0:T(8,128)(2,1)S(1)}, bf16[4,128,256]{2,1,0:T(8,128)(2,1)S(1)}, u32[]{:S(2)}, u32[]{:S(2)}) %collective-permute-start.9) | collective-permute-done | bytes 262176 | tf_op jit(solution)/shard_map/ppermute | solution.py:21
  33.8 2.7 %collective-permute-start.2 = (bf16[8,128,256]{2,1,0:T(8,128)(2,1)S(1)}, bf16[8,128,256]{2,1,0:T(8,128)(2,1)}, u32[]{:S(2)}, u32[]{:S(2)}) collective-permute-start(bf16[8,128,256]{2,1,0:T(8,128)(2,1)S(1)} %collective-permute-done.1.rest_2_), channel_id=1, source_target_pairs={{0,16},{16,0},{1,17},{17,1},{2,18},{18,2},{3,19},{19,3},{4,20},{20... | collective-permute-start | bytes 1572872 | tf_op jit(solution)/shard_map/ppermute | solution.py:21
  36.8 2.1 %collective-permute-start.4 = (bf16[8,128,256]{2,1,0:T(8,128)(2,1)S(1)}, bf16[8,128,256]{2,1,0:T(8,128)(2,1)}, u32[]{:S(2)}, u32[]{:S(2)}) collective-permute-start(bf16[8,128,256]{2,1,0:T(8,128)(2,1)S(1)} %collective-permute-done.3.rest_4_), channel_id=1, source_target_pairs={{0,16},{16,0},{1,17},{17,1},{2,18},{18,2},{3,19},{19,3},{4,20},{20... | collective-permute-start | bytes 1572872 | tf_op jit(solution)/shard_map/ppermute | solution.py:21
  41.7 2.6 %collective-permute-start.17 = (bf16[4,128,256]{2,1,0:T(8,128)(2,1)}, bf16[4,128,256]{2,1,0:T(8,128)(2,1)}, u32[]{:S(2)}, u32[]{:S(2)}) collective-permute-start(bf16[4,128,256]{2,1,0:T(8,128)(2,1)} %slice.43), channel_id=1, source_target_pairs={{0,96},{32,0},{64,32},{96,64},{1,97},{33,1},{65,33},{97,65},{2,98}... | collective-permute-start | bytes 786440 | tf_op jit(solution)/shard_map/ppermute | solution.py:21
  45.6 0.8 collective-permute-start.6
  47.7 2.4 %collective-permute-done.15.rest_16_ = bf16[4,128,256]{2,1,0:T(8,128)(2,1)} collective-permute-done((bf16[4,128,256]{2,1,0:T(8,128)(2,1)}, bf16[4,128,256]{2,1,0:T(8,128)(2,1)}, u32[]{:S(2)}, u32[]{:S(2)}) %collective-permute-start.15) | collective-permute-done | bytes 262176 | tf_op jit(solution)/shard_map/ppermute | solution.py:21
  50.1 1.0 collective-permute-start.16
  51.4 0.8 select_reduce_fusion.packed_ref
  53.6 13.2 %tile_product.1 = (bf16[2,128,256]{2,1,0:T(8,128)(2,1)}, bf16[4,128,256]{2,1,0:T(8,128)(2,1)}, bf16[4,128,256]{2,1,0:T(8,128)(2,1)}, bf16[4,128,256]{2,1,0:T(8,1...) custom-call(s32[1]{0:T(128)} %bitcast.46.count_ref, ...), custom_call_target="tpu_custom_call" | custom-call | flops 3221225472 | bytes 31457280 | tf_op jit(solution)/shard_map/tile_product/pallas_call | solution.py:131
  67.4 1.2 collective-permute-done.40
  68.6 1.0 pad_maximum_fusion.6
  69.7 11.9 %collective-permute-start.41 = (bf16[2,4,128,256]{3,2,1,0:T(8,128)(2,1)S(1)}, bf16[2,4,128,256]{3,2,1,0:T(8,128)(2,1)S(1)}, u32[]{:S(2)}, u32[]{:S(2)}) collective-permute-start(bf16[2,4,128,256]{3,2,1,0:T(8,128)(2,1)S(1)} %pad_maximum_fusion.6), channel_id=1, source_target_pairs={{0,2},{2,4},{4,6},{6,8},{8,10},{10,12},{12,14},{14,0},{16,30},{18,... | collective-permute-start | bytes 1572872 | tf_op jit(solution)/shard_map/ppermute | solution.py:231
  81.5 1.2 pad_maximum_fusion.2
  82.8 4.9 %collective-permute-done.41 = bf16[2,4,128,256]{3,2,1,0:T(8,128)(2,1)S(1)} collective-permute-done((bf16[2,4,128,256]{3,2,1,0:T(8,128)(2,1)S(1)}, bf16[2,4,128,256]{3,2,1,0:T(8,128)(2,1)S(1)}, u32[]{:S(2)}, u32[]{:S(2)}) %collective-permute-start.41) | collective-permute-done | bytes 524320 | tf_op jit(solution)/shard_map/ppermute | solution.py:231
  87.8 3.2 %collective-permute-start.42 = (bf16[2,8,128,256]{3,2,1,0:T(8,128)(2,1)S(1)}, bf16[2,8,128,256]{3,2,1,0:T(8,128)(2,1)S(1)}, u32[]{:S(2)}, u32[]{:S(2)}) collective-permute-start(bf16[2,8,128,256]{3,2,1,0:T(8,128)(2,1)S(1)} %select_add_fusion), channel_id=1, source_target_pairs={{0,2},{2,4},{4,6},{6,8},{8,10},{10,12},{12,14},{14,0},{16,30},{18,... | collective-permute-start | bytes 3145736 | tf_op jit(solution)/shard_map/ppermute | solution.py:231
  91.5 1.4 collective-permute-start.28
  92.8 0.8 collective-permute-start.26
  93.6 3.6 %collective-permute-done.30 = bf16[2,128,256]{2,1,0:T(8,128)(2,1)S(1)} collective-permute-done((bf16[2,128,256]{2,1,0:T(8,128)(2,1)}, bf16[2,128,256]{2,1,0:T(8,128)(2,1)S(1)}, u32[]{:S(2)}, u32[]{:S(2)}) %collective-permute-start.30) | collective-permute-done | bytes 131104 | tf_op jit(solution)/shard_map/ppermute | solution.py:184
  97.3 2.4 %collective-permute-done.28 = bf16[2,128,256]{2,1,0:T(8,128)(2,1)S(1)} collective-permute-done((bf16[2,128,256]{2,1,0:T(8,128)(2,1)}, bf16[2,128,256]{2,1,0:T(8,128)(2,1)S(1)}, u32[]{:S(2)}, u32[]{:S(2)}) %collective-permute-start.28) | collective-permute-done | bytes 131104 | tf_op jit(solution)/shard_map/ppermute | solution.py:184
  99.7 0.9 add_bitcast_fusion.7
  100.6 1.5 collective-permute-start.22
  102.2 1.2 pad_maximum_fusion.1
  103.8 2.5 %collective-permute-start.43 = (bf16[2,8,128,256]{3,2,1,0:T(8,128)(2,1)S(1)}, bf16[2,8,128,256]{3,2,1,0:T(8,128)(2,1)S(1)}, u32[]{:S(2)}, u32[]{:S(2)}) collective-permute-start(bf16[2,8,128,256]{3,2,1,0:T(8,128)(2,1)S(1)} %add.344), channel_id=1, source_target_pairs={{0,2},{2,4},{4,6},{6,8},{8,10},{10,12},{12,14},{14,0},{16,30},{18,... | collective-permute-start | bytes 3145736 | tf_op jit(solution)/shard_map/ppermute | solution.py:231
  106.9 3.7 %collective-permute-done.25 = bf16[4,128,256]{2,1,0:T(8,128)(2,1)S(1)} collective-permute-done((bf16[4,128,256]{2,1,0:T(8,128)(2,1)}, bf16[4,128,256]{2,1,0:T(8,128)(2,1)S(1)}, u32[]{:S(2)}, u32[]{:S(2)}) %collective-permute-start.25) | collective-permute-done | bytes 262176 | tf_op jit(solution)/shard_map/ppermute | solution.py:184
  110.8 10.0 %collective-permute-done.31 = bf16[2,2,128,256]{3,2,1,0:T(8,128)(2,1)S(1)} collective-permute-done((bf16[2,2,128,256]{3,2,1,0:T(8,128)(2,1)S(1)}, bf16[2,2,128,256]{3,2,1,0:T(8,128)(2,1)S(1)}, u32[]{:S(2)}, u32[]{:S(2)}) %collective-permute-start.31) | collective-permute-done | bytes 262176 | tf_op jit(solution)/shard_map/ppermute | solution.py:232
  120.8 2.7 %collective-permute-start.24 = (bf16[4,128,256]{2,1,0:T(8,128)(2,1)S(1)}, bf16[4,128,256]{2,1,0:T(8,128)(2,1)S(1)}, u32[]{:S(2)}, u32[]{:S(2)}) collective-permute-start(bf16[4,128,256]{2,1,0:T(8,128)(2,1)S(1)} %copy-done.21), channel_id=1, source_target_pairs={{0,17},{1,16},{16,1},{17,0},{2,19},{3,18},{18,3},{19,2},{4,21},{5,... | collective-permute-start | bytes 786440 | tf_op jit(solution)/shard_map/ppermute | solution.py:184
  123.5 2.5 %collective-permute-start.19 = (bf16[4,128,256]{2,1,0:T(8,128)(2,1)S(1)}, bf16[4,128,256]{2,1,0:T(8,128)(2,1)S(1)}, u32[]{:S(2)}, u32[]{:S(2)}) collective-permute-start(bf16[4,128,256]{2,1,0:T(8,128)(2,1)S(1)} %copy-done.20), channel_id=1, source_target_pairs={{0,1},{1,0},{2,3},{3,2},{4,5},{5,4},{6,7},{7,6},{8,9},{9,8},{10,11... | collective-permute-start | bytes 786440 | tf_op jit(solution)/shard_map/ppermute | solution.py:184
  127.2 1.3 collective-permute-done.24
  128.5 2.3 %collective-permute-start.21 = (bf16[4,128,256]{2,1,0:T(8,128)(2,1)S(1)}, bf16[4,128,256]{2,1,0:T(8,128)(2,1)S(1)}, u32[]{:S(2)}, u32[]{:S(2)}) collective-permute-start(bf16[4,128,256]{2,1,0:T(8,128)(2,1)S(1)} %copy-done.18), channel_id=1, source_target_pairs={{0,17},{1,16},{16,1},{17,0},{2,19},{3,18},{18,3},{19,2},{4,21},{5,... | collective-permute-start | bytes 786440 | tf_op jit(solution)/shard_map/ppermute | solution.py:184
  130.9 3.7 %collective-permute-done.32 = bf16[2,4,128,256]{3,2,1,0:T(8,128)(2,1)S(1)} collective-permute-done((bf16[2,4,128,256]{3,2,1,0:T(8,128)(2,1)S(1)}, bf16[2,4,128,256]{3,2,1,0:T(8,128)(2,1)S(1)}, u32[]{:S(2)}, u32[]{:S(2)}) %collective-permute-start.32) | collective-permute-done | bytes 524320 | tf_op jit(solution)/shard_map/ppermute | solution.py:232
  134.7 1.0 collective-permute-start.33
  135.7 2.6 %collective-permute-done.19 = bf16[4,128,256]{2,1,0:T(8,128)(2,1)S(1)} collective-permute-done((bf16[4,128,256]{2,1,0:T(8,128)(2,1)S(1)}, bf16[4,128,256]{2,1,0:T(8,128)(2,1)S(1)}, u32[]{:S(2)}, u32[]{:S(2)}) %collective-permute-start.19) | collective-permute-done | bytes 262176 | tf_op jit(solution)/shard_map/ppermute | solution.py:184
  138.4 1.3 collective-permute-done.21
  139.8 11.7 %collective-permute-done.33 = bf16[2,4,128,256]{3,2,1,0:T(8,128)(2,1)S(1)} collective-permute-done((bf16[2,4,128,256]{3,2,1,0:T(8,128)(2,1)S(1)}, bf16[2,4,128,256]{3,2,1,0:T(8,128)(2,1)S(1)}, u32[]{:S(2)}, u32[]{:S(2)}) %collective-permute-start.33) | collective-permute-done | bytes 524320 | tf_op jit(solution)/shard_map/ppermute | solution.py:232
  151.6 1.0 collective-permute-start.34
  152.7 1.5 collective-permute-start.36
  154.3 5.7 %collective-permute-done.34 = bf16[2,4,128,256]{3,2,1,0:T(8,128)(2,1)S(1)} collective-permute-done((bf16[2,4,128,256]{3,2,1,0:T(8,128)(2,1)S(1)}, bf16[2,4,128,256]{3,2,1,0:T(8,128)(2,1)S(1)}, u32[]{:S(2)}, u32[]{:S(2)}) %collective-permute-start.34) | collective-permute-done | bytes 524320 | tf_op jit(solution)/shard_map/ppermute | solution.py:232
  160.0 2.9 %collective-permute-start.35 = (bf16[4,128,256]{2,1,0:T(8,128)(2,1)S(1)}, bf16[4,128,256]{2,1,0:T(8,128)(2,1)S(1)}, u32[]{:S(2)}, u32[]{:S(2)}) collective-permute-start(bf16[4,128,256]{2,1,0:T(8,128)(2,1)S(1)} %slice_bitcast_fusion.2), channel_id=1, source_target_pairs={{0,16},{16,0},{1,17},{17,1},{2,18},{18,2},{3,19},{19,3},{4,20},{20... | collective-permute-start | bytes 786440 | tf_op jit(solution)/shard_map/ppermute | solution.py:184
  163.0 1.8 %collective-permute-start.46 = (bf16[4,128,256]{2,1,0:T(8,128)(2,1)S(1)}, bf16[4,128,256]{2,1,0:T(8,128)(2,1)S(1)}, u32[]{:S(2)}, u32[]{:S(2)}) collective-permute-start(bf16[4,128,256]{2,1,0:T(8,128)(2,1)S(1)} %slice.49), channel_id=1, source_target_pairs={{0,1},{1,0},{2,3},{3,2},{4,5},{5,4},{6,7},{7,6},{8,9},{9,8},{10,11... | collective-permute-start | bytes 786440 | tf_op jit(solution)/shard_map/ppermute | solution.py:184
  164.9 6.5 %collective-permute-done.46 = bf16[4,128,256]{2,1,0:T(8,128)(2,1)S(1)} collective-permute-done((bf16[4,128,256]{2,1,0:T(8,128)(2,1)S(1)}, bf16[4,128,256]{2,1,0:T(8,128)(2,1)S(1)}, u32[]{:S(2)}, u32[]{:S(2)}) %collective-permute-start.46) | collective-permute-done | bytes 262176 | tf_op jit(solution)/shard_map/ppermute | solution.py:184
  171.5 0.8 pad_maximum_fusion.7
  (130 shorter events, 11.0 us)
Async XLA Ops:
  0.0 14.7 %collective-permute-start.1 = (bf16[8,128,256]{2,1,0:T(8,128)(2,1)}, bf16[8,128,256]{2,1,0:T(8,128)(2,1)S(1)}, u32[]{:S(2)}, u32[]{:S(2)}) collective-permute-start(bf16[8,128,256]{2,1,0:T(8,128)(2,1)} %bitcast.50), channel_id=1, source_target_pairs={{0,128},{128,0},{1,129},{129,1},{2,130},{130,2},{3,131},{131,3},{4... | collective-permute-start | bytes 1572872 | tf_op jit(solution)/shard_map/ppermute | solution.py:21
  3.7 14.1 %collective-permute-start.5 = (bf16[8,128,256]{2,1,0:T(8,128)(2,1)}, bf16[8,128,256]{2,1,0:T(8,128)(2,1)S(1)}, u32[]{:S(2)}, u32[]{:S(2)}) collective-permute-start(bf16[8,128,256]{2,1,0:T(8,128)(2,1)} %bitcast.51), channel_id=1, source_target_pairs={{0,96},{32,0},{64,32},{96,64},{1,97},{33,1},{65,33},{97,65},{2,98}... | collective-permute-start | bytes 1572872 | tf_op jit(solution)/shard_map/ppermute | solution.py:21
  6.2 14.1 %collective-permute-start.3 = (bf16[8,128,256]{2,1,0:T(8,128)(2,1)}, bf16[8,128,256]{2,1,0:T(8,128)(2,1)S(1)}, u32[]{:S(2)}, u32[]{:S(2)}) collective-permute-start(bf16[8,128,256]{2,1,0:T(8,128)(2,1)} %bitcast.52), channel_id=1, source_target_pairs={{0,32},{32,64},{64,96},{96,0},{1,33},{33,65},{65,97},{97,1},{2,34}... | collective-permute-start | bytes 1572872 | tf_op jit(solution)/shard_map/ppermute | solution.py:21
  14.7 24.3 %collective-permute-start.11 = (bf16[8,128,256]{2,1,0:T(8,128)(2,1)S(1)}, bf16[8,128,256]{2,1,0:T(8,128)(2,1)S(1)}, u32[]{:S(2)}, u32[]{:S(2)}) collective-permute-start(bf16[8,128,256]{2,1,0:T(8,128)(2,1)S(1)} %collective-permute-done.1.rest_2_), channel_id=1, source_target_pairs={{0,32},{32,64},{64,96},{96,0},{1,33},{33,65},{65,97},{97,1},{2,34}... | collective-permute-start | bytes 1572872 | tf_op jit(solution)/shard_map/ppermute | solution.py:21
  16.6 22.5 %collective-permute-start.13 = (bf16[8,128,256]{2,1,0:T(8,128)(2,1)S(1)}, bf16[8,128,256]{2,1,0:T(8,128)(2,1)S(1)}, u32[]{:S(2)}, u32[]{:S(2)}) collective-permute-start(bf16[8,128,256]{2,1,0:T(8,128)(2,1)S(1)} %collective-permute-done.1.rest_2_), channel_id=1, source_target_pairs={{0,96},{32,0},{64,32},{96,64},{1,97},{33,1},{65,33},{97,65},{2,98}... | collective-permute-start | bytes 1572872 | tf_op jit(solution)/shard_map/ppermute | solution.py:21
  17.9 16.0 %collective-permute-start.9 = (bf16[4,128,256]{2,1,0:T(8,128)(2,1)S(1)}, bf16[4,128,256]{2,1,0:T(8,128)(2,1)S(1)}, u32[]{:S(2)}, u32[]{:S(2)}) collective-permute-start(bf16[4,128,256]{2,1,0:T(8,128)(2,1)S(1)} %slice.41), channel_id=1, source_target_pairs={{0,96},{32,0},{64,32},{96,64},{1,97},{33,1},{65,33},{97,65},{2,98}... | collective-permute-start | bytes 786440 | tf_op jit(solution)/shard_map/ppermute | solution.py:21
  20.3 16.5 %collective-permute-start.7 = (bf16[4,128,256]{2,1,0:T(8,128)(2,1)S(1)}, bf16[4,128,256]{2,1,0:T(8,128)(2,1)}, u32[]{:S(2)}, u32[]{:S(2)}) collective-permute-start(bf16[4,128,256]{2,1,0:T(8,128)(2,1)S(1)} %slice.40), channel_id=1, source_target_pairs={{0,32},{32,64},{64,96},{96,0},{1,33},{33,65},{65,97},{97,1},{2,34}... | collective-permute-start | bytes 786440 | tf_op jit(solution)/shard_map/ppermute | solution.py:21
  20.4 20.5 %collective-permute-start = (bf16[8,128,256]{2,1,0:T(8,128)(2,1)}, bf16[8,128,256]{2,1,0:T(8,128)(2,1)S(1)}, u32[]{:S(2)}, u32[]{:S(2)}) collective-permute-start(bf16[8,128,256]{2,1,0:T(8,128)(2,1)} %bitcast.53), channel_id=1, source_target_pairs={{0,16},{16,0},{1,17},{17,1},{2,18},{18,2},{3,19},{19,3},{4,20},{20... | collective-permute-start | bytes 1572872 | tf_op jit(solution)/shard_map/ppermute | solution.py:21
  33.8 12.6 %collective-permute-start.2 = (bf16[8,128,256]{2,1,0:T(8,128)(2,1)S(1)}, bf16[8,128,256]{2,1,0:T(8,128)(2,1)}, u32[]{:S(2)}, u32[]{:S(2)}) collective-permute-start(bf16[8,128,256]{2,1,0:T(8,128)(2,1)S(1)} %collective-permute-done.1.rest_2_), channel_id=1, source_target_pairs={{0,16},{16,0},{1,17},{17,1},{2,18},{18,2},{3,19},{19,3},{4,20},{20... | collective-permute-start | bytes 1572872 | tf_op jit(solution)/shard_map/ppermute | solution.py:21
  36.8 9.7 %collective-permute-start.4 = (bf16[8,128,256]{2,1,0:T(8,128)(2,1)S(1)}, bf16[8,128,256]{2,1,0:T(8,128)(2,1)}, u32[]{:S(2)}, u32[]{:S(2)}) collective-permute-start(bf16[8,128,256]{2,1,0:T(8,128)(2,1)S(1)} %collective-permute-done.3.rest_4_), channel_id=1, source_target_pairs={{0,16},{16,0},{1,17},{17,1},{2,18},{18,2},{3,19},{19,3},{4,20},{20... | collective-permute-start | bytes 1572872 | tf_op jit(solution)/shard_map/ppermute | solution.py:21
  38.9 2.0 %collective-permute-start.10 = (bf16[4,128,256]{2,1,0:T(8,128)(2,1)S(1)}, bf16[4,128,256]{2,1,0:T(8,128)(2,1)S(1)}, u32[]{:S(2)}, u32[]{:S(2)}) collective-permute-start(bf16[4,128,256]{2,1,0:T(8,128)(2,1)S(1)} %collective-permute-done.9.rest_10_), channel_id=1, source_target_pairs={{0,16},{16,0},{1,17},{17,1},{2,18},{18,2},{3,19},{19,3},{4,20},{20... | collective-permute-start | bytes 786440 | tf_op jit(solution)/shard_map/ppermute | solution.py:21
  39.0 6.6 %collective-permute-start.8 = (bf16[4,128,256]{2,1,0:T(8,128)(2,1)}, bf16[4,128,256]{2,1,0:T(8,128)(2,1)}, u32[]{:S(2)}, u32[]{:S(2)}) collective-permute-start(bf16[4,128,256]{2,1,0:T(8,128)(2,1)} %collective-permute-done.7.rest_8_), channel_id=1, source_target_pairs={{0,16},{16,0},{1,17},{17,1},{2,18},{18,2},{3,19},{19,3},{4,20},{20... | collective-permute-start | bytes 786440 | tf_op jit(solution)/shard_map/ppermute | solution.py:21
  40.9 9.2 %collective-permute-start.15 = (bf16[4,128,256]{2,1,0:T(8,128)(2,1)}, bf16[4,128,256]{2,1,0:T(8,128)(2,1)}, u32[]{:S(2)}, u32[]{:S(2)}) collective-permute-start(bf16[4,128,256]{2,1,0:T(8,128)(2,1)} %slice.42), channel_id=1, source_target_pairs={{0,32},{32,64},{64,96},{96,0},{1,33},{33,65},{65,97},{97,1},{2,34}... | collective-permute-start | bytes 786440 | tf_op jit(solution)/shard_map/ppermute | solution.py:21
  41.7 9.5 %collective-permute-start.17 = (bf16[4,128,256]{2,1,0:T(8,128)(2,1)}, bf16[4,128,256]{2,1,0:T(8,128)(2,1)}, u32[]{:S(2)}, u32[]{:S(2)}) collective-permute-start(bf16[4,128,256]{2,1,0:T(8,128)(2,1)} %slice.43), channel_id=1, source_target_pairs={{0,96},{32,0},{64,32},{96,64},{1,97},{33,1},{65,33},{97,65},{2,98}... | collective-permute-start | bytes 786440 | tf_op jit(solution)/shard_map/ppermute | solution.py:21
  45.6 6.5 %collective-permute-start.6 = (bf16[8,128,256]{2,1,0:T(8,128)(2,1)S(1)}, bf16[8,128,256]{2,1,0:T(8,128)(2,1)}, u32[]{:S(2)}, u32[]{:S(2)}) collective-permute-start(bf16[8,128,256]{2,1,0:T(8,128)(2,1)S(1)} %collective-permute-done.5.rest_6_), channel_id=1, source_target_pairs={{0,16},{16,0},{1,17},{17,1},{2,18},{18,2},{3,19},{19,3},{4,20},{20... | collective-permute-start | bytes 1572872 | tf_op jit(solution)/shard_map/ppermute | solution.py:21
  46.5 5.7 %collective-permute-start.12 = (bf16[8,128,256]{2,1,0:T(8,128)(2,1)S(1)}, bf16[8,128,256]{2,1,0:T(8,128)(2,1)}, u32[]{:S(2)}, u32[]{:S(2)}) collective-permute-start(bf16[8,128,256]{2,1,0:T(8,128)(2,1)S(1)} %collective-permute-done.11.rest_12_), channel_id=1, source_target_pairs={{0,16},{16,0},{1,17},{17,1},{2,18},{18,2},{3,19},{19,3},{4,20},{20... | collective-permute-start | bytes 1572872 | tf_op jit(solution)/shard_map/ppermute | solution.py:21
  46.6 5.6 %collective-permute-start.14 = (bf16[8,128,256]{2,1,0:T(8,128)(2,1)S(1)}, bf16[8,128,256]{2,1,0:T(8,128)(2,1)}, u32[]{:S(2)}, u32[]{:S(2)}) collective-permute-start(bf16[8,128,256]{2,1,0:T(8,128)(2,1)S(1)} %collective-permute-done.13.rest_14_), channel_id=1, source_target_pairs={{0,16},{16,0},{1,17},{17,1},{2,18},{18,2},{3,19},{19,3},{4,20},{20... | collective-permute-start | bytes 1572872 | tf_op jit(solution)/shard_map/ppermute | solution.py:21
  50.1 2.4 %collective-permute-start.16 = (bf16[4,128,256]{2,1,0:T(8,128)(2,1)}, bf16[4,128,256]{2,1,0:T(8,128)(2,1)S(1)}, u32[]{:S(2)}, u32[]{:S(2)}) collective-permute-start(bf16[4,128,256]{2,1,0:T(8,128)(2,1)} %collective-permute-done.15.rest_16_), channel_id=1, source_target_pairs={{0,16},{16,0},{1,17},{17,1},{2,18},{18,2},{3,19},{19,3},{4,20},{20... | collective-permute-start | bytes 786440 | tf_op jit(solution)/shard_map/ppermute | solution.py:21
  51.1 1.7 %collective-permute-start.18 = (bf16[4,128,256]{2,1,0:T(8,128)(2,1)}, bf16[4,128,256]{2,1,0:T(8,128)(2,1)S(1)}, u32[]{:S(2)}, u32[]{:S(2)}) collective-permute-start(bf16[4,128,256]{2,1,0:T(8,128)(2,1)} %collective-permute-done.17.rest_18_), channel_id=1, source_target_pairs={{0,16},{16,0},{1,17},{17,1},{2,18},{18,2},{3,19},{19,3},{4,20},{20... | collective-permute-start | bytes 786440 | tf_op jit(solution)/shard_map/ppermute | solution.py:21
  66.8 61.7 %copy-start.18 = (bf16[4,128,256]{2,1,0:T(8,128)(2,1)S(1)}, bf16[4,128,256]{2,1,0:T(8,128)(2,1)}, u32[]{:S(2)}) copy-start(bf16[4,128,256]{2,1,0:T(8,128)(2,1)} %get-tuple-element.35) | copy-start | bytes 786436
  66.8 1.8 %collective-permute-start.40 = (bf16[4,128,256]{2,1,0:T(8,128)(2,1)}, bf16[4,128,256]{2,1,0:T(8,128)(2,1)S(1)}, u32[]{:S(2)}, u32[]{:S(2)}) collective-permute-start(bf16[4,128,256]{2,1,0:T(8,128)(2,1)} %get-tuple-element.57), channel_id=1, source_target_pairs={{0,16},{16,0},{1,17},{17,1},{2,18},{18,2},{3,19},{19,3},{4,20},{20... | collective-permute-start | bytes 786440 | tf_op jit(solution)/shard_map/ppermute | solution.py:184
  66.9 14.6 %collective-permute-start.39 = (bf16[8,128,256]{2,1,0:T(8,128)(2,1)}, bf16[8,128,256]{2,1,0:T(8,128)(2,1)S(1)}, u32[]{:S(2)}, u32[]{:S(2)}) collective-permute-start(bf16[8,128,256]{2,1,0:T(8,128)(2,1)} %get-tuple-element.55), channel_id=1, source_target_pairs={{0,16},{16,0},{1,17},{17,1},{2,18},{18,2},{3,19},{19,3},{4,20},{20... | collective-permute-start | bytes 1572872 | tf_op jit(solution)/shard_map/ppermute | solution.py:184
  69.7 18.0 %collective-permute-start.41 = (bf16[2,4,128,256]{3,2,1,0:T(8,128)(2,1)S(1)}, bf16[2,4,128,256]{3,2,1,0:T(8,128)(2,1)S(1)}, u32[]{:S(2)}, u32[]{:S(2)}) collective-permute-start(bf16[2,4,128,256]{3,2,1,0:T(8,128)(2,1)S(1)} %pad_maximum_fusion.6), channel_id=1, source_target_pairs={{0,2},{2,4},{4,6},{6,8},{8,10},{10,12},{12,14},{14,0},{16,30},{18,... | collective-permute-start | bytes 1572872 | tf_op jit(solution)/shard_map/ppermute | solution.py:231
  87.8 15.7 %collective-permute-start.42 = (bf16[2,8,128,256]{3,2,1,0:T(8,128)(2,1)S(1)}, bf16[2,8,128,256]{3,2,1,0:T(8,128)(2,1)S(1)}, u32[]{:S(2)}, u32[]{:S(2)}) collective-permute-start(bf16[2,8,128,256]{3,2,1,0:T(8,128)(2,1)S(1)} %select_add_fusion), channel_id=1, source_target_pairs={{0,2},{2,4},{4,6},{6,8},{8,10},{10,12},{12,14},{14,0},{16,30},{18,... | collective-permute-start | bytes 3145736 | tf_op jit(solution)/shard_map/ppermute | solution.py:231
  91.0 1.9 %collective-permute-start.29 = (bf16[2,128,256]{2,1,0:T(8,128)(2,1)}, bf16[2,128,256]{2,1,0:T(8,128)(2,1)S(1)}, u32[]{:S(2)}, u32[]{:S(2)}) collective-permute-start(bf16[2,128,256]{2,1,0:T(8,128)(2,1)} %get-tuple-element.46), channel_id=1, source_target_pairs={{0,16},{16,0},{1,17},{17,1},{2,18},{18,2},{3,19},{19,3},{4,20},{20... | collective-permute-start | bytes 393224 | tf_op jit(solution)/shard_map/ppermute | solution.py:184
  91.0 6.3 %collective-permute-start.30 = (bf16[2,128,256]{2,1,0:T(8,128)(2,1)}, bf16[2,128,256]{2,1,0:T(8,128)(2,1)S(1)}, u32[]{:S(2)}, u32[]{:S(2)}) collective-permute-start(bf16[2,128,256]{2,1,0:T(8,128)(2,1)} %get-tuple-element.47), channel_id=1, source_target_pairs={{0,17},{1,16},{16,1},{17,0},{2,19},{3,18},{18,3},{19,2},{4,21},{5,... | collective-permute-start | bytes 393224 | tf_op jit(solution)/shard_map/ppermute | solution.py:184
  91.0 9.7 %collective-permute-start.38 = (bf16[8,128,256]{2,1,0:T(8,128)(2,1)}, bf16[8,128,256]{2,1,0:T(8,128)(2,1)S(1)}, u32[]{:S(2)}, u32[]{:S(2)}) collective-permute-start(bf16[8,128,256]{2,1,0:T(8,128)(2,1)} %get-tuple-element.53), channel_id=1, source_target_pairs={{0,16},{16,0},{1,17},{17,1},{2,18},{18,2},{3,19},{19,3},{4,20},{20... | collective-permute-start | bytes 1572872 | tf_op jit(solution)/shard_map/ppermute | solution.py:184
  91.5 8.2 %collective-permute-start.28 = (bf16[2,128,256]{2,1,0:T(8,128)(2,1)}, bf16[2,128,256]{2,1,0:T(8,128)(2,1)S(1)}, u32[]{:S(2)}, u32[]{:S(2)}) collective-permute-start(bf16[2,128,256]{2,1,0:T(8,128)(2,1)} %get-tuple-element.45), channel_id=1, source_target_pairs={{0,1},{1,0},{2,3},{3,2},{4,5},{5,4},{6,7},{7,6},{8,9},{9,8},{10,11... | collective-permute-start | bytes 393224 | tf_op jit(solution)/shard_map/ppermute | solution.py:184
  92.8 13.4 %collective-permute-start.26 = (bf16[4,128,256]{2,1,0:T(8,128)(2,1)}, bf16[4,128,256]{2,1,0:T(8,128)(2,1)S(1)}, u32[]{:S(2)}, u32[]{:S(2)}) collective-permute-start(bf16[4,128,256]{2,1,0:T(8,128)(2,1)} %get-tuple-element.42), channel_id=1, source_target_pairs={{0,16},{16,0},{1,17},{17,1},{2,18},{18,2},{3,19},{19,3},{4,20},{20... | collective-permute-start | bytes 786440 | tf_op jit(solution)/shard_map/ppermute | solution.py:184
  97.3 9.1 %collective-permute-start.27 = (bf16[4,128,256]{2,1,0:T(8,128)(2,1)}, bf16[4,128,256]{2,1,0:T(8,128)(2,1)S(1)}, u32[]{:S(2)}, u32[]{:S(2)}) collective-permute-start(bf16[4,128,256]{2,1,0:T(8,128)(2,1)} %get-tuple-element.43), channel_id=1, source_target_pairs={{0,17},{1,16},{16,1},{17,0},{2,19},{3,18},{18,3},{19,2},{4,21},{5,... | collective-permute-start | bytes 786440 | tf_op jit(solution)/shard_map/ppermute | solution.py:184
  99.7 11.0 %collective-permute-start.25 = (bf16[4,128,256]{2,1,0:T(8,128)(2,1)}, bf16[4,128,256]{2,1,0:T(8,128)(2,1)S(1)}, u32[]{:S(2)}, u32[]{:S(2)}) collective-permute-start(bf16[4,128,256]{2,1,0:T(8,128)(2,1)} %get-tuple-element.41), channel_id=1, source_target_pairs={{0,1},{1,0},{2,3},{3,2},{4,5},{5,4},{6,7},{7,6},{8,9},{9,8},{10,11... | collective-permute-start | bytes 786440 | tf_op jit(solution)/shard_map/ppermute | solution.py:184
  100.6 26.0 %collective-permute-start.22 = (bf16[4,128,256]{2,1,0:T(8,128)(2,1)}, bf16[4,128,256]{2,1,0:T(8,128)(2,1)S(1)}, u32[]{:S(2)}, u32[]{:S(2)}) collective-permute-start(bf16[4,128,256]{2,1,0:T(8,128)(2,1)} %get-tuple-element.37), channel_id=1, source_target_pairs={{0,1},{1,0},{2,3},{3,2},{4,5},{5,4},{6,7},{7,6},{8,9},{9,8},{10,11... | collective-permute-start | bytes 786440 | tf_op jit(solution)/shard_map/ppermute | solution.py:184
  103.8 22.4 %collective-permute-start.43 = (bf16[2,8,128,256]{3,2,1,0:T(8,128)(2,1)S(1)}, bf16[2,8,128,256]{3,2,1,0:T(8,128)(2,1)S(1)}, u32[]{:S(2)}, u32[]{:S(2)}) collective-permute-start(bf16[2,8,128,256]{3,2,1,0:T(8,128)(2,1)S(1)} %add.344), channel_id=1, source_target_pairs={{0,2},{2,4},{4,6},{6,8},{8,10},{10,12},{12,14},{14,0},{16,30},{18,... | collective-permute-start | bytes 3145736 | tf_op jit(solution)/shard_map/ppermute | solution.py:231
  106.3 20.5 %collective-permute-start.23 = (bf16[4,128,256]{2,1,0:T(8,128)(2,1)}, bf16[4,128,256]{2,1,0:T(8,128)(2,1)S(1)}, u32[]{:S(2)}, u32[]{:S(2)}) collective-permute-start(bf16[4,128,256]{2,1,0:T(8,128)(2,1)} %get-tuple-element.38), channel_id=1, source_target_pairs={{0,16},{16,0},{1,17},{17,1},{2,18},{18,2},{3,19},{19,3},{4,20},{20... | collective-permute-start | bytes 786440 | tf_op jit(solution)/shard_map/ppermute | solution.py:184
  106.4 17.1 %collective-permute-start.37 = (bf16[8,128,256]{2,1,0:T(8,128)(2,1)S(1)}, bf16[8,128,256]{2,1,0:T(8,128)(2,1)S(1)}, u32[]{:S(2)}, u32[]{:S(2)}) collective-permute-start(bf16[8,128,256]{2,1,0:T(8,128)(2,1)S(1)} %copy-done.16), channel_id=1, source_target_pairs={{0,16},{16,0},{1,17},{17,1},{2,18},{18,2},{3,19},{19,3},{4,20},{20... | collective-permute-start | bytes 1572872 | tf_op jit(solution)/shard_map/ppermute | solution.py:184
  110.7 10.1 %collective-permute-start.31 = (bf16[2,2,128,256]{3,2,1,0:T(8,128)(2,1)S(1)}, bf16[2,2,128,256]{3,2,1,0:T(8,128)(2,1)S(1)}, u32[]{:S(2)}, u32[]{:S(2)}) collective-permute-start(bf16[2,2,128,256]{3,2,1,0:T(8,128)(2,1)S(1)} %pad_maximum_fusion.8), channel_id=1, source_target_pairs={{0,2},{2,4},{4,6},{6,8},{8,10},{10,12},{12,14},{14,0},{16,30},{18,... | collective-permute-start | bytes 786440 | tf_op jit(solution)/shard_map/ppermute | solution.py:232
  120.8 7.7 %collective-permute-start.24 = (bf16[4,128,256]{2,1,0:T(8,128)(2,1)S(1)}, bf16[4,128,256]{2,1,0:T(8,128)(2,1)S(1)}, u32[]{:S(2)}, u32[]{:S(2)}) collective-permute-start(bf16[4,128,256]{2,1,0:T(8,128)(2,1)S(1)} %copy-done.21), channel_id=1, source_target_pairs={{0,17},{1,16},{16,1},{17,0},{2,19},{3,18},{18,3},{19,2},{4,21},{5,... | collective-permute-start | bytes 786440 | tf_op jit(solution)/shard_map/ppermute | solution.py:184
  123.5 14.8 %collective-permute-start.19 = (bf16[4,128,256]{2,1,0:T(8,128)(2,1)S(1)}, bf16[4,128,256]{2,1,0:T(8,128)(2,1)S(1)}, u32[]{:S(2)}, u32[]{:S(2)}) collective-permute-start(bf16[4,128,256]{2,1,0:T(8,128)(2,1)S(1)} %copy-done.20), channel_id=1, source_target_pairs={{0,1},{1,0},{2,3},{3,2},{4,5},{5,4},{6,7},{7,6},{8,9},{9,8},{10,11... | collective-permute-start | bytes 786440 | tf_op jit(solution)/shard_map/ppermute | solution.py:184
  126.2 8.4 %collective-permute-start.32 = (bf16[2,4,128,256]{3,2,1,0:T(8,128)(2,1)S(1)}, bf16[2,4,128,256]{3,2,1,0:T(8,128)(2,1)S(1)}, u32[]{:S(2)}, u32[]{:S(2)}) collective-permute-start(bf16[2,4,128,256]{3,2,1,0:T(8,128)(2,1)S(1)} %select_add_fusion.1), channel_id=1, source_target_pairs={{0,2},{2,4},{4,6},{6,8},{8,10},{10,12},{12,14},{14,0},{16,30},{18,... | collective-permute-start | bytes 1572872 | tf_op jit(solution)/shard_map/ppermute | solution.py:232
  126.6 26.0 %collective-permute-start.44 = (bf16[2,8,128,256]{3,2,1,0:T(8,128)(2,1)S(1)}, bf16[2,8,128,256]{3,2,1,0:T(8,128)(2,1)S(1)}, u32[]{:S(2)}, u32[]{:S(2)}) collective-permute-start(bf16[2,8,128,256]{3,2,1,0:T(8,128)(2,1)S(1)} %add.345), channel_id=1, source_target_pairs={{0,2},{2,4},{4,6},{6,8},{8,10},{10,12},{12,14},{14,0},{16,30},{18,... | collective-permute-start | bytes 3145736 | tf_op jit(solution)/shard_map/ppermute | solution.py:231
  126.8 11.6 %collective-permute-start.20 = (bf16[4,128,256]{2,1,0:T(8,128)(2,1)S(1)}, bf16[4,128,256]{2,1,0:T(8,128)(2,1)S(1)}, u32[]{:S(2)}, u32[]{:S(2)}) collective-permute-start(bf16[4,128,256]{2,1,0:T(8,128)(2,1)S(1)} %copy-done.19), channel_id=1, source_target_pairs={{0,16},{16,0},{1,17},{17,1},{2,18},{18,2},{3,19},{19,3},{4,20},{20... | collective-permute-start | bytes 786440 | tf_op jit(solution)/shard_map/ppermute | solution.py:184
  128.5 11.2 %collective-permute-start.21 = (bf16[4,128,256]{2,1,0:T(8,128)(2,1)S(1)}, bf16[4,128,256]{2,1,0:T(8,128)(2,1)S(1)}, u32[]{:S(2)}, u32[]{:S(2)}) collective-permute-start(bf16[4,128,256]{2,1,0:T(8,128)(2,1)S(1)} %copy-done.18), channel_id=1, source_target_pairs={{0,17},{1,16},{16,1},{17,0},{2,19},{3,18},{18,3},{19,2},{4,21},{5,... | collective-permute-start | bytes 786440 | tf_op jit(solution)/shard_map/ppermute | solution.py:184
  134.7 16.7 %collective-permute-start.33 = (bf16[2,4,128,256]{3,2,1,0:T(8,128)(2,1)S(1)}, bf16[2,4,128,256]{3,2,1,0:T(8,128)(2,1)S(1)}, u32[]{:S(2)}, u32[]{:S(2)}) collective-permute-start(bf16[2,4,128,256]{3,2,1,0:T(8,128)(2,1)S(1)} %add.338), channel_id=1, source_target_pairs={{0,2},{2,4},{4,6},{6,8},{8,10},{10,12},{12,14},{14,0},{16,30},{18,... | collective-permute-start | bytes 1572872 | tf_op jit(solution)/shard_map/ppermute | solution.py:232
  151.6 8.4 %collective-permute-start.34 = (bf16[2,4,128,256]{3,2,1,0:T(8,128)(2,1)S(1)}, bf16[2,4,128,256]{3,2,1,0:T(8,128)(2,1)S(1)}, u32[]{:S(2)}, u32[]{:S(2)}) collective-permute-start(bf16[2,4,128,256]{3,2,1,0:T(8,128)(2,1)S(1)} %add.339), channel_id=1, source_target_pairs={{0,2},{2,4},{4,6},{6,8},{8,10},{10,12},{12,14},{14,0},{16,30},{18,... | collective-permute-start | bytes 1572872 | tf_op jit(solution)/shard_map/ppermute | solution.py:232
  152.6 10.3 %collective-permute-start.45 = (bf16[8,128,256]{2,1,0:T(8,128)(2,1)S(1)}, bf16[8,128,256]{2,1,0:T(8,128)(2,1)S(1)}, u32[]{:S(2)}, u32[]{:S(2)}) collective-permute-start(bf16[8,128,256]{2,1,0:T(8,128)(2,1)S(1)} %slice_bitcast_fusion), channel_id=1, source_target_pairs={{0,16},{16,0},{1,17},{17,1},{2,18},{18,2},{3,19},{19,3},{4,20},{20... | collective-permute-start | bytes 1572872 | tf_op jit(solution)/shard_map/ppermute | solution.py:184
  152.7 12.1 %collective-permute-start.36 = (bf16[4,128,256]{2,1,0:T(8,128)(2,1)S(1)}, bf16[4,128,256]{2,1,0:T(8,128)(2,1)S(1)}, u32[]{:S(2)}, u32[]{:S(2)}) collective-permute-start(bf16[4,128,256]{2,1,0:T(8,128)(2,1)S(1)} %copy-done.17), channel_id=1, source_target_pairs={{0,1},{1,0},{2,3},{3,2},{4,5},{5,4},{6,7},{7,6},{8,9},{9,8},{10,11... | collective-permute-start | bytes 786440 | tf_op jit(solution)/shard_map/ppermute | solution.py:184
  160.0 4.8 %collective-permute-start.35 = (bf16[4,128,256]{2,1,0:T(8,128)(2,1)S(1)}, bf16[4,128,256]{2,1,0:T(8,128)(2,1)S(1)}, u32[]{:S(2)}, u32[]{:S(2)}) collective-permute-start(bf16[4,128,256]{2,1,0:T(8,128)(2,1)S(1)} %slice_bitcast_fusion.2), channel_id=1, source_target_pairs={{0,16},{16,0},{1,17},{17,1},{2,18},{18,2},{3,19},{19,3},{4,20},{20... | collective-permute-start | bytes 786440 | tf_op jit(solution)/shard_map/ppermute | solution.py:184
  163.0 8.4 %collective-permute-start.46 = (bf16[4,128,256]{2,1,0:T(8,128)(2,1)S(1)}, bf16[4,128,256]{2,1,0:T(8,128)(2,1)S(1)}, u32[]{:S(2)}, u32[]{:S(2)}) collective-permute-start(bf16[4,128,256]{2,1,0:T(8,128)(2,1)S(1)} %slice.49), channel_id=1, source_target_pairs={{0,1},{1,0},{2,3},{3,2},{4,5},{5,4},{6,7},{7,6},{8,9},{9,8},{10,11... | collective-permute-start | bytes 786440 | tf_op jit(solution)/shard_map/ppermute | solution.py:184
  (21 other events, 725.9 us)
